TPU v7x, 32 devices: a whole 2x2x4 slice. The times are simulated.
32 devices in a mesh: grp: 8 (over z, x), tbl: 4 (over y, core).
Axes of the slice: x: 2, y: 2, z: 4, core: 2. Of those that a mesh axis runs over, the one named last changes fastest.
Arguments:
- next_ids: int32 [4096, 224], P(('grp', 'tbl')), may hold values from 0 to 6143
- next_lengths: int32 [4096, 26], P(('grp', 'tbl')), may hold values from 1 to 8
- slot_of_table: int32 [26], replicated, may hold values from 0 to 27, as said below
- tables: bfloat16 [28, 6144, 128], P('tbl'), may hold values from -2.5 to 2.5
- cross_input: bfloat16 [4096, 3456], P(('grp', 'tbl')), may hold values from -6 to 6
- cotangent: bfloat16 [4096, 3456], P(('grp', 'tbl')), may hold values from -6 to 6
- up_weight: bfloat16 [256, 3456], replicated, may hold values from -0.375 to 0.375
- down_weight: bfloat16 [3456, 256], replicated, may hold values from -0.109375 to 0.109375
Outputs:
- next_embedded: bfloat16 [4096, 3328], P(('grp', 'tbl'))
- grad_up: float32 [256, 3456], P('tbl', 'grp')
- grad_down: float32 [3456, 256], P('grp', 'tbl')
Inputs may be any that keep to these rules, and one draw needn't show every extreme that they name: `next_ids`: entry 8 * s + k of an example's row is the k-th id of the bag held in slot s; entries with k at or past the bag's length, and all entries of slots that hold no table, are padding. `slot_of_table`: distinct slots; owner o along tbl holds slots o * 7 to o * 7 + 6, so an owner holds up to 7 tables and some owner holds exactly 7.
All inputs are finite; a program needn't handle non-finite values.
Results may differ from a plain program's by a relative error of at most 0.0049.
Values may be sent and summed in bfloat16 or wider, within the bound.
No kernel may reach another device: no remote copies, remote signals or barrier semaphores. Data moves between devices by JAX's collectives and lax.ppermute only.
A program may use at most 128 MiB of HBM per device.

v0:
```python
import math

import jax
import jax.numpy as jnp
from jax import lax
from jax.sharding import PartitionSpec as P


def pool_rows(table_flat, ids, lens, slots, maxlen):
    count = ids.shape[0]
    width = table_flat.shape[1]
    rows_each = table_flat.shape[0] // slots
    ids_three = ids.reshape(count, slots, maxlen)
    offset = lax.broadcasted_iota(jnp.int32, (1, slots, 1), 1) * rows_each
    picked = jnp.take(table_flat, (ids_three + offset).reshape(-1), axis=0).reshape(
        count, slots, maxlen, width
    )
    keep = lax.broadcasted_iota(jnp.int32, (count, slots, maxlen), 2) < lens[:, :, None]
    masked = jnp.where(keep[..., None], picked, jnp.zeros((), picked.dtype))
    pooled = jnp.sum(masked, axis=2, dtype=jnp.float32)
    return pooled.astype(jnp.bfloat16).reshape(count, slots * width)


def on_device(
    next_ids, next_lengths, slot_of_table, tables, cross_input, cotangent, up_weight, down_weight
):
    batch = next_ids.shape[0]
    owners = lax.axis_size("tbl")
    slots = tables.shape[0]
    slots_all = slots * owners
    maxlen = next_ids.shape[1] // slots_all
    width = tables.shape[2]
    feats = slot_of_table.shape[0]
    hit = (slot_of_table[:, None] == lax.broadcasted_iota(jnp.int32, (1, slots_all), 1)).astype(
        jnp.int32
    )
    slot_lengths = jnp.sum(next_lengths[:, :, None] * hit[None, :, :], axis=1)
    block = 64
    items = batch // block
    id_blocks = next_ids.reshape(items, block, slots_all * maxlen)
    len_blocks = slot_lengths.reshape(items, block, slots_all)
    table_flat = tables.reshape(slots * tables.shape[1], width)
    got_ids = lax.all_to_all(id_blocks, "tbl", split_axis=2, concat_axis=1, tiled=True)
    got_lens = lax.all_to_all(len_blocks, "tbl", split_axis=2, concat_axis=1, tiled=True)
    pooled = lax.map(
        lambda pair: pool_rows(table_flat, pair[0], pair[1], slots, maxlen), (got_ids, got_lens)
    )
    returned = lax.all_to_all(pooled, "tbl", split_axis=1, concat_axis=2, tiled=True)
    by_slot = returned.reshape(batch, slots_all, width)
    next_embedded = jnp.take(by_slot, slot_of_table, axis=1).reshape(batch, feats * width)
    low = jnp.dot(cross_input, down_weight, preferred_element_type=jnp.float32).astype(jnp.bfloat16)
    dz = (cotangent.astype(jnp.float32) * cross_input.astype(jnp.float32)).astype(jnp.bfloat16)
    dlow = jnp.dot(dz, up_weight.T, preferred_element_type=jnp.float32).astype(jnp.bfloat16)
    total = batch * lax.axis_size("grp") * owners
    factor = 1.0 / math.sqrt(total)
    part_up = jnp.dot(low.T, dz, preferred_element_type=jnp.float32) * factor
    part_down = jnp.dot(cross_input.T, dlow, preferred_element_type=jnp.float32) * factor
    owner_up, owner_down = (
        lax.psum_scatter(part_up, "tbl", scatter_dimension=0, tiled=True),
        lax.psum_scatter(part_down, "tbl", scatter_dimension=1, tiled=True),
    )
    grad_up, grad_down = (
        lax.psum_scatter(owner_up, "grp", scatter_dimension=1, tiled=True),
        lax.psum_scatter(owner_down, "grp", scatter_dimension=0, tiled=True),
    )
    return (next_embedded, grad_up, grad_down)


def solution(mesh):
    return jax.shard_map(
        on_device,
        mesh=mesh,
        in_specs=(
            P(("grp", "tbl"), None),
            P(("grp", "tbl"), None),
            P(),
            P("tbl", None, None),
            P(("grp", "tbl"), None),
            P(("grp", "tbl"), None),
            P(),
            P(),
        ),
        out_specs=(P(("grp", "tbl"), None), P("tbl", "grp"), P("grp", "tbl")),
        check_vma=False,
    )
```

profile of v0, /device:TPU:0, one launch (start us, length us, event | category | flops | bytes accessed | tf_op | source)
XLA Modules:
  0.0 268.0 jit_solution(345015347760096953)
XLA Ops:
  7.2 1.4 copy-done
  8.6 5.0 %convolution_multiply_fusion.1 = f32[256,3456]{1,0:T(8,128)} fusion(bf16[128,3456]{1,0:T(8,128)(2,1)} %param.14, bf16[3456,256]{1,0:T(8,128)(2,1)S(1)} %copy-done, bf16[128,3456]{1,0:T(8,128)(2,1)} %param.15), kind=kOutput, calls=%fused_computation.14 | convolution fusion | flops 455671808 | bytes 7077888 | tf_op jit(solution)/shard_map/dot_general | solution.py:56
  13.7 1.1 copy-done.1
  14.8 0.3 copy-done.2
  15.1 5.4 %fusion = f32[3456,256]{0,1:T(8,128)} fusion(bf16[128,3456]{1,0:T(8,128)(2,1)S(1)} %copy-done.1, bf16[256,3456]{1,0:T(8,128)(2,1)} %param.16, bf16[128,3456]{1,0:T(8,128)(2,1)S(1)} %copy-done.2), kind=kOutput, calls=%fused_computation.15 | convolution fusion | flops 455671808 | bytes 7077888 | tf_op jit(solution)/shard_map/dot_general | solution.py:57
  20.6 36.4 %reduce-scatter.9.cloned.1.call-done = f32[64,3456]{1,0:T(8,128)} async-done(((f32[256,3456]{1,0:T(8,128)}), f32[64,3456]{1,0:T(8,128)}) %reduce-scatter.9.cloned.1.call-update) | async-done | bytes 884752 | tf_op jit(solution)/shard_map/reduce_scatter | solution.py:59
  56.9 2.9 %copy.70 = f32[64,3456]{0,1:T(8,128)} copy(f32[64,3456]{1,0:T(8,128)} %reduce-scatter.9.cloned.1.call-done) | data formatting | bytes 1769472
  60.0 0.2 multiply_reduce_fusion
  60.2 0.1 reshape.124
  60.3 0.7 reshape.149
  60.9 3.3 %all-to-all-start = ((s32[4,1,896]{2,1,0:T(1,128)}), s32[4,1,896]{2,1,0:T(1,128)S(1)}, u32[]{:S(2)}, u32[]{:S(2)}) async-start(s32[4,1,896]{2,1,0:T(1,128)} %reshape.149), calls=%async_computation | async-start | bytes 28672 | tf_op jit(solution)/shard_map/all_to_all | solution.py:44
  64.2 0.1 copy.56
  64.3 0.1 copy.57
  64.5 0.9 reshape.151
  65.4 2.7 all-to-all-done
  68.0 3.3 %all-to-all-start.1 = ((s32[4,1,7168]{2,1,0:T(1,128)}), s32[4,1,7168]{2,1,0:T(1,128)S(1)}, u32[]{:S(2)}, u32[]{:S(2)}) async-start(s32[4,1,7168]{2,1,0:T(1,128)} %reshape.151), calls=%async_computation.1 | async-start | bytes 229376 | tf_op jit(solution)/shard_map/all_to_all | solution.py:43
  71.4 0.5 broadcast.113
  71.9 0.7 reduce.4
  72.6 0.1 reshape.150
  72.7 0.1 copy.67
  72.9 2.9 %all-to-all-done.1 = s32[4,1,7168]{2,1,0:T(1,128)S(1)} async-done(((s32[4,1,7168]{2,1,0:T(1,128)}), s32[4,1,7168]{2,1,0:T(1,128)S(1)}, u32[]{:S(2)}, u32[]{:S(2)}) %all-to-all-start.1) | async-done | bytes 114720 | tf_op jit(solution)/shard_map/all_to_all | solution.py:43
  75.7 0.9 reduce.5
  76.7 0.2 reshape.152
  76.9 0.1 copy.76
  77.0 0.2 all_to_all.44
  77.2 22.8 %reduce-scatter.11.cloned.1.call-done = f32[3456,64]{0,1:T(8,128)} async-done(((f32[3456,256]{0,1:T(8,128)}), f32[3456,64]{0,1:T(8,128)}) %reduce-scatter.11.cloned.1.call-update) | async-done | bytes 884752 | tf_op jit(solution)/shard_map/reduce_scatter | solution.py:60
  99.9 3.0 %copy.72 = f32[3456,64]{1,0:T(8,128)} copy(f32[3456,64]{0,1:T(8,128)} %reduce-scatter.11.cloned.1.call-done) | data formatting | bytes 1769472
  102.9 127.0 %while.12 = (s32[]{:T(128)}, bf16[2,256,896]{1,2,0:T(8,128)(2,1)}, s32[2,256,7]{2,1,0:T(8,128)S(1)}, s32[2,256,56]{1,2,0:T(8,128)S(1)}, bf16[43008,128]{1,0:T(8,128)(2,1)}, /*index=5*/s32[]{:T(128)}) while((s32[]{:T(128)}, bf16[2,256,896]{1,2,0:T(8,128)(2,1)}, s32[2,256,7]{2,1,0:T(8,128)S(1)}, s32[2,256,56]{1,2,0:T(8,128)S(1)}, ...), condition=%wide.region_3.4_spmd, body=%wide.region_1.3_spmd.sunk | while | flops 5462025 | bytes 14272161 | solution.py:45
  102.9 0.1 compare_and_fusion.3
  103.0 0.1 copy.80
  103.1 0.2 reshape.158
  103.3 0.1 add.68.clone.2
  103.4 0.4 add.114
  103.8 0.1 compare_select_fusion.4
  103.9 54.2 %gather_fusion = bf16[14336,128]{1,0:T(8,128)(2,1)} fusion(bf16[43008,128]{1,0:T(8,128)(2,1)} %get-tuple-element.159, s32[14336]{0:T(1024)S(1)} %broadcast_clamp_fusion.2), kind=kCustom, calls=%fused_computation.clone.1 | custom fusion | bytes 7397376 | tf_op jit(solution)/shard_map/while/body/eval_jaxpr/jit(_take)/gather | solution.py:15
  158.1 0.5 copy.81
  158.6 0.3 iota_compare_fusion.3
  158.9 6.3 %select_reduce_fusion.2 = bf16[256,7,128]{2,1,0:T(8,128)(2,1)S(1)} fusion(bf16[256,7,8,128]{3,2,1,0:T(8,128)(2,1)} %bitcast.58, pred[256,7,8]{2,1,0:T(8,128)(4,1)S(1)} %copy.81, pred[256,7,8]{2,1,0:T(8,128)(4,1)S(1)} %iota_compare_fusion.3), kind=kLoop, calls=%fused_computation.2.clone.1 | loop fusion | flops 5275648 | bytes 4157440 | tf_op jit(solution)/shard_map/while/body/eval_jaxpr/reduce_sum | solution.py:20
  165.2 0.3 copy.82
  165.6 0.8 constant_dynamic-update-slice_fusion.2
  166.4 0.1 compare_and_fusion.3
  166.5 0.1 copy.80
  166.6 0.2 reshape.158
  166.7 0.1 add.68.clone.2
  166.9 0.4 add.114
  167.4 54.2 %gather_fusion = bf16[14336,128]{1,0:T(8,128)(2,1)} fusion(bf16[43008,128]{1,0:T(8,128)(2,1)} %get-tuple-element.159, s32[14336]{0:T(1024)S(1)} %broadcast_clamp_fusion.2), kind=kCustom, calls=%fused_computation.clone.1 | custom fusion | bytes 7397376 | tf_op jit(solution)/shard_map/while/body/eval_jaxpr/jit(_take)/gather | solution.py:15
  221.6 0.5 copy.81
  222.1 0.3 iota_compare_fusion.3
  222.4 6.3 %select_reduce_fusion.2 = bf16[256,7,128]{2,1,0:T(8,128)(2,1)S(1)} fusion(bf16[256,7,8,128]{3,2,1,0:T(8,128)(2,1)} %bitcast.58, pred[256,7,8]{2,1,0:T(8,128)(4,1)S(1)} %copy.81, pred[256,7,8]{2,1,0:T(8,128)(4,1)S(1)} %iota_compare_fusion.3), kind=kLoop, calls=%fused_computation.2.clone.1 | loop fusion | flops 5275648 | bytes 4157440 | tf_op jit(solution)/shard_map/while/body/eval_jaxpr/reduce_sum | solution.py:20
  228.7 0.3 copy.82
  229.1 0.8 constant_dynamic-update-slice_fusion.2
  229.9 3.7 %copy.61 = bf16[2,256,896]{2,0,1:T(2,128)(2,1)} copy(bf16[2,256,896]{1,2,0:T(8,128)(2,1)} %get-tuple-element.68) | data formatting | bytes 1835008 | tf_op jit(solution)/shard_map/while | solution.py:45
  233.5 3.7 %all-to-all-start.2 = ((bf16[2,256,896]{2,0,1:T(2,128)(2,1)}), bf16[2,256,896]{2,0,1:T(2,128)(2,1)S(1)}, u32[]{:S(2)}, u32[]{:S(2)}) async-start(bf16[2,256,896]{2,0,1:T(2,128)(2,1)} %copy.61), calls=%async_computation.2 | async-start | bytes 1835008 | tf_op jit(solution)/shard_map/all_to_all | solution.py:48
  237.3 12.7 %all-to-all-done.2 = bf16[2,256,896]{2,0,1:T(2,128)(2,1)S(1)} async-done(((bf16[2,256,896]{2,0,1:T(2,128)(2,1)}), bf16[2,256,896]{2,0,1:T(2,128)(2,1)S(1)}, u32[]{:S(2)}, u32[]{:S(2)}) %all-to-all-start.2) | async-done | bytes 917536 | tf_op jit(solution)/shard_map/all_to_all | solution.py:48
  250.0 0.1 copy.62
  250.1 0.7 copy.63
  250.9 1.3 reshape.127
  252.2 1.6 copy.64
  253.8 0.7 gather_fusion.1
  254.5 0.6 copy.65
  255.1 1.7 bitcast_select_fusion
  256.8 1.3 copy.66
  258.1 1.7 copy.71
  259.8 1.7 copy.73
  (32 shorter events, 0.6 us)
Async XLA Ops:
  7.2 1.5 copy-start
  7.2 49.8 %reduce-scatter.9.cloned.1.call-start = ((), (), s32[]{:S(2)}) async-start(), calls=%async_computation.7 | async-start | bytes 4423680 | tf_op jit(solution)/shard_map/reduce_scatter | solution.py:59
  13.7 1.2 copy-start.1
  13.7 1.4 copy-start.2
  13.7 86.2 %reduce-scatter.11.cloned.1.call-start = ((), (), s32[]{:S(2)}) async-start(), calls=%async_computation.8 | async-start | bytes 4423680 | tf_op jit(solution)/shard_map/reduce_scatter | solution.py:60
  20.5 39.4 %copy-start.5 = (s32[26]{0:T(128)S(1)}, s32[26]{0:T(128)}, u32[]{:S(2)}) copy-start(s32[26]{0:T(128)} %param.12) | copy-start | bytes 316
  20.5 39.5 %copy-start.4 = (s32[128,26]{0,1:T(8,128)S(1)}, s32[128,26]{0,1:T(8,128)}, u32[]{:S(2)}) copy-start(s32[128,26]{0,1:T(8,128)} %param.11) | copy-start | bytes 39940
  20.5 43.7 %copy-start.3 = (s32[128,224]{0,1:T(8,128)S(1)}, s32[128,224]{0,1:T(8,128)}, u32[]{:S(2)}) copy-start(s32[128,224]{0,1:T(8,128)} %param.10) | copy-start | bytes 344068
  20.5 237.6 %reduce-scatter.13.cloned.1.call-start = ((), (), s32[]{:S(2)}) async-start(), calls=%async_computation.9 | async-start | bytes 1990656
  60.9 7.1 %all-to-all-start = ((s32[4,1,896]{2,1,0:T(1,128)}), s32[4,1,896]{2,1,0:T(1,128)S(1)}, u32[]{:S(2)}, u32[]{:S(2)}) async-start(s32[4,1,896]{2,1,0:T(1,128)} %reshape.149), calls=%async_computation | async-start | bytes 28672 | tf_op jit(solution)/shard_map/all_to_all | solution.py:44
  68.0 7.7 %all-to-all-start.1 = ((s32[4,1,7168]{2,1,0:T(1,128)}), s32[4,1,7168]{2,1,0:T(1,128)S(1)}, u32[]{:S(2)}, u32[]{:S(2)}) async-start(s32[4,1,7168]{2,1,0:T(1,128)} %reshape.151), calls=%async_computation.1 | async-start | bytes 229376 | tf_op jit(solution)/shard_map/all_to_all | solution.py:43
  71.3 188.5 %reduce-scatter.15.cloned.1.call-start = ((), (), s32[]{:S(2)}) async-start(), calls=%async_computation.10 | async-start | bytes 1990656
  233.5 16.5 %all-to-all-start.2 = ((bf16[2,256,896]{2,0,1:T(2,128)(2,1)}), bf16[2,256,896]{2,0,1:T(2,128)(2,1)S(1)}, u32[]{:S(2)}, u32[]{:S(2)}) async-start(bf16[2,256,896]{2,0,1:T(2,128)(2,1)} %copy.61), calls=%async_computation.2 | async-start | bytes 1835008 | tf_op jit(solution)/shard_map/all_to_all | solution.py:48
Sparse Core Ops, SparseCore 0:
  13.8 43.0 reduce-scatter.8
  59.5 40.3 reduce-scatter.10
  103.4 66.5 reduce-scatter.12
  173.3 65.5 reduce-scatter.14
where the time goes:
time: 269 us; the launch traced here: 268 us
  local copies, waits for them, and re-layouts  138 us (51%)
  waiting for transfers between devices  77.4 us (29%)
  other arithmetic  17.2 us (6%)
  between operations  14 us (5%)
  starting transfers between devices  10.4 us (4%)
  matrix products  10.4 us (4%)
    gather x2, local copies, waits for them, and re-layouts, pool_rows(): jnp.take(table_flat, (ids_three + offset).reshape(-1), axis=0)  108 us
    reduce_scatter x1, waiting for transfers between devices, on_device(): lax.psum_scatter(part_up, 'tbl', scatter_dimension=0, tiled=True)  36.4 us
    reduce_scatter x1, waiting for transfers between devices, on_device(): lax.psum_scatter(part_down, 'tbl', scatter_dimension=1, tiled=True)  22.8 us
    unnamed x22, local copies, waits for them, and re-layouts  15.3 us
    all_to_all x1, waiting for transfers between devices, on_device(): lax.all_to_all(pooled, 'tbl', split_axis=1, concat_axis=2, tiled=True)  12.7 us
    reduce_sum x2, other arithmetic, pool_rows(): pooled = jnp.sum(masked, axis=2, dtype=jnp.float32)  12.6 us
    dot_general x1, matrix products, on_device(): jnp.dot(cross_input.T, dlow, preferred_element_type=jnp.float32) * factor  5.39 us
  transfers between devices with their start and end apart: 7, of which 5 were waited for; matrix products, arithmetic and copies ran while one was open for 58% of the time, Pallas kernels for 0%

commit v1 on v0

v1 whole, which is shorter than its diff:
```python
import functools
import math

import jax
import jax.numpy as jnp
from jax import lax
from jax.experimental import pallas as pl
from jax.experimental.pallas import tpu as pltpu
from jax.sharding import PartitionSpec as P

F32 = jnp.float32
BF16 = jnp.bfloat16
LANES = 128


def whole(memory=pltpu.VMEM):
    return pl.BlockSpec(memory_space=memory)


def mask_ids_kernel(slot_ref, ids_ref, lens_ref, out_ref, *, maxlen, rows):
    entries, batch = out_ref.shape
    feats = lens_ref.shape[1]
    slot_of_row = lax.broadcasted_iota(jnp.int32, (entries, feats), 0) // maxlen
    hit = (slot_of_row == slot_ref[...]).astype(F32)
    lens = lax.dot_general(
        hit, lens_ref[...].astype(F32), (((1,), (1,)), ((), ())), preferred_element_type=F32
    )
    place = lax.broadcasted_iota(jnp.int32, (entries, batch), 0) % maxlen
    keep = place.astype(F32) + 0.5 < lens
    out_ref[...] = jnp.where(keep, ids_ref[...].T, rows)


def mask_ids(slot_of_table, ids, lengths, maxlen, rows):
    return pl.pallas_call(
        functools.partial(mask_ids_kernel, maxlen=maxlen, rows=rows),
        in_specs=[whole()] * 3,
        out_specs=whole(),
        out_shape=jax.ShapeDtypeStruct((ids.shape[1], ids.shape[0]), jnp.int32),
        name="mask_ids",
    )(slot_of_table.reshape(1, -1), ids, lengths)


def pool_kernel(ids_ref, table_ref, out_ref, wide_ref, sum_ref, *, rows, chunk):
    groups, maxlen, batch = ids_ref.shape

    def widen(i, carry):
        start = pl.multiple_of(i * chunk, chunk)
        wide_ref[pl.ds(start, chunk), :] = table_ref[0, pl.ds(start, chunk), :].astype(F32)
        return carry

    lax.fori_loop(0, rows // chunk, widen, 0)
    wide_ref[pl.ds(rows, 8), :] = jnp.zeros((8, wide_ref.shape[1]), F32)

    def pool(g, carry):
        for b in range(batch):
            total = wide_ref[pl.ds(ids_ref[g, 0, b], 1), :]
            for k in range(1, maxlen):
                total = total + wide_ref[pl.ds(ids_ref[g, k, b], 1), :]
            sum_ref[pl.ds(b, 1), :] = total
        out_ref[g, 0] = sum_ref[...].astype(BF16)
        return carry

    lax.fori_loop(0, groups, pool, 0)


def pool_slots(ids, tables, first, count, maxlen):
    groups, entries, batch = ids.shape
    rows, width = tables.shape[1:]
    chunk = math.gcd(rows, 512)
    return pl.pallas_call(
        functools.partial(pool_kernel, rows=rows, chunk=chunk),
        grid=(count,),
        in_specs=[
            pl.BlockSpec(
                (groups, maxlen, batch), lambda s: (0, s + first, 0), memory_space=pltpu.SMEM
            ),
            pl.BlockSpec((1, rows, width), lambda s: (s + first, 0, 0)),
        ],
        out_specs=pl.BlockSpec((groups, 1, batch, width), lambda s: (0, s, 0, 0)),
        out_shape=jax.ShapeDtypeStruct((groups, count, batch, width), BF16),
        scratch_shapes=[pltpu.VMEM((rows + 8, width), F32), pltpu.VMEM((batch, width), F32)],
        name="pool_slots",
    )(ids, tables)


def place_kernel(slot_ref, *refs, slots, firsts, counts):
    parts, out_ref = refs[:-1], refs[-1]
    width = parts[0].shape[3]
    for f in range(slot_ref.shape[0]):
        slot = slot_ref[f]
        owner = slot // slots
        local = slot - owner * slots
        for part, first, count in zip(parts, firsts, counts):

            def put(part=part, first=first, f=f):
                out_ref[:, f * width : (f + 1) * width] = part[owner, local - first]

            if len(parts) == 1:
                put()
            else:
                pl.when((local >= first) & (local < first + count))(put)


def place(slot_of_table, parts, firsts, counts, slots):
    batch, width = parts[0].shape[2:]
    feats = slot_of_table.shape[0]
    return pl.pallas_call(
        functools.partial(place_kernel, slots=slots, firsts=firsts, counts=counts),
        in_specs=[whole(pltpu.SMEM)] + [whole()] * len(parts),
        out_specs=whole(),
        out_shape=jax.ShapeDtypeStruct((batch, feats * width), BF16),
        name="place",
    )(slot_of_table, *parts)


def grads_kernel(
    pos_ref, x_ref, ct_ref, xs_ref, cts_ref, down_ref, up_ref, *refs, owners, groups, rows_a
):
    tall = owners // 2
    far = groups // 2
    qa, qb = refs[:tall], refs[tall : tall + 2]
    both_ref, sum_ref = refs[tall + 2 :]
    core, y, x, z = pos_ref[0], pos_ref[1], pos_ref[2], pos_ref[3]
    batch, wide = x_ref.shape
    rank = down_ref.shape[1]
    part = rank // owners
    pair = 2 * batch
    for at, (a_ref, b_ref) in enumerate(((x_ref, ct_ref), (xs_ref, cts_ref))):
        a = a_ref[...]
        both_ref[pl.ds(at * batch, batch), :] = (b_ref[...].astype(F32) * a.astype(F32)).astype(BF16)
        both_ref[pl.ds(pair + at * batch, batch), :] = a
    low = jnp.dot(both_ref[pl.ds(pair, pair), :], down_ref[...], preferred_element_type=F32)
    dlow = lax.dot_general(
        both_ref[pl.ds(0, pair), :],
        up_ref[...],
        (((1,), (1,)), ((), ())),
        preferred_element_type=F32,
    )
    none = jnp.zeros((pair, part), F32)
    columns = []
    for ry in range(tall):
        owner = 2 * lax.rem(y + ry, tall) + core
        lo, dl = none, none
        for t in range(owners):
            lo = jnp.where(owner == t, low[:, t * part : (t + 1) * part], lo)
            dl = jnp.where(owner == t, dlow[:, t * part : (t + 1) * part], dl)
        columns.append(
            jnp.concatenate(
                [jnp.concatenate([lo, none], axis=1), jnp.concatenate([none, dl], axis=1)], axis=0
            )
        )
    right = jnp.concatenate(columns, axis=1).astype(BF16)
    step = 384 if wide % 384 == 0 else wide
    for d in range(0, wide, step):
        sum_ref[pl.ds(d, step), :] = lax.dot_general(
            both_ref[:, d : d + step], right, (((0,), (0,)), ((), ())), preferred_element_type=F32
        )
    each = wide // groups
    rows_b = each - rows_a
    block = 2 * part
    for rx in range(2):
        for r in range(far):
            g = 2 * lax.rem(z + r, far) + (x + rx - 2 * x * rx)
            start = pl.multiple_of(g * each, 16)
            for ry in range(tall):
                cols = slice(ry * block, (ry + 1) * block)
                qa[ry][rx, r] = sum_ref[pl.ds(start, rows_a), cols].astype(qa[ry].dtype)
                qb[rx][ry, r] = sum_ref[pl.ds(start + rows_a, rows_b), cols].astype(qb[rx].dtype)


def part_grads(pos, x, ct, xs, cts, down, up, owners, groups, rows_a):
    wide, rank = down.shape
    batch = x.shape[0]
    tall, far = owners // 2, groups // 2
    rows_b = wide // groups - rows_a
    block = 2 * (rank // owners)
    shape = jax.ShapeDtypeStruct
    qa = [shape((2, far, rows_a, block), F32 if ry == 0 else BF16) for ry in range(tall)]
    qb = [shape((tall, far, rows_b, block), F32 if rx == 0 else BF16) for rx in range(2)]
    out = pl.pallas_call(
        functools.partial(grads_kernel, owners=owners, groups=groups, rows_a=rows_a),
        in_specs=[whole(pltpu.SMEM)] + [whole()] * 6,
        out_specs=[whole()] * (tall + 2),
        out_shape=qa + qb,
        scratch_shapes=[
            pltpu.VMEM((4 * batch, wide), BF16),
            pltpu.VMEM((wide, tall * block), F32),
        ],
        name="part_grads",
    )(pos, x, ct, xs, cts, down, up)
    return out[:tall], out[tall:]


def fold_kernel(*refs, tall):
    ka, kb, ra, rb = refs[0], refs[1], refs[2 : tall + 1], refs[tall + 1]
    outs = refs[tall + 2 :]
    a_keep, a_send, b_keep, b_send = outs[0], outs[1], outs[2], outs[3:]

    def at_a(i):
        total = ka[i]
        for r in ra:
            total = total + r[i].astype(F32)
        return total

    def at_b(i):
        return kb[i] + rb[i].astype(F32)

    a_keep[...] = at_a(0)
    a_send[...] = at_a(1).astype(BF16)
    b_keep[...] = at_b(0)
    for ry in range(1, tall):
        b_send[ry - 1][...] = at_b(ry).astype(BF16)


def fold(ka, kb, ra, rb, tall):
    shape = jax.ShapeDtypeStruct
    a, b = ka.shape[1:], kb.shape[1:]
    out = [shape(a, F32), shape(a, BF16), shape(b, F32)] + [shape(b, BF16)] * (tall - 1)
    res = pl.pallas_call(
        functools.partial(fold_kernel, tall=tall),
        in_specs=[whole()] * (tall + 2),
        out_specs=[whole()] * len(out),
        out_shape=out,
        name="fold",
    )(ka, kb, *ra, rb)
    return res[0], res[1], res[2], res[3:]


def join_kernel(*refs, tall, far):
    ka, kb, ra, rb, outs = refs[0], refs[1], refs[2], refs[3 : tall + 2], refs[tall + 2 :]
    rows_a = ka.shape[1]
    for r in range(far):
        sa = ka[r] + ra[r].astype(F32)
        sb = kb[r]
        for one in rb:
            sb = sb + one[r].astype(F32)
        outs[r][0:rows_a, :] = sa.astype(outs[r].dtype)
        outs[r][rows_a:, :] = sb.astype(outs[r].dtype)


def join(ka, kb, ra, rb, tall, far):
    rows, block = ka.shape[1] + kb.shape[1], ka.shape[2]
    out = [jax.ShapeDtypeStruct((rows, block), F32 if r == 0 else BF16) for r in range(far)]
    return pl.pallas_call(
        functools.partial(join_kernel, tall=tall, far=far),
        in_specs=[whole()] * (tall + 2),
        out_specs=[whole()] * far,
        out_shape=out,
        name="join",
    )(ka, kb, ra, *rb)


def finish_kernel(*refs, factor):
    up_ref, down_ref = refs[-2:]
    total = refs[0][...]
    for r in refs[1:-2]:
        total = total + r[...].astype(F32)
    total = total * factor
    half = total.shape[1] // 2
    up_ref[...] = total.T[:half, :]
    down_ref[...] = total[:, half:]


def finish(keep, came, factor):
    rows, block = keep.shape
    half = block // 2
    shape = jax.ShapeDtypeStruct
    return pl.pallas_call(
        functools.partial(finish_kernel, factor=factor),
        in_specs=[whole()] * (1 + len(came)),
        out_specs=[whole()] * 2,
        out_shape=[shape((half, rows), F32), shape((rows, half), F32)],
        name="finish",
    )(keep, *came)


def grads_by_exchange(x, ct, up, down, factor):
    owners, groups = lax.axis_size("tbl"), lax.axis_size("grp")
    tall, far = owners // 2, groups // 2
    t, g = lax.axis_index("tbl"), lax.axis_index("grp")
    pos = jnp.stack([t % 2, t // 2, g % 2, g // 2]).astype(jnp.int32)
    other_core = [(i, i ^ 1) for i in range(owners)]
    other_x = [(i, i ^ 1) for i in range(groups)]

    def to_y(ry):
        return [(i, 2 * ((i // 2 + ry) % tall) + i % 2) for i in range(owners)]

    def to_z(r):
        return [(i, 2 * ((i // 2 + r) % far) + i % 2) for i in range(groups)]

    xs = lax.ppermute(x, "tbl", other_core)
    cts = lax.ppermute(ct, "tbl", other_core)
    rows_a = (x.shape[1] // groups // 2) // 16 * 16
    qa, qb = part_grads(pos, x, ct, xs, cts, down, up, owners, groups, rows_a)
    ra = [lax.ppermute(qa[ry], "tbl", to_y(ry)) for ry in range(1, tall)]
    rb = lax.ppermute(qb[1], "grp", other_x)
    ka, sa, kb, sb = fold(qa[0], qb[0], ra, rb, tall)
    ra = lax.ppermute(sa, "grp", other_x)
    rb = [lax.ppermute(s, "tbl", to_y(ry + 1)) for ry, s in enumerate(sb)]
    out = join(ka, kb, ra, rb, tall, far)
    came = [lax.ppermute(out[r], "grp", to_z(r)) for r in range(1, far)]
    return finish(out[0], came, factor)


def grads_plain(x, ct, up, down, factor):
    low = jnp.dot(x, down, preferred_element_type=F32).astype(BF16)
    dz = (ct.astype(F32) * x.astype(F32)).astype(BF16)
    dlow = jnp.dot(dz, up.T, preferred_element_type=F32).astype(BF16)
    part_up = jnp.dot(low.T, dz, preferred_element_type=F32) * factor
    part_down = jnp.dot(x.T, dlow, preferred_element_type=F32) * factor
    owner_up = lax.psum_scatter(part_up, "tbl", scatter_dimension=0, tiled=True)
    owner_down = lax.psum_scatter(part_down, "tbl", scatter_dimension=1, tiled=True)
    return (
        lax.psum_scatter(owner_up, "grp", scatter_dimension=1, tiled=True),
        lax.psum_scatter(owner_down, "grp", scatter_dimension=0, tiled=True),
    )


def on_device(ids, lengths, slot_of_table, tables, x, ct, up, down):
    owners, groups = lax.axis_size("tbl"), lax.axis_size("grp")
    batch = ids.shape[0]
    slots, rows = tables.shape[:2]
    maxlen = ids.shape[1] // (slots * owners)
    factor = 1.0 / math.sqrt(batch * owners * groups)

    masked = mask_ids(slot_of_table, ids, lengths, maxlen, rows)
    got = lax.all_to_all(masked.reshape(owners, slots * maxlen, batch), "tbl", 0, 0)

    each, part = x.shape[1] // groups, down.shape[1] // owners
    tiled = owners % 2 == 0 and groups % 2 == 0 and each % 16 == 0 and 2 * part % LANES == 0
    grads = grads_by_exchange if tiled else grads_plain
    grad_up, grad_down = grads(x, ct, up, down, factor)

    cut = (slots + 1) // 2
    firsts, counts = (0, cut), (cut, slots - cut)
    parts = [
        lax.all_to_all(pool_slots(got, tables, first, count, maxlen), "tbl", 0, 0)
        for first, count in zip(firsts, counts)
    ]
    embedded = place(slot_of_table, parts, firsts, counts, slots)
    return embedded, grad_up, grad_down


def solution(mesh):
    rows = P(("grp", "tbl"), None)
    return jax.shard_map(
        on_device,
        mesh=mesh,
        in_specs=(rows, rows, P(), P("tbl", None, None), rows, rows, P(), P()),
        out_specs=(rows, P("tbl", "grp"), P("grp", "tbl")),
        check_vma=False,
    )
```

time: 269 us -> 97.1 us (0.36)
  local copies, waits for them, and re-layouts: 138 us -> 7.83 us
  waiting for transfers between devices: 77.4 us -> 16.1 us
  Pallas kernels: 0 us -> 48.1 us
  other arithmetic: 17.2 us -> 0.58 us
  between operations: 14 us -> 0.71 us
  starting transfers between devices: 10.4 us -> 23.3 us
  matrix products: 10.4 us -> 0 us
    gather x4 -> x0, local copies, waits for them, and re-layouts: 110 us -> none  [the longest x2 108 us: pool_rows(): jnp.take(table_flat, (ids_three + offset).reshape(-1), axis=0)]
    reduce_scatter x2 -> x0, waiting for transfers between devices: 59.1 us -> none  [the longest x1 36.4 us: on_device(): lax.psum_scatter(part_up, 'tbl', scatter_dimension=0, tiled=True)]
    pallas_call x0 -> x8, Pallas kernels: none -> 48.1 us  [the longest x2 29.1 us: pool_slots(): pl.pallas_call(functools.partial(pool_kernel, rows=rows, chunk=chunk), gr...]
    all_to_all x3, waiting for transfers between devices: 18.2 us -> 2.98 us  [the longest x1 2.97 us: on_device(): lax.all_to_all(masked.reshape(owners, slots * maxlen, batch), 'tbl', 0, 0)]
    ppermute x0 -> x9, waiting for transfers between devices: none -> 13.1 us  [the longest x1 7.16 us: grads_by_exchange(): ra = lax.ppermute(sa, 'grp', other_x)]
    ppermute x0 -> x9, starting transfers between devices: none -> 13 us  [the longest x3 5.52 us: grads_by_exchange(): came = [lax.ppermute(out[r], 'grp', to_z(r)) for r in range(1, far)]]
    reduce_sum x3 -> x0, other arithmetic: 12.8 us -> none  [the longest x2 12.6 us: pool_rows(): pooled = jnp.sum(masked, axis=2, dtype=jnp.float32)]
    dot_general x2 -> x0, matrix products: 10.4 us -> none  [the longest x1 5.39 us: on_device(): jnp.dot(cross_input.T, dlow, preferred_element_type=jnp.float32) * factor]
  transfers between devices with their start and end apart: 7 -> 12, of which waited for: 5 -> 6; matrix products, arithmetic and copies ran while one was open for 58% -> 2% of each run, Pallas kernels for 0% -> 40%
where the time goes in v1:
time: 97.1 us; the launch traced here: 96.6 us
  Pallas kernels  48.1 us (50%)
  starting transfers between devices  23.3 us (24%)
  waiting for transfers between devices  16.1 us (17%)
  local copies, waits for them, and re-layouts  7.83 us (8%)
    pallas_call x2, Pallas kernels, pool_slots(): pl.pallas_call(functools.partial(pool_kernel, rows=rows, chunk=chunk), gr...  29.1 us
    unnamed x31, local copies, waits for them, and re-layouts  7.83 us
    pallas_call x1, Pallas kernels, part_grads(): pl.pallas_call(functools.partial(grads_kernel, owners=owners, groups=grou...  7.58 us
    ppermute x1, waiting for transfers between devices, grads_by_exchange(): ra = lax.ppermute(sa, 'grp', other_x)  7.16 us
    all_to_all x2, starting transfers between devices, on_device(): lax.all_to_all(pool_slots(got, tables, first, count, maxlen), 'tbl', 0, 0)  6.93 us
    ppermute x3, starting transfers between devices, grads_by_exchange(): came = [lax.ppermute(out[r], 'grp', to_z(r)) for r in range(1, far)]  5.52 us
    all_to_all x1, starting transfers between devices, on_device(): lax.all_to_all(masked.reshape(owners, slots * maxlen, batch), 'tbl', 0, 0)  3.32 us
    all_to_all x1, waiting for transfers between devices, on_device(): lax.all_to_all(masked.reshape(owners, slots * maxlen, batch), 'tbl', 0, 0)  2.97 us
  transfers between devices with their start and end apart: 12, of which 6 were waited for; matrix products, arithmetic and copies ran while one was open for 2% of the time, Pallas kernels for 40%

profile of v1, /device:TPU:0, one launch (start us, length us, event | category | flops | bytes accessed | tf_op | source)
XLA Modules:
  0.0 96.6 jit_solution(13118763176137802504)
XLA Ops:
  0.6 0.6 collective-permute-start
  1.2 0.1 collective-permute-start.1
  1.3 0.6 pad_add_fusion.pos_ref
  1.8 0.0 copy-start.9
  1.9 0.0 copy-start.13
  1.9 1.6 %collective-permute-done.xs_ref = bf16[128,3456]{1,0:T(8,128)(2,1)S(1)} collective-permute-done((bf16[128,3456]{1,0:T(8,128)(2,1)}, bf16[128,3456]{1,0:T(8,128)(2,1)S(1)}, u32[]{:S(2)}, u32[]{:S(2)}) %collective-permute-start) | collective-permute-done | bytes 884768 | tf_op jit(solution)/shard_map/ppermute | solution.py:291
  3.5 0.0 copy-start.3
  3.5 1.3 %collective-permute-done.1.cts_ref = bf16[128,3456]{1,0:T(8,128)(2,1)S(1)} collective-permute-done((bf16[128,3456]{1,0:T(8,128)(2,1)}, bf16[128,3456]{1,0:T(8,128)(2,1)S(1)}, u32[]{:S(2)}, u32[]{:S(2)}) %collective-permute-start.1) | collective-permute-done | bytes 884768 | tf_op jit(solution)/shard_map/ppermute | solution.py:292
  4.7 0.0 copy-done.3
  4.7 0.0 copy-start.4
  4.7 0.9 copy-done.4
  5.6 7.6 %part_grads.1 = (f32[2,4,208,128]{3,2,1,0:T(8,128)}, bf16[2,4,208,128]{3,2,1,0:T(8,128)(2,1)}, f32[2,4,224,128]{3,2,1,0:T(8,128)}, bf16[2,4,224,128]{3,2,1,0:T(8,128)(2,1)}) custom-call(s32[4]{0:T(128)} %pad_add_fusion.pos_ref, bf16[128,3456]{1,0:T(8,128)(2,1)} %x_ref.1, bf16[128,3456]{1,0:T(8,128)(2,1)} %ct_ref.1, bf16[128,3456]{1,0:T(8,128)(2,1)} %copy-done.3, ...), custom_call_target="tpu_custom_call" | custom-call | tf_op jit(solution)/shard_map/part_grads/pallas_call | solution.py:180
  13.2 2.8 %collective-permute-start.3 = (bf16[2,4,224,128]{3,2,1,0:T(8,128)(2,1)}, bf16[2,4,224,128]{3,2,1,0:T(8,128)(2,1)S(1)}, u32[]{:S(2)}, u32[]{:S(2)}) collective-permute-start(bf16[2,4,224,128]{3,2,1,0:T(8,128)(2,1)} %get-tuple-element.20), channel_id=1, source_target_pairs={{0,4},{4,0},{8,12},{12,8},{16,20},{20,16},{24,28},{28,24},{1,5},{5... | collective-permute-start | bytes 1376264 | tf_op jit(solution)/shard_map/ppermute | solution.py:296
  16.1 0.0 copy-done.9
  16.1 0.8 copy.11.ids_ref
  16.8 0.0 copy-done.13
  16.8 0.7 copy.12.lens_ref
  17.6 1.7 %mask_ids.1 = s32[224,128]{1,0:T(8,128)} custom-call(s32[1,26]{1,0:T(1,128)} %bitcast.7, s32[128,224]{1,0:T(8,128)} %copy.11.ids_ref, s32[128,26]{1,0:T(8,128)} %copy.12.lens_ref), custom_call_target="tpu_custom_call" | custom-call | tf_op jit(solution)/shard_map/mask_ids/pallas_call | solution.py:34
  19.3 3.3 %all-to-all-start = ((s32[4,56,128]{2,1,0:T(8,128)}), s32[4,56,128]{2,1,0:T(8,128)S(1)}, u32[]{:S(2)}, u32[]{:S(2)}) async-start(s32[4,56,128]{2,1,0:T(8,128)} %bitcast.6), calls=%async_computation | async-start | bytes 229376 | tf_op jit(solution)/shard_map/all_to_all | solution.py:327
  22.6 2.0 %collective-permute-start.2 = (bf16[2,4,208,128]{3,2,1,0:T(8,128)(2,1)}, bf16[2,4,208,128]{3,2,1,0:T(8,128)(2,1)S(1)}, u32[]{:S(2)}, u32[]{:S(2)}) collective-permute-start(bf16[2,4,208,128]{3,2,1,0:T(8,128)(2,1)} %get-tuple-element.19), channel_id=1, source_target_pairs={{0,2},{1,3},{2,0},{3,1},{4,6},{5,7},{6,4},{7,5},{8,10},{9,11},{10,... | collective-permute-start | bytes 1277960 | tf_op jit(solution)/shard_map/ppermute | solution.py:295
  24.6 3.0 %all-to-all-done.ids_ref = s32[4,56,128]{2,1,0:T(8,128)S(1)} async-done(((s32[4,56,128]{2,1,0:T(8,128)}), s32[4,56,128]{2,1,0:T(8,128)S(1)}, u32[]{:S(2)}, u32[]{:S(2)}) %all-to-all-start) | async-done | bytes 114720 | tf_op jit(solution)/shard_map/all_to_all | solution.py:327
  27.6 0.0 copy-start.2
  27.6 0.6 copy-done.2
  28.2 12.8 %pool_slots.3 = bf16[4,3,128,128]{3,2,1,0:T(8,128)(2,1)} custom-call(s32[4,56,128]{2,1,0:T(8,128)} %copy-done.2, bf16[7,6144,128]{2,1,0:T(8,128)(2,1)} %table_ref.3), custom_call_target="tpu_custom_call" | custom-call | tf_op jit(solution)/shard_map/pool_slots/pallas_call | solution.py:70
  41.0 3.5 %all-to-all-start.2 = ((bf16[4,3,128,128]{3,2,1,0:T(8,128)(2,1)}), bf16[4,3,128,128]{3,2,1,0:T(8,128)(2,1)S(1)}, u32[]{:S(2)}, u32[]{:S(2)}) async-start(bf16[4,3,128,128]{3,2,1,0:T(8,128)(2,1)} %pool_slots.3), calls=%async_computation.2 | async-start | bytes 786432 | tf_op jit(solution)/shard_map/all_to_all | solution.py:337
  44.5 16.3 %pool_slots.2 = bf16[4,4,128,128]{3,2,1,0:T(8,128)(2,1)} custom-call(s32[4,56,128]{2,1,0:T(8,128)} %copy-done.2, bf16[7,6144,128]{2,1,0:T(8,128)(2,1)} %table_ref.3), custom_call_target="tpu_custom_call" | custom-call | tf_op jit(solution)/shard_map/pool_slots/pallas_call | solution.py:70
  60.8 0.0 all-to-all-done.2.refs_1_
  60.8 0.0 copy-start.1
  60.8 3.5 %all-to-all-start.1 = ((bf16[4,4,128,128]{3,2,1,0:T(8,128)(2,1)}), bf16[4,4,128,128]{3,2,1,0:T(8,128)(2,1)S(1)}, u32[]{:S(2)}, u32[]{:S(2)}) async-start(bf16[4,4,128,128]{3,2,1,0:T(8,128)(2,1)} %pool_slots.2), calls=%async_computation.1 | async-start | bytes 1048576 | tf_op jit(solution)/shard_map/all_to_all | solution.py:337
  64.3 0.0 collective-permute-done.2.refs_2_
  64.3 0.0 copy-start.6
  64.3 0.0 collective-permute-done.3.refs_3_
  64.3 0.0 copy-start.5
  64.3 0.7 copy-done.6
  65.0 0.2 copy-done.5
  65.2 2.8 %fold.1 = (f32[4,208,128]{2,1,0:T(8,128)}, bf16[4,208,128]{2,1,0:T(8,128)(2,1)}, f32[4,224,128]{2,1,0:T(8,128)}, bf16[4,224,128]{2,1,0:T(8,128)(2,1)}) custom-call(f32[2,4,208,128]{3,2,1,0:T(8,128)} %get-tuple-element.17.refs_0_, f32[2,4,224,128]{3,2,1,0:T(8,128)} %get-tuple-element.18.refs_1_, bf16[2,4,208,128]{3,2,1,0:T(8,128)(2,1)} %copy-done.6, ...), custom_call_target="tpu_custom_call" | custom-call | tf_op jit(solution)/shard_map/fold/pallas_call | solution.py:219
  68.0 0.0 copy-done.1
  68.0 2.0 %collective-permute-start.5 = (bf16[4,224,128]{2,1,0:T(8,128)(2,1)}, bf16[4,224,128]{2,1,0:T(8,128)(2,1)S(1)}, u32[]{:S(2)}, u32[]{:S(2)}) collective-permute-start(bf16[4,224,128]{2,1,0:T(8,128)(2,1)} %get-tuple-element.24), channel_id=1, source_target_pairs={{0,2},{1,3},{2,0},{3,1},{4,6},{5,7},{6,4},{7,5},{8,10},{9,11},{10,... | collective-permute-start | bytes 688136 | tf_op jit(solution)/shard_map/ppermute | solution.py:299
  70.0 0.0 collective-permute-start.4
  70.0 7.2 %collective-permute-done.4.refs_2_ = bf16[4,208,128]{2,1,0:T(8,128)(2,1)S(1)} collective-permute-done((bf16[4,208,128]{2,1,0:T(8,128)(2,1)}, bf16[4,208,128]{2,1,0:T(8,128)(2,1)S(1)}, u32[]{:S(2)}, u32[]{:S(2)}) %collective-permute-start.4) | collective-permute-done | bytes 213024 | tf_op jit(solution)/shard_map/ppermute | solution.py:298
  77.2 0.0 copy-start.8
  77.2 0.8 collective-permute-done.5.refs_3_
  78.0 0.0 copy-start.7
  78.0 0.0 copy-done.8
  78.0 0.7 copy-done.7
  78.7 2.1 %join.1 = (f32[432,128]{1,0:T(8,128)}, bf16[432,128]{1,0:T(8,128)(2,1)}, bf16[432,128]{1,0:T(8,128)(2,1)}, bf16[432,128]{1,0:T(8,128)(2,1)}) custom-call(f32[4,208,128]{2,1,0:T(8,128)} %get-tuple-element.21.refs_0_, f32[4,224,128]{2,1,0:T(8,128)} %get-tuple-element.22.refs_1_, bf16[4,208,128]{2,1,0:T(8,128)(2,1)} %copy-done.8, bf16[4,224,128]{2,1,0:T(8,128)(2,1)} %copy-done.7), custom_call_target="tpu_custom_call" | custom-call | tf_op jit(solution)/shard_map/join/pallas_call | solution.py:244
  80.7 1.6 %collective-permute-start.6 = (bf16[432,128]{1,0:T(8,128)(2,1)}, bf16[432,128]{1,0:T(8,128)(2,1)S(1)}, u32[]{:S(2)}, u32[]{:S(2)}) collective-permute-start(bf16[432,128]{1,0:T(8,128)(2,1)} %get-tuple-element.26), channel_id=1, source_target_pairs={{0,8},{4,12},{8,16},{12,20},{16,24},{20,28},{24,0},{28,4},{1,9},{5... | collective-permute-start | bytes 331784 | tf_op jit(solution)/shard_map/ppermute | solution.py:301
  82.3 2.6 %collective-permute-start.7 = (bf16[432,128]{1,0:T(8,128)(2,1)}, bf16[432,128]{1,0:T(8,128)(2,1)S(1)}, u32[]{:S(2)}, u32[]{:S(2)}) collective-permute-start(bf16[432,128]{1,0:T(8,128)(2,1)} %get-tuple-element.27), channel_id=1, source_target_pairs={{0,16},{4,20},{8,24},{12,28},{16,0},{20,4},{24,8},{28,12},{1,17},{... | collective-permute-start | bytes 331784 | tf_op jit(solution)/shard_map/ppermute | solution.py:301
  84.9 1.3 %collective-permute-start.8 = (bf16[432,128]{1,0:T(8,128)(2,1)}, bf16[432,128]{1,0:T(8,128)(2,1)S(1)}, u32[]{:S(2)}, u32[]{:S(2)}) collective-permute-start(bf16[432,128]{1,0:T(8,128)(2,1)} %get-tuple-element.28), channel_id=1, source_target_pairs={{0,24},{4,28},{8,0},{12,4},{16,8},{20,12},{24,16},{28,20},{1,25},{... | collective-permute-start | bytes 331784 | tf_op jit(solution)/shard_map/ppermute | solution.py:301
  86.3 0.0 all-to-all-done.1.refs_0_
  86.3 0.0 copy-start
  86.3 0.8 copy-done
  87.1 2.9 %place.1 = bf16[128,3328]{1,0:T(8,128)(2,1)} custom-call(s32[26]{0:T(128)} %slot_ref.1, bf16[4,4,128,128]{3,2,1,0:T(8,128)(2,1)} %copy-done, bf16[4,3,128,128]{3,2,1,0:T(8,128)(2,1)} %copy-done.1), custom_call_target="tpu_custom_call" | custom-call | tf_op jit(solution)/shard_map/place/pallas_call | solution.py:107
  89.9 0.0 collective-permute-done.6.refs_1_
  89.9 0.0 copy-start.10
  89.9 2.3 %collective-permute-done.7.refs_2_ = bf16[432,128]{1,0:T(8,128)(2,1)S(1)} collective-permute-done((bf16[432,128]{1,0:T(8,128)(2,1)}, bf16[432,128]{1,0:T(8,128)(2,1)S(1)}, u32[]{:S(2)}, u32[]{:S(2)}) %collective-permute-start.7) | collective-permute-done | bytes 110624 | tf_op jit(solution)/shard_map/ppermute | solution.py:301
  92.2 0.0 copy-start.11
  92.2 0.0 collective-permute-done.8.refs_3_
  92.3 0.0 copy-start.12
  92.3 0.0 copy-done.10
  92.3 0.6 copy-done.11
  92.9 0.0 copy-done.12
  92.9 2.0 %finish.1 = (f32[64,432]{1,0:T(8,128)}, f32[432,64]{1,0:T(8,128)}) custom-call(f32[432,128]{1,0:T(8,128)} %get-tuple-element.25.refs_0_, bf16[432,128]{1,0:T(8,128)(2,1)} %copy-done.10, bf16[432,128]{1,0:T(8,128)(2,1)} %copy-done.11, bf16[432,128]{1,0:T(8,128)(2,1)} %copy-done.12), custom_call_target="tpu_custom_call" | custom-call | tf_op jit(solution)/shard_map/finish/pallas_call | solution.py:268
  94.9 1.7 %copy.13 = f32[432,64]{0,1:T(8,128)} copy(f32[432,64]{1,0:T(8,128)} %get-tuple-element.33) | data formatting | bytes 221184
Async XLA Ops:
  0.6 2.8 %collective-permute-start = (bf16[128,3456]{1,0:T(8,128)(2,1)}, bf16[128,3456]{1,0:T(8,128)(2,1)S(1)}, u32[]{:S(2)}, u32[]{:S(2)}) collective-permute-start(bf16[128,3456]{1,0:T(8,128)(2,1)} %x_ref.1), channel_id=1, source_target_pairs={{0,1},{1,0},{2,3},{3,2},{4,5},{5,4},{6,7},{7,6},{8,9},{9,8},{10,11... | collective-permute-start | bytes 2654216 | tf_op jit(solution)/shard_map/ppermute | solution.py:291
  1.2 3.5 %collective-permute-start.1 = (bf16[128,3456]{1,0:T(8,128)(2,1)}, bf16[128,3456]{1,0:T(8,128)(2,1)S(1)}, u32[]{:S(2)}, u32[]{:S(2)}) collective-permute-start(bf16[128,3456]{1,0:T(8,128)(2,1)} %ct_ref.1), channel_id=1, source_target_pairs={{0,1},{1,0},{2,3},{3,2},{4,5},{5,4},{6,7},{7,6},{8,9},{9,8},{10,11... | collective-permute-start | bytes 2654216 | tf_op jit(solution)/shard_map/ppermute | solution.py:292
  1.8 14.2 %copy-start.9 = (s32[128,224]{0,1:T(8,128)S(1)}, s32[128,224]{0,1:T(8,128)}, u32[]{:S(2)}) copy-start(s32[128,224]{0,1:T(8,128)} %param.8) | copy-start | bytes 344068
  1.9 15.0 %copy-start.13 = (s32[128,26]{0,1:T(8,128)S(1)}, s32[128,26]{0,1:T(8,128)}, u32[]{:S(2)}) copy-start(s32[128,26]{0,1:T(8,128)} %param.9) | copy-start | bytes 39940
  3.5 1.3 %copy-start.3 = (bf16[128,3456]{1,0:T(8,128)(2,1)}, bf16[128,3456]{1,0:T(8,128)(2,1)S(1)}, u32[]{:S(2)}) copy-start(bf16[128,3456]{1,0:T(8,128)(2,1)S(1)} %collective-permute-done.xs_ref) | copy-start | bytes 2654212
  4.7 0.9 copy-start.4
  13.2 51.1 %collective-permute-start.3 = (bf16[2,4,224,128]{3,2,1,0:T(8,128)(2,1)}, bf16[2,4,224,128]{3,2,1,0:T(8,128)(2,1)S(1)}, u32[]{:S(2)}, u32[]{:S(2)}) collective-permute-start(bf16[2,4,224,128]{3,2,1,0:T(8,128)(2,1)} %get-tuple-element.20), channel_id=1, source_target_pairs={{0,4},{4,0},{8,12},{12,8},{16,20},{20,16},{24,28},{28,24},{1,5},{5... | collective-permute-start | bytes 1376264 | tf_op jit(solution)/shard_map/ppermute | solution.py:296
  19.3 8.3 %all-to-all-start = ((s32[4,56,128]{2,1,0:T(8,128)}), s32[4,56,128]{2,1,0:T(8,128)S(1)}, u32[]{:S(2)}, u32[]{:S(2)}) async-start(s32[4,56,128]{2,1,0:T(8,128)} %bitcast.6), calls=%async_computation | async-start | bytes 229376 | tf_op jit(solution)/shard_map/all_to_all | solution.py:327
  22.6 41.6 %collective-permute-start.2 = (bf16[2,4,208,128]{3,2,1,0:T(8,128)(2,1)}, bf16[2,4,208,128]{3,2,1,0:T(8,128)(2,1)S(1)}, u32[]{:S(2)}, u32[]{:S(2)}) collective-permute-start(bf16[2,4,208,128]{3,2,1,0:T(8,128)(2,1)} %get-tuple-element.19), channel_id=1, source_target_pairs={{0,2},{1,3},{2,0},{3,1},{4,6},{5,7},{6,4},{7,5},{8,10},{9,11},{10,... | collective-permute-start | bytes 1277960 | tf_op jit(solution)/shard_map/ppermute | solution.py:295
  27.6 0.6 copy-start.2
  41.0 19.8 %all-to-all-start.2 = ((bf16[4,3,128,128]{3,2,1,0:T(8,128)(2,1)}), bf16[4,3,128,128]{3,2,1,0:T(8,128)(2,1)S(1)}, u32[]{:S(2)}, u32[]{:S(2)}) async-start(bf16[4,3,128,128]{3,2,1,0:T(8,128)(2,1)} %pool_slots.3), calls=%async_computation.2 | async-start | bytes 786432 | tf_op jit(solution)/shard_map/all_to_all | solution.py:337
  60.8 7.2 %copy-start.1 = (bf16[4,3,128,128]{3,2,1,0:T(8,128)(2,1)}, bf16[4,3,128,128]{3,2,1,0:T(8,128)(2,1)S(1)}, u32[]{:S(2)}) copy-start(bf16[4,3,128,128]{3,2,1,0:T(8,128)(2,1)S(1)} %all-to-all-done.2.refs_1_) | copy-start | bytes 1179652
  60.8 25.5 %all-to-all-start.1 = ((bf16[4,4,128,128]{3,2,1,0:T(8,128)(2,1)}), bf16[4,4,128,128]{3,2,1,0:T(8,128)(2,1)S(1)}, u32[]{:S(2)}, u32[]{:S(2)}) async-start(bf16[4,4,128,128]{3,2,1,0:T(8,128)(2,1)} %pool_slots.2), calls=%async_computation.1 | async-start | bytes 1048576 | tf_op jit(solution)/shard_map/all_to_all | solution.py:337
  64.3 0.8 copy-start.6
  64.3 0.9 copy-start.5
  68.0 10.0 %collective-permute-start.5 = (bf16[4,224,128]{2,1,0:T(8,128)(2,1)}, bf16[4,224,128]{2,1,0:T(8,128)(2,1)S(1)}, u32[]{:S(2)}, u32[]{:S(2)}) collective-permute-start(bf16[4,224,128]{2,1,0:T(8,128)(2,1)} %get-tuple-element.24), channel_id=1, source_target_pairs={{0,2},{1,3},{2,0},{3,1},{4,6},{5,7},{6,4},{7,5},{8,10},{9,11},{10,... | collective-permute-start | bytes 688136 | tf_op jit(solution)/shard_map/ppermute | solution.py:299
  70.0 7.2 %collective-permute-start.4 = (bf16[4,208,128]{2,1,0:T(8,128)(2,1)}, bf16[4,208,128]{2,1,0:T(8,128)(2,1)S(1)}, u32[]{:S(2)}, u32[]{:S(2)}) collective-permute-start(bf16[4,208,128]{2,1,0:T(8,128)(2,1)} %get-tuple-element.23), channel_id=1, source_target_pairs={{0,4},{4,0},{8,12},{12,8},{16,20},{20,16},{24,28},{28,24},{1,5},{5... | collective-permute-start | bytes 638984 | tf_op jit(solution)/shard_map/ppermute | solution.py:298
  77.2 0.8 copy-start.8
  78.0 0.7 copy-start.7
  80.7 9.2 %collective-permute-start.6 = (bf16[432,128]{1,0:T(8,128)(2,1)}, bf16[432,128]{1,0:T(8,128)(2,1)S(1)}, u32[]{:S(2)}, u32[]{:S(2)}) collective-permute-start(bf16[432,128]{1,0:T(8,128)(2,1)} %get-tuple-element.26), channel_id=1, source_target_pairs={{0,8},{4,12},{8,16},{12,20},{16,24},{20,28},{24,0},{28,4},{1,9},{5... | collective-permute-start | bytes 331784 | tf_op jit(solution)/shard_map/ppermute | solution.py:301
  82.3 9.9 %collective-permute-start.7 = (bf16[432,128]{1,0:T(8,128)(2,1)}, bf16[432,128]{1,0:T(8,128)(2,1)S(1)}, u32[]{:S(2)}, u32[]{:S(2)}) collective-permute-start(bf16[432,128]{1,0:T(8,128)(2,1)} %get-tuple-element.27), channel_id=1, source_target_pairs={{0,16},{4,20},{8,24},{12,28},{16,0},{20,4},{24,8},{28,12},{1,17},{... | collective-permute-start | bytes 331784 | tf_op jit(solution)/shard_map/ppermute | solution.py:301
  84.9 7.4 %collective-permute-start.8 = (bf16[432,128]{1,0:T(8,128)(2,1)}, bf16[432,128]{1,0:T(8,128)(2,1)S(1)}, u32[]{:S(2)}, u32[]{:S(2)}) collective-permute-start(bf16[432,128]{1,0:T(8,128)(2,1)} %get-tuple-element.28), channel_id=1, source_target_pairs={{0,24},{4,28},{8,0},{12,4},{16,8},{20,12},{24,16},{28,20},{1,25},{... | collective-permute-start | bytes 331784 | tf_op jit(solution)/shard_map/ppermute | solution.py:301
  86.3 0.8 copy-start
  89.9 2.3 %copy-start.10 = (bf16[432,128]{1,0:T(8,128)(2,1)}, bf16[432,128]{1,0:T(8,128)(2,1)S(1)}, u32[]{:S(2)}) copy-start(bf16[432,128]{1,0:T(8,128)(2,1)S(1)} %collective-permute-done.6.refs_1_) | copy-start | bytes 331780
  92.2 0.6 copy-start.11
  92.3 0.6 copy-start.12

commit v2 on v1

v2 whole, which is shorter than its diff:
```python
import functools
import math

import jax
import jax.numpy as jnp
from jax import lax
from jax.experimental import pallas as pl
from jax.experimental.pallas import tpu as pltpu
from jax.sharding import PartitionSpec as P


F32 = jnp.float32
BF16 = jnp.bfloat16
LANES = 128


def room(mebibytes):
    return pltpu.CompilerParams(vmem_limit_bytes=mebibytes * 2**20)


def whole(memory=pltpu.VMEM):
    return pl.BlockSpec(memory_space=memory)


def in_hbm(x):
    return pltpu.with_memory_space_constraint(x, pltpu.HBM)


def mask_ids_kernel(slot_ref, ids_ref, lens_ref, out_ref, *, maxlen, rows):
    entries, batch = out_ref.shape
    feats = lens_ref.shape[0]
    slot_of_row = lax.broadcasted_iota(jnp.int32, (entries, feats), 0) // maxlen
    hit = (slot_of_row == slot_ref[...]).astype(F32)
    lens = jnp.dot(hit, lens_ref[...].astype(F32), preferred_element_type=F32)
    place = lax.broadcasted_iota(jnp.int32, (entries, batch), 0) % maxlen
    keep = place.astype(F32) + 0.5 < lens
    out_ref[...] = jnp.where(keep, ids_ref[...], rows)


def mask_ids(slot_of_table, ids, lengths, maxlen, rows):
    return pl.pallas_call(
        functools.partial(mask_ids_kernel, maxlen=maxlen, rows=rows),
        in_specs=[whole()] * 3,
        out_specs=whole(),
        out_shape=jax.ShapeDtypeStruct((ids.shape[1], ids.shape[0]), jnp.int32),
        compiler_params=room(4),
        name="mask_ids",
    )(slot_of_table.reshape(1, -1), ids.T, lengths.T)


def pool_kernel(ids_ref, table_ref, out_ref, wide_ref, sum_ref, *rest, first, chunk):
    rows, width = table_ref.shape[1:]
    groups, _, batch, _ = out_ref.shape
    near, sem = rest[:groups], rest[groups]
    maxlen = near[0].shape[0]
    step, steps = pl.program_id(0), pl.num_programs(0)

    def fetch(g, at):
        start = pl.multiple_of((first + at) * maxlen, maxlen)
        return pltpu.make_async_copy(ids_ref.at[g, pl.ds(start, maxlen)], near[g], sem.at[g])

    @pl.when(step == 0)
    def _():
        for g in range(groups):
            fetch(g, 0).start()

    def widen(i, carry):
        start = pl.multiple_of(i * chunk, chunk)
        wide_ref[pl.ds(start, chunk), :] = table_ref[0, pl.ds(start, chunk), :].astype(F32)
        return carry

    lax.fori_loop(0, rows // chunk, widen, 0)
    wide_ref[pl.ds(rows, 8), :] = jnp.zeros((8, width), F32)
    for g in range(groups):
        fetch(g, step).wait()
        for b in range(batch):
            total = wide_ref[pl.ds(near[g][0, b], 1), :]
            for k in range(1, maxlen):
                total = total + wide_ref[pl.ds(near[g][k, b], 1), :]
            sum_ref[pl.ds(b, 1), :] = total
        out_ref[g, 0] = sum_ref[...].astype(BF16)

        @pl.when(step + 1 < steps)
        def _(g=g):
            fetch(g, step + 1).start()


def pool_slots(ids, tables, first, count, maxlen):
    groups, _, batch = ids.shape
    rows, width = tables.shape[1:]
    return pl.pallas_call(
        functools.partial(pool_kernel, first=first, chunk=math.gcd(rows, 512)),
        grid=(count,),
        in_specs=[
            pl.BlockSpec(memory_space=pl.ANY),
            pl.BlockSpec((1, rows, width), lambda s: (s + first, 0, 0)),
        ],
        out_specs=pl.BlockSpec((groups, 1, batch, width), lambda s: (0, s, 0, 0)),
        out_shape=jax.ShapeDtypeStruct((groups, count, batch, width), BF16),
        scratch_shapes=[pltpu.VMEM((rows + 8, width), F32), pltpu.VMEM((batch, width), F32)]
        + [pltpu.SMEM((maxlen, batch), jnp.int32)] * groups
        + [pltpu.SemaphoreType.DMA((groups,))],
        compiler_params=room(12),
        name="pool_slots",
    )(ids, in_hbm(tables))


def place_kernel(slot_ref, *refs, slots, firsts, counts):
    parts, out_ref = refs[:-1], refs[-1]
    width = parts[0].shape[3]
    for f in range(slot_ref.shape[0]):
        slot = slot_ref[f]
        owner = slot // slots
        local = slot - owner * slots
        for part, first, count in zip(parts, firsts, counts):

            def put(part=part, first=first, f=f):
                out_ref[:, f * width : (f + 1) * width] = part[owner, local - first]

            if len(parts) == 1:
                put()
            else:
                pl.when((local >= first) & (local < first + count))(put)


def place(slot_of_table, parts, firsts, counts, slots):
    batch, width = parts[0].shape[2:]
    feats = slot_of_table.shape[0]
    return pl.pallas_call(
        functools.partial(place_kernel, slots=slots, firsts=firsts, counts=counts),
        in_specs=[whole(pltpu.SMEM)] + [whole()] * len(parts),
        out_specs=whole(),
        out_shape=jax.ShapeDtypeStruct((batch, feats * width), BF16),
        compiler_params=room(8),
        name="place",
    )(slot_of_table, *parts)


def grads_kernel(pos_ref, x_ref, ct_ref, xs_ref, cts_ref, down_ref, up_ref, *refs, owners, groups):
    tall, far = owners // 2, groups // 2
    outs = refs[: 2 * tall]
    both_ref, sum_ref = refs[2 * tall :]
    core, y, x, z = pos_ref[0], pos_ref[1], pos_ref[2], pos_ref[3]
    batch, wide = x_ref.shape
    rank = down_ref.shape[1]
    part = rank // owners
    pair = 2 * batch
    for at, (a_ref, b_ref) in enumerate(((x_ref, ct_ref), (xs_ref, cts_ref))):
        a = a_ref[...]
        both_ref[pl.ds(at * batch, batch), :] = (b_ref[...].astype(F32) * a.astype(F32)).astype(BF16)
        both_ref[pl.ds(pair + at * batch, batch), :] = a
    low = jnp.dot(both_ref[pl.ds(pair, pair), :], down_ref[...], preferred_element_type=F32)
    dlow = lax.dot_general(
        both_ref[pl.ds(0, pair), :],
        up_ref[...],
        (((1,), (1,)), ((), ())),
        preferred_element_type=F32,
    )
    none = jnp.zeros((pair, part), F32)
    columns = []
    for ry in range(tall):
        owner = 2 * lax.rem(y + ry, tall) + core
        lo, dl = none, none
        for t in range(owners):
            lo = jnp.where(owner == t, low[:, t * part : (t + 1) * part], lo)
            dl = jnp.where(owner == t, dlow[:, t * part : (t + 1) * part], dl)
        columns.append(
            jnp.concatenate(
                [jnp.concatenate([lo, none], axis=1), jnp.concatenate([none, dl], axis=1)], axis=0
            )
        )
    right = jnp.concatenate(columns, axis=1).astype(BF16)
    step = math.gcd(wide, 384)
    for d in range(0, wide, step):
        sum_ref[pl.ds(d, step), :] = lax.dot_general(
            both_ref[:, d : d + step], right, (((0,), (0,)), ((), ())), preferred_element_type=F32
        )
    each = wide // groups
    block = 2 * part
    for r in range(far):
        for rx in range(2):
            g = 2 * lax.rem(z + r, far) + (x + rx - 2 * x * rx)
            start = pl.multiple_of(g * each, 16)
            for ry in range(tall):
                out = outs[rx * tall + ry]
                cols = slice(ry * block, (ry + 1) * block)
                out[r] = sum_ref[pl.ds(start, each), cols].astype(out.dtype)


def part_grads(pos, x, ct, xs, cts, down, up, owners, groups):
    wide, rank = down.shape
    batch = x.shape[0]
    tall, far = owners // 2, groups // 2
    block = 2 * (rank // owners)
    shape = (far, wide // groups, block)
    return pl.pallas_call(
        functools.partial(grads_kernel, owners=owners, groups=groups),
        in_specs=[whole(pltpu.SMEM)] + [whole()] * 6,
        out_specs=[whole()] * (2 * tall),
        out_shape=[jax.ShapeDtypeStruct(shape, BF16 if i else F32) for i in range(2 * tall)],
        scratch_shapes=[
            pltpu.VMEM((4 * batch, wide), BF16),
            pltpu.VMEM((wide, tall * block), F32),
        ],
        compiler_params=room(24),
        name="part_grads",
    )(pos, in_hbm(x), in_hbm(ct), xs, cts, in_hbm(down), in_hbm(up))


def fold_kernel(keep, *refs, far):
    came, outs = refs[:-far], refs[-far:]
    for r in range(far):
        total = keep[r]
        for one in came:
            total = total + one[r].astype(F32)
        outs[r][...] = total.astype(outs[r].dtype)


def fold(keep, came):
    far, rows, block = keep.shape
    return pl.pallas_call(
        functools.partial(fold_kernel, far=far),
        in_specs=[whole()] * (1 + len(came)),
        out_specs=[whole()] * far,
        out_shape=[jax.ShapeDtypeStruct((rows, block), BF16 if r else F32) for r in range(far)],
        compiler_params=room(12),
        name="fold",
    )(keep, *came)


def finish_kernel(*refs, factor):
    up_ref, down_ref = refs[-2:]
    total = refs[0][...]
    for r in refs[1:-2]:
        total = total + r[...].astype(F32)
    total = total * factor
    half = total.shape[1] // 2
    flat = total.T
    up_ref[...] = flat[:half, :]
    down_ref[...] = flat[half:, :]


def finish(keep, came, factor):
    rows, block = keep.shape
    half = block // 2
    shape = jax.ShapeDtypeStruct
    up, down = pl.pallas_call(
        functools.partial(finish_kernel, factor=factor),
        in_specs=[whole()] * (1 + len(came)),
        out_specs=[whole()] * 2,
        out_shape=[shape((half, rows), F32)] * 2,
        compiler_params=room(8),
        name="finish",
    )(keep, *came)
    return up, down.T


def exchange_start(x, ct, up, down, after):
    owners, groups = lax.axis_size("tbl"), lax.axis_size("grp")
    tall = owners // 2
    t, g = lax.axis_index("tbl"), lax.axis_index("grp")
    pos = jnp.stack([t % 2, t // 2, g % 2, g // 2]).astype(jnp.int32)
    other_core = [(i, i ^ 1) for i in range(owners)]
    xs = lax.ppermute(x, "tbl", other_core)
    cts = lax.ppermute(ct, "tbl", other_core)
    xs, cts, after = lax.optimization_barrier((xs, cts, after))
    parts = part_grads(pos, x, ct, xs, cts, down, up, owners, groups)

    def to(rx, ry):
        return [
            (i * owners + j, (i ^ rx) * owners + 2 * ((j // 2 + ry) % tall) + j % 2)
            for i in range(groups)
            for j in range(owners)
        ]

    came = []
    for i in range(1, 2 * tall):
        came.append(lax.ppermute(parts[i], ("grp", "tbl"), to(i // tall, i % tall)))
    return parts[0], came, after


def exchange_end(keep, came, factor):
    groups = lax.axis_size("grp")
    far = groups // 2

    def to_z(r):
        return [(i, 2 * ((i // 2 + r) % far) + i % 2) for i in range(groups)]

    out = fold(keep, came)
    last = []
    for r in range(1, far):
        last.append(lax.ppermute(out[r], "grp", to_z(r)))
    return finish(out[0], last, factor)


def grads_plain(x, ct, up, down, factor):
    low = jnp.dot(x, down, preferred_element_type=F32).astype(BF16)
    dz = (ct.astype(F32) * x.astype(F32)).astype(BF16)
    dlow = jnp.dot(dz, up.T, preferred_element_type=F32).astype(BF16)
    part_up = jnp.dot(low.T, dz, preferred_element_type=F32) * factor
    part_down = jnp.dot(x.T, dlow, preferred_element_type=F32) * factor
    owner_up = lax.psum_scatter(part_up, "tbl", scatter_dimension=0, tiled=True)
    owner_down = lax.psum_scatter(part_down, "tbl", scatter_dimension=1, tiled=True)
    return (
        lax.psum_scatter(owner_up, "grp", scatter_dimension=1, tiled=True),
        lax.psum_scatter(owner_down, "grp", scatter_dimension=0, tiled=True),
    )


def on_device(ids, lengths, slot_of_table, tables, x, ct, up, down):
    owners, groups = lax.axis_size("tbl"), lax.axis_size("grp")
    batch = ids.shape[0]
    slots, rows = tables.shape[:2]
    maxlen = ids.shape[1] // (slots * owners)
    factor = 1.0 / math.sqrt(batch * owners * groups)
    tiled = by_exchange(owners, groups, *down.shape)

    masked = mask_ids(slot_of_table, ids, lengths, maxlen, rows)
    if tiled:
        keep, came, masked = exchange_start(x, ct, up, down, masked)
    got = lax.all_to_all(masked.reshape(owners, slots * maxlen, batch), "tbl", 0, 0)
    if tiled:
        got, keep = lax.optimization_barrier((got, keep))
    firsts, counts = (0,), (slots,)
    parts = []
    for first, count in zip(firsts, counts):
        pooled = pool_slots(got, tables, first, count, maxlen)
        parts.append(lax.all_to_all(pooled, "tbl", 0, 0))
    embedded = place(slot_of_table, parts, firsts, counts, slots)
    if tiled:
        grad_up, grad_down = exchange_end(keep, came, factor)
    else:
        grad_up, grad_down = grads_plain(x, ct, up, down, factor)
    return embedded, grad_up, grad_down


def by_exchange(owners, groups, wide, rank):
    each, part = wide // groups, rank // owners
    return owners % 2 == 0 and groups % 2 == 0 and each % 16 == 0 and 2 * part % LANES == 0


def solution(mesh):
    rows = P(("grp", "tbl"), None)
    return jax.shard_map(
        on_device,
        mesh=mesh,
        in_specs=(rows, rows, P(), P("tbl", None, None), rows, rows, P(), P()),
        out_specs=(rows, P("tbl", "grp"), P("grp", "tbl")),
        check_vma=False,
    )
```

time: 97.1 us -> 86.9 us (0.89)
  Pallas kernels: 48.1 us -> 29.3 us
  waiting for transfers between devices: 16.1 us -> 34 us
  starting transfers between devices: 23.3 us -> 18.6 us
  local copies, waits for them, and re-layouts: 7.83 us -> 3.82 us
    ppermute x9 -> x8, waiting for transfers between devices: 13.1 us -> 34 us  [the longest x3 27.9 us: exchange_start(): came.append(lax.ppermute(parts[i], ('grp', 'tbl'), to(i // tall, i % tall)))]
    pallas_call x4 -> x2, Pallas kernels: 34 us -> 20.4 us  [the longest x1 20.2 us: pool_slots(): pl.pallas_call(functools.partial(pool_kernel, first=first, chunk=math.gcd...]
    unnamed x31 -> x16, local copies, waits for them, and re-layouts: 7.83 us -> 3.82 us
    all_to_all x2 -> x1, starting transfers between devices: 6.93 us -> 3.65 us  [on_device(): parts.append(lax.all_to_all(pooled, 'tbl', 0, 0))]
    all_to_all x1, waiting for transfers between devices: 2.97 us -> 0.01 us  [on_device(): lax.all_to_all(masked.reshape(owners, slots * maxlen, batch), 'tbl', 0, 0)]
    ppermute x9 -> x8, starting transfers between devices: 13 us -> 10.8 us  [the longest x3 6.06 us: exchange_end(): last.append(lax.ppermute(out[r], 'grp', to_z(r)))]
    pallas_call x1, Pallas kernels: 7.58 us -> 5.53 us  [part_grads(): pl.pallas_call(functools.partial(grads_kernel, owners=owners, groups=grou...]
    pallas_call x1, Pallas kernels: 1.99 us -> 0.83 us  [finish(): pl.pallas_call(functools.partial(finish_kernel, factor=factor), in_specs=...]
  transfers between devices with their start and end apart: 12 -> 10, of which waited for: 6 -> 4; matrix products, arithmetic and copies ran while one was open for 2% -> 0% of each run, Pallas kernels for 40% -> 8%
where the time goes in v2:
time: 86.9 us; the launch traced here: 86.5 us
  waiting for transfers between devices  34 us (39%)
  Pallas kernels  29.3 us (34%)
  starting transfers between devices  18.6 us (21%)
  local copies, waits for them, and re-layouts  3.82 us (4%)
    ppermute x3, waiting for transfers between devices, exchange_start(): came.append(lax.ppermute(parts[i], ('grp', 'tbl'), to(i // tall, i % tall)))  27.9 us
    pallas_call x1, Pallas kernels, pool_slots(): pl.pallas_call(functools.partial(pool_kernel, first=first, chunk=math.gcd...  20.2 us
    ppermute x3, starting transfers between devices, exchange_end(): last.append(lax.ppermute(out[r], 'grp', to_z(r)))  6.06 us
    ppermute x3, waiting for transfers between devices, exchange_end(): last.append(lax.ppermute(out[r], 'grp', to_z(r)))  5.74 us
    pallas_call x1, Pallas kernels, part_grads(): pl.pallas_call(functools.partial(grads_kernel, owners=owners, groups=grou...  5.53 us
    all_to_all x1, starting transfers between devices, on_device(): lax.all_to_all(masked.reshape(owners, slots * maxlen, batch), 'tbl', 0, 0)  4.15 us
    ppermute x3, starting transfers between devices, exchange_start(): came.append(lax.ppermute(parts[i], ('grp', 'tbl'), to(i // tall, i % tall)))  4.09 us
    unnamed x16, local copies, waits for them, and re-layouts  3.82 us
  transfers between devices with their start and end apart: 10, of which 4 were waited for; matrix products, arithmetic and copies ran while one was open for 0% of the time, Pallas kernels for 8%

profile of v2, /device:TPU:0, one launch (start us, length us, event | category | flops | bytes accessed | tf_op | source)
XLA Modules:
  0.0 86.5 jit_solution(9808809174730711095)
XLA Ops:
  0.6 0.6 collective-permute-start
  1.2 0.1 collective-permute-start.1
  1.3 0.0 copy-start
  1.3 0.9 %copy-done = s32[128,224]{0,1:T(8,128)S(1)} copy-done((s32[128,224]{0,1:T(8,128)S(1)}, s32[128,224]{0,1:T(8,128)}, u32[]{:S(2)}) %copy-start) | copy-done | bytes 114712
  2.2 0.0 copy-start.1
  2.2 0.7 copy-done.1
  2.9 0.0 copy-start.2
  2.9 0.7 copy-done.2
  3.5 0.8 mask_ids.1
  4.3 0.0 collective-permute-done.xs_ref
  4.3 0.4 collective-permute-done.1.cts_ref
  4.7 4.1 %all-to-all-start = ((s32[4,56,128]{2,1,0:T(8,128)}), s32[4,56,128]{2,1,0:T(8,128)S(1)}, u32[]{:S(2)}, u32[]{:S(2)}) async-start(s32[4,56,128]{2,1,0:T(8,128)} %bitcast.3), calls=%async_computation | async-start | bytes 229376 | tf_op jit(solution)/shard_map/all_to_all | solution.py:321
  8.9 0.1 pad_add_fusion.pos_ref
  8.9 5.5 %part_grads.1 = (f32[4,432,128]{2,1,0:T(8,128)S(1)}, bf16[4,432,128]{2,1,0:T(8,128)(2,1)S(1)}, bf16[4,432,128]{2,1,0:T(8,128)(2,1)S(1)}, bf16[4,432,128]{2,1,0:T(8,128)(2,1)S(1)}) custom-call(s32[4]{0:T(128)S(1)} %pad_add_fusion.pos_ref, bf16[128,3456]{1,0:T(8,128)(2,1)} %x_ref.1, bf16[128,3456]{1,0:T(8,128)(2,1)} %ct_ref.1, ...), custom_call_target="tpu_custom_call" | custom-call | tf_op jit(solution)/shard_map/part_grads/pallas_call | solution.py:196
  14.5 0.0 copy-start.4
  14.5 0.8 copy-done.4
  15.3 0.0 copy-start.6
  15.3 0.8 copy-done.6
  16.0 0.0 all-to-all-done.ids_ref
  16.0 20.2 %pool_slots.1 = bf16[4,7,128,128]{3,2,1,0:T(8,128)(2,1)} custom-call(s32[4,56,128]{2,1,0:T(8,128)S(1)} %all-to-all-done.ids_ref, bf16[7,6144,128]{2,1,0:T(8,128)(2,1)} %table_ref.1), custom_call_target="tpu_custom_call" | custom-call | tf_op jit(solution)/shard_map/pool_slots/pallas_call | solution.py:91
  36.2 0.0 copy-start.7
  36.3 0.0 copy-start.5
  36.3 3.6 %all-to-all-start.1 = ((bf16[4,7,128,128]{3,2,1,0:T(8,128)(2,1)}), bf16[4,7,128,128]{3,2,1,0:T(8,128)(2,1)S(1)}, u32[]{:S(2)}, u32[]{:S(2)}) async-start(bf16[4,7,128,128]{3,2,1,0:T(8,128)(2,1)} %pool_slots.1), calls=%async_computation.1 | async-start | bytes 1835008 | tf_op jit(solution)/shard_map/all_to_all | solution.py:328
  39.9 0.0 copy-start.3
  39.9 0.0 copy-done.7
  39.9 2.1 %collective-permute-start.2 = (bf16[4,432,128]{2,1,0:T(8,128)(2,1)S(1)}, bf16[4,432,128]{2,1,0:T(8,128)(2,1)S(1)}, u32[]{:S(2)}, u32[]{:S(2)}) collective-permute-start(bf16[4,432,128]{2,1,0:T(8,128)(2,1)S(1)} %copy-done.7), channel_id=1, source_target_pairs={{0,2},{1,3},{2,0},{3,1},{4,6},{5,7},{6,4},{7,5},{8,10},{9,11},{10,... | collective-permute-start | bytes 1327112 | tf_op jit(solution)/shard_map/ppermute | solution.py:278
  42.1 0.0 copy-done.5
  42.1 2.0 %collective-permute-start.3 = (bf16[4,432,128]{2,1,0:T(8,128)(2,1)S(1)}, bf16[4,432,128]{2,1,0:T(8,128)(2,1)S(1)}, u32[]{:S(2)}, u32[]{:S(2)}) collective-permute-start(bf16[4,432,128]{2,1,0:T(8,128)(2,1)S(1)} %copy-done.5), channel_id=1, source_target_pairs={{0,4},{1,5},{2,6},{3,7},{4,0},{5,1},{6,2},{7,3},{8,12},{9,13},{10,... | collective-permute-start | bytes 1327112 | tf_op jit(solution)/shard_map/ppermute | solution.py:278
  44.0 0.0 collective-permute-start.4
  44.0 27.9 %collective-permute-done.2.refs_0_ = bf16[4,432,128]{2,1,0:T(8,128)(2,1)S(1)} collective-permute-done((bf16[4,432,128]{2,1,0:T(8,128)(2,1)S(1)}, bf16[4,432,128]{2,1,0:T(8,128)(2,1)S(1)}, u32[]{:S(2)}, u32[]{:S(2)}) %collective-permute-start.2) | collective-permute-done | bytes 442400 | tf_op jit(solution)/shard_map/ppermute | solution.py:278
  71.9 0.0 collective-permute-done.3.refs_1_
  71.9 0.0 collective-permute-done.4.refs_2_
  71.9 0.2 fold.1
  72.1 2.1 %collective-permute-start.5 = (bf16[432,128]{1,0:T(8,128)(2,1)S(1)}, bf16[432,128]{1,0:T(8,128)(2,1)S(1)}, u32[]{:S(2)}, u32[]{:S(2)}) collective-permute-start(bf16[432,128]{1,0:T(8,128)(2,1)S(1)} %get-tuple-element.28), channel_id=1, source_target_pairs={{0,8},{4,12},{8,16},{12,20},{16,24},{20,28},{24,0},{28,4},{1,9},{5... | collective-permute-start | bytes 331784 | tf_op jit(solution)/shard_map/ppermute | solution.py:292
  74.2 2.6 %collective-permute-start.6 = (bf16[432,128]{1,0:T(8,128)(2,1)S(1)}, bf16[432,128]{1,0:T(8,128)(2,1)S(1)}, u32[]{:S(2)}, u32[]{:S(2)}) collective-permute-start(bf16[432,128]{1,0:T(8,128)(2,1)S(1)} %get-tuple-element.29), channel_id=1, source_target_pairs={{0,16},{4,20},{8,24},{12,28},{16,0},{20,4},{24,8},{28,12},{1,17},{... | collective-permute-start | bytes 331784 | tf_op jit(solution)/shard_map/ppermute | solution.py:292
  76.8 1.3 %collective-permute-start.7 = (bf16[432,128]{1,0:T(8,128)(2,1)S(1)}, bf16[432,128]{1,0:T(8,128)(2,1)S(1)}, u32[]{:S(2)}, u32[]{:S(2)}) collective-permute-start(bf16[432,128]{1,0:T(8,128)(2,1)S(1)} %get-tuple-element.30), channel_id=1, source_target_pairs={{0,24},{4,28},{8,0},{12,4},{16,8},{20,12},{24,16},{28,20},{1,25},{... | collective-permute-start | bytes 331784 | tf_op jit(solution)/shard_map/ppermute | solution.py:292
  78.2 2.0 %collective-permute-done.5.refs_1_ = bf16[432,128]{1,0:T(8,128)(2,1)S(1)} collective-permute-done((bf16[432,128]{1,0:T(8,128)(2,1)S(1)}, bf16[432,128]{1,0:T(8,128)(2,1)S(1)}, u32[]{:S(2)}, u32[]{:S(2)}) %collective-permute-start.5) | collective-permute-done | bytes 110624 | tf_op jit(solution)/shard_map/ppermute | solution.py:292
  80.1 3.8 %collective-permute-done.6.refs_2_ = bf16[432,128]{1,0:T(8,128)(2,1)S(1)} collective-permute-done((bf16[432,128]{1,0:T(8,128)(2,1)S(1)}, bf16[432,128]{1,0:T(8,128)(2,1)S(1)}, u32[]{:S(2)}, u32[]{:S(2)}) %collective-permute-start.6) | collective-permute-done | bytes 110624 | tf_op jit(solution)/shard_map/ppermute | solution.py:292
  83.9 0.0 collective-permute-done.7.refs_3_
  83.9 0.8 finish.1
  84.7 0.0 all-to-all-done.1.refs_0_
  84.8 0.0 copy-done.3
  84.8 1.7 %place.1 = bf16[128,3328]{1,0:T(8,128)(2,1)} custom-call(s32[26]{0:T(128)S(1)} %copy-done.3, bf16[4,7,128,128]{3,2,1,0:T(8,128)(2,1)S(1)} %all-to-all-done.1.refs_0_), custom_call_target="tpu_custom_call" | custom-call | tf_op jit(solution)/shard_map/place/pallas_call | solution.py:129
Async XLA Ops:
  0.6 3.7 %collective-permute-start = (bf16[128,3456]{1,0:T(8,128)(2,1)}, bf16[128,3456]{1,0:T(8,128)(2,1)S(1)}, u32[]{:S(2)}, u32[]{:S(2)}) collective-permute-start(bf16[128,3456]{1,0:T(8,128)(2,1)} %x_ref.1), channel_id=1, source_target_pairs={{0,1},{1,0},{2,3},{3,2},{4,5},{5,4},{6,7},{7,6},{8,9},{9,8},{10,11... | collective-permute-start | bytes 2654216 | tf_op jit(solution)/shard_map/ppermute | solution.py:264
  1.2 3.5 %collective-permute-start.1 = (bf16[128,3456]{1,0:T(8,128)(2,1)}, bf16[128,3456]{1,0:T(8,128)(2,1)S(1)}, u32[]{:S(2)}, u32[]{:S(2)}) collective-permute-start(bf16[128,3456]{1,0:T(8,128)(2,1)} %ct_ref.1), channel_id=1, source_target_pairs={{0,1},{1,0},{2,3},{3,2},{4,5},{5,4},{6,7},{7,6},{8,9},{9,8},{10,11... | collective-permute-start | bytes 2654216 | tf_op jit(solution)/shard_map/ppermute | solution.py:265
  1.3 0.9 %copy-start = (s32[128,224]{0,1:T(8,128)S(1)}, s32[128,224]{0,1:T(8,128)}, u32[]{:S(2)}) copy-start(s32[128,224]{0,1:T(8,128)} %param.8) | copy-start | bytes 344068
  2.2 0.7 copy-start.1
  2.9 0.7 copy-start.2
  4.7 11.3 %all-to-all-start = ((s32[4,56,128]{2,1,0:T(8,128)}), s32[4,56,128]{2,1,0:T(8,128)S(1)}, u32[]{:S(2)}, u32[]{:S(2)}) async-start(s32[4,56,128]{2,1,0:T(8,128)} %bitcast.3), calls=%async_computation | async-start | bytes 229376 | tf_op jit(solution)/shard_map/all_to_all | solution.py:321
  14.5 0.8 copy-start.4
  15.3 0.8 copy-start.6
  36.2 3.7 %copy-start.7 = (bf16[4,432,128]{2,1,0:T(8,128)(2,1)S(1)}, bf16[4,432,128]{2,1,0:T(8,128)(2,1)}, u32[]{:S(2)}) copy-start(bf16[4,432,128]{2,1,0:T(8,128)(2,1)} %copy-done.6) | copy-start | bytes 1327108
  36.3 5.8 %copy-start.5 = (bf16[4,432,128]{2,1,0:T(8,128)(2,1)S(1)}, bf16[4,432,128]{2,1,0:T(8,128)(2,1)}, u32[]{:S(2)}) copy-start(bf16[4,432,128]{2,1,0:T(8,128)(2,1)} %copy-done.4) | copy-start | bytes 1327108
  36.3 48.5 %all-to-all-start.1 = ((bf16[4,7,128,128]{3,2,1,0:T(8,128)(2,1)}), bf16[4,7,128,128]{3,2,1,0:T(8,128)(2,1)S(1)}, u32[]{:S(2)}, u32[]{:S(2)}) async-start(bf16[4,7,128,128]{3,2,1,0:T(8,128)(2,1)} %pool_slots.1), calls=%async_computation.1 | async-start | bytes 1835008 | tf_op jit(solution)/shard_map/all_to_all | solution.py:328
  39.9 44.8 %copy-start.3 = (s32[26]{0:T(128)S(1)}, s32[26]{0:T(128)}, u32[]{:S(2)}) copy-start(s32[26]{0:T(128)} %slot_ref.1) | copy-start | bytes 316
  39.9 32.0 %collective-permute-start.2 = (bf16[4,432,128]{2,1,0:T(8,128)(2,1)S(1)}, bf16[4,432,128]{2,1,0:T(8,128)(2,1)S(1)}, u32[]{:S(2)}, u32[]{:S(2)}) collective-permute-start(bf16[4,432,128]{2,1,0:T(8,128)(2,1)S(1)} %copy-done.7), channel_id=1, source_target_pairs={{0,2},{1,3},{2,0},{3,1},{4,6},{5,7},{6,4},{7,5},{8,10},{9,11},{10,... | collective-permute-start | bytes 1327112 | tf_op jit(solution)/shard_map/ppermute | solution.py:278
  42.1 29.8 %collective-permute-start.3 = (bf16[4,432,128]{2,1,0:T(8,128)(2,1)S(1)}, bf16[4,432,128]{2,1,0:T(8,128)(2,1)S(1)}, u32[]{:S(2)}, u32[]{:S(2)}) collective-permute-start(bf16[4,432,128]{2,1,0:T(8,128)(2,1)S(1)} %copy-done.5), channel_id=1, source_target_pairs={{0,4},{1,5},{2,6},{3,7},{4,0},{5,1},{6,2},{7,3},{8,12},{9,13},{10,... | collective-permute-start | bytes 1327112 | tf_op jit(solution)/shard_map/ppermute | solution.py:278
  44.0 27.9 %collective-permute-start.4 = (bf16[4,432,128]{2,1,0:T(8,128)(2,1)S(1)}, bf16[4,432,128]{2,1,0:T(8,128)(2,1)S(1)}, u32[]{:S(2)}, u32[]{:S(2)}) collective-permute-start(bf16[4,432,128]{2,1,0:T(8,128)(2,1)S(1)} %get-tuple-element.26), channel_id=1, source_target_pairs={{0,6},{1,7},{2,4},{3,5},{4,2},{5,3},{6,0},{7,1},{8,14},{9,15},{10,... | collective-permute-start | bytes 1327112 | tf_op jit(solution)/shard_map/ppermute | solution.py:278
  72.1 8.0 %collective-permute-start.5 = (bf16[432,128]{1,0:T(8,128)(2,1)S(1)}, bf16[432,128]{1,0:T(8,128)(2,1)S(1)}, u32[]{:S(2)}, u32[]{:S(2)}) collective-permute-start(bf16[432,128]{1,0:T(8,128)(2,1)S(1)} %get-tuple-element.28), channel_id=1, source_target_pairs={{0,8},{4,12},{8,16},{12,20},{16,24},{20,28},{24,0},{28,4},{1,9},{5... | collective-permute-start | bytes 331784 | tf_op jit(solution)/shard_map/ppermute | solution.py:292
  74.2 9.7 %collective-permute-start.6 = (bf16[432,128]{1,0:T(8,128)(2,1)S(1)}, bf16[432,128]{1,0:T(8,128)(2,1)S(1)}, u32[]{:S(2)}, u32[]{:S(2)}) collective-permute-start(bf16[432,128]{1,0:T(8,128)(2,1)S(1)} %get-tuple-element.29), channel_id=1, source_target_pairs={{0,16},{4,20},{8,24},{12,28},{16,0},{20,4},{24,8},{28,12},{1,17},{... | collective-permute-start | bytes 331784 | tf_op jit(solution)/shard_map/ppermute | solution.py:292
  76.8 7.1 %collective-permute-start.7 = (bf16[432,128]{1,0:T(8,128)(2,1)S(1)}, bf16[432,128]{1,0:T(8,128)(2,1)S(1)}, u32[]{:S(2)}, u32[]{:S(2)}) collective-permute-start(bf16[432,128]{1,0:T(8,128)(2,1)S(1)} %get-tuple-element.30), channel_id=1, source_target_pairs={{0,24},{4,28},{8,0},{12,4},{16,8},{20,12},{24,16},{28,20},{1,25},{... | collective-permute-start | bytes 331784 | tf_op jit(solution)/shard_map/ppermute | solution.py:292

commit v3 on v2

--- a/solution.py
+++ b/solution.py
@@ -45,7 +45,7 @@
         out_shape=jax.ShapeDtypeStruct((ids.shape[1], ids.shape[0]), jnp.int32),
         compiler_params=room(4),
         name="mask_ids",
-    )(slot_of_table.reshape(1, -1), ids.T, lengths.T)
+    )(in_hbm(slot_of_table.reshape(1, -1)), in_hbm(ids.T), in_hbm(lengths.T))
 
 
 def pool_kernel(ids_ref, table_ref, out_ref, wide_ref, sum_ref, *rest, first, chunk):
@@ -106,21 +106,29 @@
 
 
 def place_kernel(slot_ref, *refs, slots, firsts, counts):
-    parts, out_ref = refs[:-1], refs[-1]
+    parts, out_ref, sem = refs[:-2], refs[-2], refs[-1]
     width = parts[0].shape[3]
-    for f in range(slot_ref.shape[0]):
+    feats = slot_ref.shape[0]
+
+    def put(f, part, owner, local):
+        to = out_ref.at[:, pl.ds(f * width, width)]
+        return pltpu.make_async_copy(part.at[owner, local], to, sem.at[f])
+
+    for f in range(feats):
         slot = slot_ref[f]
         owner = slot // slots
         local = slot - owner * slots
         for part, first, count in zip(parts, firsts, counts):
-
-            def put(part=part, first=first, f=f):
-                out_ref[:, f * width : (f + 1) * width] = part[owner, local - first]
-
             if len(parts) == 1:
-                put()
+                put(f, part, owner, local).start()
             else:
-                pl.when((local >= first) & (local < first + count))(put)
+
+                @pl.when((local >= first) & (local < first + count))
+                def _(f=f, part=part, owner=owner, at=local - first):
+                    put(f, part, owner, at).start()
+
+    for f in range(feats):
+        put(f, parts[0], 0, 0).wait()
 
 
 def place(slot_of_table, parts, firsts, counts, slots):
@@ -128,28 +136,42 @@
     feats = slot_of_table.shape[0]
     return pl.pallas_call(
         functools.partial(place_kernel, slots=slots, firsts=firsts, counts=counts),
-        in_specs=[whole(pltpu.SMEM)] + [whole()] * len(parts),
-        out_specs=whole(),
+        in_specs=[whole(pltpu.SMEM)] + [whole(pl.ANY)] * len(parts),
+        out_specs=whole(pl.ANY),
         out_shape=jax.ShapeDtypeStruct((batch, feats * width), BF16),
-        compiler_params=room(8),
+        scratch_shapes=[pltpu.SemaphoreType.DMA((feats,))],
+        compiler_params=room(4),
         name="place",
     )(slot_of_table, *parts)
 
 
-def grads_kernel(pos_ref, x_ref, ct_ref, xs_ref, cts_ref, down_ref, up_ref, *refs, owners, groups):
+def grads_kernel(pos_ref, xs_ref, cts_ref, x_hbm, ct_hbm, down_hbm, up_hbm, *refs, owners, groups):
     tall, far = owners // 2, groups // 2
     outs = refs[: 2 * tall]
-    both_ref, sum_ref = refs[2 * tall :]
-    core, y, x, z = pos_ref[0], pos_ref[1], pos_ref[2], pos_ref[3]
+    both_ref, sum_ref, x_ref, ct_ref, down_ref, up_ref, sem = refs[2 * tall :]
+    core, y, x, z = pos_ref[0] & 1, pos_ref[0] >> 1, pos_ref[1] & 1, pos_ref[1] >> 1
     batch, wide = x_ref.shape
     rank = down_ref.shape[1]
     part = rank // owners
     pair = 2 * batch
-    for at, (a_ref, b_ref) in enumerate(((x_ref, ct_ref), (xs_ref, cts_ref))):
+    loads = [
+        pltpu.make_async_copy(src, dst, sem.at[i])
+        for i, (src, dst) in enumerate(
+            ((x_hbm, x_ref), (ct_hbm, ct_ref), (down_hbm, down_ref), (up_hbm, up_ref))
+        )
+    ]
+    for load in loads:
+        load.start()
+    for at, (a_ref, b_ref) in enumerate(((xs_ref, cts_ref), (x_ref, ct_ref))):
+        if at:
+            loads[0].wait()
+            loads[1].wait()
         a = a_ref[...]
         both_ref[pl.ds(at * batch, batch), :] = (b_ref[...].astype(F32) * a.astype(F32)).astype(BF16)
         both_ref[pl.ds(pair + at * batch, batch), :] = a
+    loads[2].wait()
     low = jnp.dot(both_ref[pl.ds(pair, pair), :], down_ref[...], preferred_element_type=F32)
+    loads[3].wait()
     dlow = lax.dot_general(
         both_ref[pl.ds(0, pair), :],
         up_ref[...],
@@ -195,16 +217,18 @@
     shape = (far, wide // groups, block)
     return pl.pallas_call(
         functools.partial(grads_kernel, owners=owners, groups=groups),
-        in_specs=[whole(pltpu.SMEM)] + [whole()] * 6,
+        in_specs=[whole(pltpu.SMEM)] + [whole()] * 2 + [whole(pl.ANY)] * 4,
         out_specs=[whole()] * (2 * tall),
-        out_shape=[jax.ShapeDtypeStruct(shape, BF16 if i else F32) for i in range(2 * tall)],
+        out_shape=[pltpu.VMEM(shape, BF16 if i else F32) for i in range(2 * tall)],
         scratch_shapes=[
             pltpu.VMEM((4 * batch, wide), BF16),
             pltpu.VMEM((wide, tall * block), F32),
-        ],
+        ]
+        + [pltpu.VMEM(a.shape, BF16) for a in (x, ct, down, up)]
+        + [pltpu.SemaphoreType.DMA((4,))],
         compiler_params=room(24),
         name="part_grads",
-    )(pos, in_hbm(x), in_hbm(ct), xs, cts, in_hbm(down), in_hbm(up))
+    )(pos, xs, cts, in_hbm(x), in_hbm(ct), in_hbm(down), in_hbm(up))
 
 
 def fold_kernel(keep, *refs, far):
@@ -259,7 +283,7 @@
     owners, groups = lax.axis_size("tbl"), lax.axis_size("grp")
     tall = owners // 2
     t, g = lax.axis_index("tbl"), lax.axis_index("grp")
-    pos = jnp.stack([t % 2, t // 2, g % 2, g // 2]).astype(jnp.int32)
+    pos = jnp.stack([t, g]).astype(jnp.int32)
     other_core = [(i, i ^ 1) for i in range(owners)]
     xs = lax.ppermute(x, "tbl", other_core)
     cts = lax.ppermute(ct, "tbl", other_core)

time: 86.9 us -> 87.8 us (1.010)
  local copies, waits for them, and re-layouts: 3.82 us -> 1.54 us
  Pallas kernels: 29.3 us -> 31.2 us
  waiting for transfers between devices: 34 us -> 35.4 us
    unnamed x16 -> x10, local copies, waits for them, and re-layouts: 3.82 us -> 1.54 us
    pallas_call x1, Pallas kernels: 5.53 us -> 6.66 us  [part_grads(): pl.pallas_call(functools.partial(grads_kernel, owners=owners, groups=grou...]
    pallas_call x1, Pallas kernels: 0.78 us -> 1.68 us  [mask_ids(): pl.pallas_call(functools.partial(mask_ids_kernel, maxlen=maxlen, rows=row...]
  transfers between devices with their start and end apart: 10 -> 10, of which waited for: 4 -> 5; matrix products, arithmetic and copies ran while one was open for 0% -> 0% of each run, Pallas kernels for 8% -> 11%
where the time goes in v3:
time: 87.8 us; the launch traced here: 87.5 us
  waiting for transfers between devices  35.4 us (40%)
  Pallas kernels  31.2 us (36%)
  starting transfers between devices  18.6 us (21%)
  local copies, waits for them, and re-layouts  1.54 us (2%)
    ppermute x3, waiting for transfers between devices, exchange_start(): came.append(lax.ppermute(parts[i], ('grp', 'tbl'), to(i // tall, i % tall)))  27.9 us
    pallas_call x1, Pallas kernels, pool_slots(): pl.pallas_call(functools.partial(pool_kernel, first=first, chunk=math.gcd...  20.2 us
    pallas_call x1, Pallas kernels, part_grads(): pl.pallas_call(functools.partial(grads_kernel, owners=owners, groups=grou...  6.66 us
    ppermute x3, starting transfers between devices, exchange_end(): last.append(lax.ppermute(out[r], 'grp', to_z(r)))  6.06 us
    ppermute x3, waiting for transfers between devices, exchange_end(): last.append(lax.ppermute(out[r], 'grp', to_z(r)))  5.75 us
    all_to_all x1, starting transfers between devices, on_device(): lax.all_to_all(masked.reshape(owners, slots * maxlen, batch), 'tbl', 0, 0)  4.15 us
    ppermute x3, starting transfers between devices, exchange_start(): came.append(lax.ppermute(parts[i], ('grp', 'tbl'), to(i // tall, i % tall)))  4.1 us
    all_to_all x1, starting transfers between devices, on_device(): parts.append(lax.all_to_all(pooled, 'tbl', 0, 0))  3.65 us
  transfers between devices with their start and end apart: 10, of which 5 were waited for; matrix products, arithmetic and copies ran while one was open for 0% of the time, Pallas kernels for 11%

profile of v3, /device:TPU:0, one launch (start us, length us, event | category | flops | bytes accessed | tf_op | source)
XLA Modules:
  0.0 87.5 jit_solution(15816272015389214322)
XLA Ops:
  0.6 0.6 collective-permute-start
  1.2 0.1 collective-permute-start.1
  1.3 1.7 %mask_ids.1 = s32[224,128]{1,0:T(8,128)} custom-call(s32[1,26]{1,0:T(1,128)} %bitcast.7, s32[224,128]{1,0:T(8,128)} %bitcast.8, s32[26,128]{1,0:T(8,128)} %bitcast.9), custom_call_target="tpu_custom_call" | custom-call | tf_op jit(solution)/shard_map/mask_ids/pallas_call | solution.py:41
  2.9 0.5 collective-permute-done.xs_ref
  3.5 1.3 %collective-permute-done.1.cts_ref = bf16[128,3456]{1,0:T(8,128)(2,1)S(1)} collective-permute-done((bf16[128,3456]{1,0:T(8,128)(2,1)}, bf16[128,3456]{1,0:T(8,128)(2,1)S(1)}, u32[]{:S(2)}, u32[]{:S(2)}) %collective-permute-start.1) | collective-permute-done | bytes 884768 | tf_op jit(solution)/shard_map/ppermute | solution.py:289
  4.7 4.1 %all-to-all-start = ((s32[4,56,128]{2,1,0:T(8,128)}), s32[4,56,128]{2,1,0:T(8,128)S(1)}, u32[]{:S(2)}, u32[]{:S(2)}) async-start(s32[4,56,128]{2,1,0:T(8,128)} %bitcast.3), calls=%async_computation | async-start | bytes 229376 | tf_op jit(solution)/shard_map/all_to_all | solution.py:345
  8.9 0.1 pad_add_fusion.pos_ref
  8.9 6.7 %part_grads.1 = (f32[4,432,128]{2,1,0:T(8,128)S(1)}, bf16[4,432,128]{2,1,0:T(8,128)(2,1)S(1)}, bf16[4,432,128]{2,1,0:T(8,128)(2,1)S(1)}, bf16[4,432,128]{2,1,0:T(8,128)(2,1)S(1)}) custom-call(s32[2]{0:T(128)S(1)} %pad_add_fusion.pos_ref, bf16[128,3456]{1,0:T(8,128)(2,1)S(1)} %collective-permute-done.xs_ref, ...), custom_call_target="tpu_custom_call" | custom-call | tf_op jit(solution)/shard_map/part_grads/pallas_call | solution.py:218
  15.6 0.0 copy-start.1
  15.6 0.8 copy-done.1
  16.4 0.0 copy-start.3
  16.4 0.8 copy-done.3
  17.1 0.0 all-to-all-done.ids_ref
  17.1 20.2 %pool_slots.1 = bf16[4,7,128,128]{3,2,1,0:T(8,128)(2,1)} custom-call(s32[4,56,128]{2,1,0:T(8,128)S(1)} %all-to-all-done.ids_ref, bf16[7,6144,128]{2,1,0:T(8,128)(2,1)} %table_ref.1), custom_call_target="tpu_custom_call" | custom-call | tf_op jit(solution)/shard_map/pool_slots/pallas_call | solution.py:91
  37.3 0.0 copy-start.4
  37.3 0.0 copy-start.2
  37.3 3.6 %all-to-all-start.1 = ((bf16[4,7,128,128]{3,2,1,0:T(8,128)(2,1)}), bf16[4,7,128,128]{3,2,1,0:T(8,128)(2,1)S(1)}, u32[]{:S(2)}, u32[]{:S(2)}) async-start(bf16[4,7,128,128]{3,2,1,0:T(8,128)(2,1)} %pool_slots.1), calls=%async_computation.1 | async-start | bytes 1835008 | tf_op jit(solution)/shard_map/all_to_all | solution.py:352
  41.0 0.0 copy-start
  41.0 0.0 copy-done.4
  41.0 2.1 %collective-permute-start.2 = (bf16[4,432,128]{2,1,0:T(8,128)(2,1)S(1)}, bf16[4,432,128]{2,1,0:T(8,128)(2,1)S(1)}, u32[]{:S(2)}, u32[]{:S(2)}) collective-permute-start(bf16[4,432,128]{2,1,0:T(8,128)(2,1)S(1)} %copy-done.4), channel_id=1, source_target_pairs={{0,2},{1,3},{2,0},{3,1},{4,6},{5,7},{6,4},{7,5},{8,10},{9,11},{10,... | collective-permute-start | bytes 1327112 | tf_op jit(solution)/shard_map/ppermute | solution.py:302
  43.1 0.0 copy-done.2
  43.1 2.0 %collective-permute-start.3 = (bf16[4,432,128]{2,1,0:T(8,128)(2,1)S(1)}, bf16[4,432,128]{2,1,0:T(8,128)(2,1)S(1)}, u32[]{:S(2)}, u32[]{:S(2)}) collective-permute-start(bf16[4,432,128]{2,1,0:T(8,128)(2,1)S(1)} %copy-done.2), channel_id=1, source_target_pairs={{0,4},{1,5},{2,6},{3,7},{4,0},{5,1},{6,2},{7,3},{8,12},{9,13},{10,... | collective-permute-start | bytes 1327112 | tf_op jit(solution)/shard_map/ppermute | solution.py:302
  45.1 0.0 collective-permute-start.4
  45.1 27.9 %collective-permute-done.2.refs_0_ = bf16[4,432,128]{2,1,0:T(8,128)(2,1)S(1)} collective-permute-done((bf16[4,432,128]{2,1,0:T(8,128)(2,1)S(1)}, bf16[4,432,128]{2,1,0:T(8,128)(2,1)S(1)}, u32[]{:S(2)}, u32[]{:S(2)}) %collective-permute-start.2) | collective-permute-done | bytes 442400 | tf_op jit(solution)/shard_map/ppermute | solution.py:302
  73.0 0.0 collective-permute-done.3.refs_1_
  73.0 0.0 collective-permute-done.4.refs_2_
  73.0 0.2 fold.1
  73.2 2.1 %collective-permute-start.5 = (bf16[432,128]{1,0:T(8,128)(2,1)S(1)}, bf16[432,128]{1,0:T(8,128)(2,1)S(1)}, u32[]{:S(2)}, u32[]{:S(2)}) collective-permute-start(bf16[432,128]{1,0:T(8,128)(2,1)S(1)} %get-tuple-element.28), channel_id=1, source_target_pairs={{0,8},{4,12},{8,16},{12,20},{16,24},{20,28},{24,0},{28,4},{1,9},{5... | collective-permute-start | bytes 331784 | tf_op jit(solution)/shard_map/ppermute | solution.py:316
  75.3 2.6 %collective-permute-start.6 = (bf16[432,128]{1,0:T(8,128)(2,1)S(1)}, bf16[432,128]{1,0:T(8,128)(2,1)S(1)}, u32[]{:S(2)}, u32[]{:S(2)}) collective-permute-start(bf16[432,128]{1,0:T(8,128)(2,1)S(1)} %get-tuple-element.29), channel_id=1, source_target_pairs={{0,16},{4,20},{8,24},{12,28},{16,0},{20,4},{24,8},{28,12},{1,17},{... | collective-permute-start | bytes 331784 | tf_op jit(solution)/shard_map/ppermute | solution.py:316
  77.9 1.3 %collective-permute-start.7 = (bf16[432,128]{1,0:T(8,128)(2,1)S(1)}, bf16[432,128]{1,0:T(8,128)(2,1)S(1)}, u32[]{:S(2)}, u32[]{:S(2)}) collective-permute-start(bf16[432,128]{1,0:T(8,128)(2,1)S(1)} %get-tuple-element.30), channel_id=1, source_target_pairs={{0,24},{4,28},{8,0},{12,4},{16,8},{20,12},{24,16},{28,20},{1,25},{... | collective-permute-start | bytes 331784 | tf_op jit(solution)/shard_map/ppermute | solution.py:316
  79.3 2.0 %collective-permute-done.5.refs_1_ = bf16[432,128]{1,0:T(8,128)(2,1)S(1)} collective-permute-done((bf16[432,128]{1,0:T(8,128)(2,1)S(1)}, bf16[432,128]{1,0:T(8,128)(2,1)S(1)}, u32[]{:S(2)}, u32[]{:S(2)}) %collective-permute-start.5) | collective-permute-done | bytes 110624 | tf_op jit(solution)/shard_map/ppermute | solution.py:316
  81.2 3.8 %collective-permute-done.6.refs_2_ = bf16[432,128]{1,0:T(8,128)(2,1)S(1)} collective-permute-done((bf16[432,128]{1,0:T(8,128)(2,1)S(1)}, bf16[432,128]{1,0:T(8,128)(2,1)S(1)}, u32[]{:S(2)}, u32[]{:S(2)}) %collective-permute-start.6) | collective-permute-done | bytes 110624 | tf_op jit(solution)/shard_map/ppermute | solution.py:316
  85.0 0.0 collective-permute-done.7.refs_3_
  85.0 0.8 finish.1
  85.8 0.0 all-to-all-done.1.refs_0_
  85.8 0.0 copy-done
  85.8 1.7 %place.1 = bf16[128,3328]{1,0:T(8,128)(2,1)} custom-call(s32[26]{0:T(128)S(1)} %copy-done, bf16[4,7,128,128]{3,2,1,0:T(8,128)(2,1)S(1)} %all-to-all-done.1.refs_0_), custom_call_target="tpu_custom_call" | custom-call | tf_op jit(solution)/shard_map/place/pallas_call | solution.py:137
Async XLA Ops:
  0.6 2.8 %collective-permute-start = (bf16[128,3456]{1,0:T(8,128)(2,1)}, bf16[128,3456]{1,0:T(8,128)(2,1)S(1)}, u32[]{:S(2)}, u32[]{:S(2)}) collective-permute-start(bf16[128,3456]{1,0:T(8,128)(2,1)} %x_hbm.1), channel_id=1, source_target_pairs={{0,1},{1,0},{2,3},{3,2},{4,5},{5,4},{6,7},{7,6},{8,9},{9,8},{10,11... | collective-permute-start | bytes 2654216 | tf_op jit(solution)/shard_map/ppermute | solution.py:288
  1.2 3.5 %collective-permute-start.1 = (bf16[128,3456]{1,0:T(8,128)(2,1)}, bf16[128,3456]{1,0:T(8,128)(2,1)S(1)}, u32[]{:S(2)}, u32[]{:S(2)}) collective-permute-start(bf16[128,3456]{1,0:T(8,128)(2,1)} %ct_hbm.1), channel_id=1, source_target_pairs={{0,1},{1,0},{2,3},{3,2},{4,5},{5,4},{6,7},{7,6},{8,9},{9,8},{10,11... | collective-permute-start | bytes 2654216 | tf_op jit(solution)/shard_map/ppermute | solution.py:289
  4.7 12.4 %all-to-all-start = ((s32[4,56,128]{2,1,0:T(8,128)}), s32[4,56,128]{2,1,0:T(8,128)S(1)}, u32[]{:S(2)}, u32[]{:S(2)}) async-start(s32[4,56,128]{2,1,0:T(8,128)} %bitcast.3), calls=%async_computation | async-start | bytes 229376 | tf_op jit(solution)/shard_map/all_to_all | solution.py:345
  15.6 0.8 copy-start.1
  16.4 0.8 copy-start.3
  37.3 3.7 %copy-start.4 = (bf16[4,432,128]{2,1,0:T(8,128)(2,1)S(1)}, bf16[4,432,128]{2,1,0:T(8,128)(2,1)}, u32[]{:S(2)}) copy-start(bf16[4,432,128]{2,1,0:T(8,128)(2,1)} %copy-done.3) | copy-start | bytes 1327108
  37.3 5.8 %copy-start.2 = (bf16[4,432,128]{2,1,0:T(8,128)(2,1)S(1)}, bf16[4,432,128]{2,1,0:T(8,128)(2,1)}, u32[]{:S(2)}) copy-start(bf16[4,432,128]{2,1,0:T(8,128)(2,1)} %copy-done.1) | copy-start | bytes 1327108
  37.3 48.5 %all-to-all-start.1 = ((bf16[4,7,128,128]{3,2,1,0:T(8,128)(2,1)}), bf16[4,7,128,128]{3,2,1,0:T(8,128)(2,1)S(1)}, u32[]{:S(2)}, u32[]{:S(2)}) async-start(bf16[4,7,128,128]{3,2,1,0:T(8,128)(2,1)} %pool_slots.1), calls=%async_computation.1 | async-start | bytes 1835008 | tf_op jit(solution)/shard_map/all_to_all | solution.py:352
  41.0 44.8 %copy-start = (s32[26]{0:T(128)S(1)}, s32[26]{0:T(128)}, u32[]{:S(2)}) copy-start(s32[26]{0:T(128)} %slot_ref.1) | copy-start | bytes 316
  41.0 32.0 %collective-permute-start.2 = (bf16[4,432,128]{2,1,0:T(8,128)(2,1)S(1)}, bf16[4,432,128]{2,1,0:T(8,128)(2,1)S(1)}, u32[]{:S(2)}, u32[]{:S(2)}) collective-permute-start(bf16[4,432,128]{2,1,0:T(8,128)(2,1)S(1)} %copy-done.4), channel_id=1, source_target_pairs={{0,2},{1,3},{2,0},{3,1},{4,6},{5,7},{6,4},{7,5},{8,10},{9,11},{10,... | collective-permute-start | bytes 1327112 | tf_op jit(solution)/shard_map/ppermute | solution.py:302
  43.1 29.8 %collective-permute-start.3 = (bf16[4,432,128]{2,1,0:T(8,128)(2,1)S(1)}, bf16[4,432,128]{2,1,0:T(8,128)(2,1)S(1)}, u32[]{:S(2)}, u32[]{:S(2)}) collective-permute-start(bf16[4,432,128]{2,1,0:T(8,128)(2,1)S(1)} %copy-done.2), channel_id=1, source_target_pairs={{0,4},{1,5},{2,6},{3,7},{4,0},{5,1},{6,2},{7,3},{8,12},{9,13},{10,... | collective-permute-start | bytes 1327112 | tf_op jit(solution)/shard_map/ppermute | solution.py:302
  45.1 27.9 %collective-permute-start.4 = (bf16[4,432,128]{2,1,0:T(8,128)(2,1)S(1)}, bf16[4,432,128]{2,1,0:T(8,128)(2,1)S(1)}, u32[]{:S(2)}, u32[]{:S(2)}) collective-permute-start(bf16[4,432,128]{2,1,0:T(8,128)(2,1)S(1)} %get-tuple-element.26), channel_id=1, source_target_pairs={{0,6},{1,7},{2,4},{3,5},{4,2},{5,3},{6,0},{7,1},{8,14},{9,15},{10,... | collective-permute-start | bytes 1327112 | tf_op jit(solution)/shard_map/ppermute | solution.py:302
  73.2 8.0 %collective-permute-start.5 = (bf16[432,128]{1,0:T(8,128)(2,1)S(1)}, bf16[432,128]{1,0:T(8,128)(2,1)S(1)}, u32[]{:S(2)}, u32[]{:S(2)}) collective-permute-start(bf16[432,128]{1,0:T(8,128)(2,1)S(1)} %get-tuple-element.28), channel_id=1, source_target_pairs={{0,8},{4,12},{8,16},{12,20},{16,24},{20,28},{24,0},{28,4},{1,9},{5... | collective-permute-start | bytes 331784 | tf_op jit(solution)/shard_map/ppermute | solution.py:316
  75.3 9.7 %collective-permute-start.6 = (bf16[432,128]{1,0:T(8,128)(2,1)S(1)}, bf16[432,128]{1,0:T(8,128)(2,1)S(1)}, u32[]{:S(2)}, u32[]{:S(2)}) collective-permute-start(bf16[432,128]{1,0:T(8,128)(2,1)S(1)} %get-tuple-element.29), channel_id=1, source_target_pairs={{0,16},{4,20},{8,24},{12,28},{16,0},{20,4},{24,8},{28,12},{1,17},{... | collective-permute-start | bytes 331784 | tf_op jit(solution)/shard_map/ppermute | solution.py:316
  77.9 7.1 %collective-permute-start.7 = (bf16[432,128]{1,0:T(8,128)(2,1)S(1)}, bf16[432,128]{1,0:T(8,128)(2,1)S(1)}, u32[]{:S(2)}, u32[]{:S(2)}) collective-permute-start(bf16[432,128]{1,0:T(8,128)(2,1)S(1)} %get-tuple-element.30), channel_id=1, source_target_pairs={{0,24},{4,28},{8,0},{12,4},{16,8},{20,12},{24,16},{28,20},{1,25},{... | collective-permute-start | bytes 331784 | tf_op jit(solution)/shard_map/ppermute | solution.py:316

commit v4 on v3

--- a/solution.py
+++ b/solution.py
@@ -26,26 +26,70 @@
     return pltpu.with_memory_space_constraint(x, pltpu.HBM)
 
 
-def mask_ids_kernel(slot_ref, ids_ref, lens_ref, out_ref, *, maxlen, rows):
-    entries, batch = out_ref.shape
+def masked_ids(slot_ref, ids_ref, lens_ref, maxlen, rows):
+    entries, batch = ids_ref.shape
     feats = lens_ref.shape[0]
     slot_of_row = lax.broadcasted_iota(jnp.int32, (entries, feats), 0) // maxlen
     hit = (slot_of_row == slot_ref[...]).astype(F32)
     lens = jnp.dot(hit, lens_ref[...].astype(F32), preferred_element_type=F32)
     place = lax.broadcasted_iota(jnp.int32, (entries, batch), 0) % maxlen
     keep = place.astype(F32) + 0.5 < lens
-    out_ref[...] = jnp.where(keep, ids_ref[...], rows)
+    return jnp.where(keep, ids_ref[...], rows)
+
+
+def mask_kernel(slot_ref, ids_ref, lens_ref, out_ref, *, maxlen, rows):
+    out_ref[...] = masked_ids(slot_ref, ids_ref, lens_ref, maxlen, rows)
 
 
 def mask_ids(slot_of_table, ids, lengths, maxlen, rows):
     return pl.pallas_call(
-        functools.partial(mask_ids_kernel, maxlen=maxlen, rows=rows),
+        functools.partial(mask_kernel, maxlen=maxlen, rows=rows),
         in_specs=[whole()] * 3,
         out_specs=whole(),
         out_shape=jax.ShapeDtypeStruct((ids.shape[1], ids.shape[0]), jnp.int32),
         compiler_params=room(4),
         name="mask_ids",
-    )(in_hbm(slot_of_table.reshape(1, -1)), in_hbm(ids.T), in_hbm(lengths.T))
+    )(slot_of_table.reshape(1, -1), ids.T, lengths.T)
+
+
+def prep_kernel(*refs, maxlen, rows):
+    sources, (masked_ref, rank_ref), targets, sem = refs[:7], refs[7:9], refs[9:16], refs[16]
+    slot_ref, ids_ref, lens_ref, x_ref, ct_ref, down_ref, up_ref = targets
+    loads = [
+        pltpu.make_async_copy(src, dst, sem.at[i]) for i, (src, dst) in enumerate(zip(sources, targets))
+    ]
+    for load in loads:
+        load.start()
+    for load in loads[:3]:
+        load.wait()
+    masked_ref[...] = masked_ids(slot_ref, ids_ref, lens_ref, maxlen, rows)
+    for load in loads[3:5]:
+        load.wait()
+    x = x_ref[...]
+    dz = (ct_ref[...].astype(F32) * x.astype(F32)).astype(BF16)
+    loads[5].wait()
+    rank_ref[0] = jnp.dot(x, down_ref[...], preferred_element_type=F32).astype(BF16)
+    loads[6].wait()
+    rank_ref[1] = lax.dot_general(
+        dz, up_ref[...], (((1,), (1,)), ((), ())), preferred_element_type=F32
+    ).astype(BF16)
+
+
+def prep(slot_of_table, ids, lengths, x, ct, down, up, maxlen, rows):
+    sources = [slot_of_table.reshape(1, -1), ids.T, lengths.T, x, ct, down, up]
+    return pl.pallas_call(
+        functools.partial(prep_kernel, maxlen=maxlen, rows=rows),
+        in_specs=[whole(pl.ANY)] * 7,
+        out_specs=[whole()] * 2,
+        out_shape=[
+            jax.ShapeDtypeStruct(ids.shape[::-1], jnp.int32),
+            jax.ShapeDtypeStruct((2, x.shape[0], down.shape[1]), BF16),
+        ],
+        scratch_shapes=[pltpu.VMEM(a.shape, a.dtype) for a in sources]
+        + [pltpu.SemaphoreType.DMA((7,))],
+        compiler_params=room(16),
+        name="prep",
+    )(*[in_hbm(a) for a in sources])
 
 
 def pool_kernel(ids_ref, table_ref, out_ref, wide_ref, sum_ref, *rest, first, chunk):
@@ -145,39 +189,30 @@
     )(slot_of_table, *parts)
 
 
-def grads_kernel(pos_ref, xs_ref, cts_ref, x_hbm, ct_hbm, down_hbm, up_hbm, *refs, owners, groups):
+def grads_kernel(pos_ref, own_ref, sib_ref, *refs, owners, groups, chunks):
     tall, far = owners // 2, groups // 2
-    outs = refs[: 2 * tall]
-    both_ref, sum_ref, x_ref, ct_ref, down_ref, up_ref, sem = refs[2 * tall :]
-    core, y, x, z = pos_ref[0] & 1, pos_ref[0] >> 1, pos_ref[1] & 1, pos_ref[1] >> 1
-    batch, wide = x_ref.shape
-    rank = down_ref.shape[1]
-    part = rank // owners
+    sources, keep_ref, sends = refs[:4], refs[4], refs[5 : 4 + 2 * tall]
+    both_ref, sum_ref, near_ref, in_sem, sem = refs[4 + 2 * tall : 9 + 2 * tall]
+    targets = refs[9 + 2 * tall :]
+    g, t = lax.div(pos_ref[0], owners), lax.rem(pos_ref[0], owners)
+    core, y, x, z = t & 1, t >> 1, g & 1, g >> 1
+    batch, wide = sources[0].shape
+    part = own_ref.shape[2] // owners
     pair = 2 * batch
-    loads = [
-        pltpu.make_async_copy(src, dst, sem.at[i])
-        for i, (src, dst) in enumerate(
-            ((x_hbm, x_ref), (ct_hbm, ct_ref), (down_hbm, down_ref), (up_hbm, up_ref))
+    span = wide // chunks
+    loads = []
+    for c in range(chunks):
+        at = pl.ds(c * span, span)
+        loads.append(
+            [
+                pltpu.make_async_copy(src.at[:, at], dst.at[:, at], in_sem.at[4 * c + i])
+                for i, (src, dst) in enumerate(zip(sources, targets))
+            ]
         )
-    ]
-    for load in loads:
-        load.start()
-    for at, (a_ref, b_ref) in enumerate(((xs_ref, cts_ref), (x_ref, ct_ref))):
-        if at:
-            loads[0].wait()
-            loads[1].wait()
-        a = a_ref[...]
-        both_ref[pl.ds(at * batch, batch), :] = (b_ref[...].astype(F32) * a.astype(F32)).astype(BF16)
-        both_ref[pl.ds(pair + at * batch, batch), :] = a
-    loads[2].wait()
-    low = jnp.dot(both_ref[pl.ds(pair, pair), :], down_ref[...], preferred_element_type=F32)
-    loads[3].wait()
-    dlow = lax.dot_general(
-        both_ref[pl.ds(0, pair), :],
-        up_ref[...],
-        (((1,), (1,)), ((), ())),
-        preferred_element_type=F32,
-    )
+        for load in loads[-1]:
+            load.start()
+    low = jnp.concatenate([own_ref[0], sib_ref[0]], axis=0).astype(F32)
+    dlow = jnp.concatenate([own_ref[1], sib_ref[1]], axis=0).astype(F32)
     none = jnp.zeros((pair, part), F32)
     columns = []
     for ry in range(tall):
@@ -192,43 +227,65 @@
             )
         )
     right = jnp.concatenate(columns, axis=1).astype(BF16)
-    step = math.gcd(wide, 384)
-    for d in range(0, wide, step):
-        sum_ref[pl.ds(d, step), :] = lax.dot_general(
-            both_ref[:, d : d + step], right, (((0,), (0,)), ((), ())), preferred_element_type=F32
-        )
+    step = math.gcd(span, 384)
+    for c in range(chunks):
+        for load in loads[c]:
+            load.wait()
+        for d in range(c * span, (c + 1) * span, step):
+            cols = slice(d, d + step)
+            for i in range(2):
+                a = targets[2 * i][:, cols]
+                dz = targets[2 * i + 1][:, cols].astype(F32) * a.astype(F32)
+                both_ref[pl.ds(i * batch, batch), :] = dz.astype(BF16)
+                both_ref[pl.ds(pair + i * batch, batch), :] = a
+            sum_ref[pl.ds(d, step), :] = lax.dot_general(
+                both_ref[...], right, (((0,), (0,)), ((), ())), preferred_element_type=F32
+            )
     each = wide // groups
     block = 2 * part
-    for r in range(far):
-        for rx in range(2):
+    copies = []
+    for i in range(2 * tall - 1, -1, -1):
+        rx, ry = i // tall, i % tall
+        cols = slice(ry * block, (ry + 1) * block)
+        for r in range(far):
             g = 2 * lax.rem(z + r, far) + (x + rx - 2 * x * rx)
-            start = pl.multiple_of(g * each, 16)
-            for ry in range(tall):
-                out = outs[rx * tall + ry]
-                cols = slice(ry * block, (ry + 1) * block)
-                out[r] = sum_ref[pl.ds(start, each), cols].astype(out.dtype)
-
-
-def part_grads(pos, x, ct, xs, cts, down, up, owners, groups):
-    wide, rank = down.shape
-    batch = x.shape[0]
+            found = sum_ref[pl.ds(pl.multiple_of(g * each, 16), each), cols]
+            if i:
+                near_ref[i - 1, r] = found.astype(BF16)
+            else:
+                keep_ref[r] = found
+        if i:
+            copies.append(pltpu.make_async_copy(near_ref.at[i - 1], sends[i - 1], sem.at[i - 1]))
+            copies[-1].start()
+    for copy in copies:
+        copy.wait()
+
+
+def part_grads(pos, own, sib, x, ct, xs, cts, owners, groups):
+    batch, wide = x.shape
+    rank = own.shape[2]
     tall, far = owners // 2, groups // 2
     block = 2 * (rank // owners)
     shape = (far, wide // groups, block)
-    return pl.pallas_call(
-        functools.partial(grads_kernel, owners=owners, groups=groups),
+    others = 2 * tall - 1
+    chunks = 3 if wide % (3 * LANES) == 0 else 1
+    step = math.gcd(wide // chunks, 384)
+    return pl.pallas_call(
+        functools.partial(grads_kernel, owners=owners, groups=groups, chunks=chunks),
         in_specs=[whole(pltpu.SMEM)] + [whole()] * 2 + [whole(pl.ANY)] * 4,
-        out_specs=[whole()] * (2 * tall),
-        out_shape=[pltpu.VMEM(shape, BF16 if i else F32) for i in range(2 * tall)],
+        out_specs=[whole()] + [whole(pl.ANY)] * others,
+        out_shape=[jax.ShapeDtypeStruct(shape, F32)] + [jax.ShapeDtypeStruct(shape, BF16)] * others,
         scratch_shapes=[
-            pltpu.VMEM((4 * batch, wide), BF16),
+            pltpu.VMEM((4 * batch, step), BF16),
             pltpu.VMEM((wide, tall * block), F32),
+            pltpu.VMEM((others, *shape), BF16),
+            pltpu.SemaphoreType.DMA((4 * chunks,)),
+            pltpu.SemaphoreType.DMA((others,)),
         ]
-        + [pltpu.VMEM(a.shape, BF16) for a in (x, ct, down, up)]
-        + [pltpu.SemaphoreType.DMA((4,))],
-        compiler_params=room(24),
+        + [pltpu.VMEM((batch, wide), BF16)] * 4,
+        compiler_params=room(20),
         name="part_grads",
-    )(pos, xs, cts, in_hbm(x), in_hbm(ct), in_hbm(down), in_hbm(up))
+    )(pos, own, sib, in_hbm(x), in_hbm(ct), xs, cts)
 
 
 def fold_kernel(keep, *refs, far):
@@ -279,16 +336,15 @@
     return up, down.T
 
 
-def exchange_start(x, ct, up, down, after):
+def exchange_start(x, ct, own):
     owners, groups = lax.axis_size("tbl"), lax.axis_size("grp")
     tall = owners // 2
-    t, g = lax.axis_index("tbl"), lax.axis_index("grp")
-    pos = jnp.stack([t, g]).astype(jnp.int32)
+    pos = lax.axis_index(("grp", "tbl")).astype(jnp.int32).reshape(1)
     other_core = [(i, i ^ 1) for i in range(owners)]
     xs = lax.ppermute(x, "tbl", other_core)
     cts = lax.ppermute(ct, "tbl", other_core)
-    xs, cts, after = lax.optimization_barrier((xs, cts, after))
-    parts = part_grads(pos, x, ct, xs, cts, down, up, owners, groups)
+    sib = lax.ppermute(own, "tbl", other_core)
+    parts = part_grads(pos, own, sib, x, ct, xs, cts, owners, groups)
 
     def to(rx, ry):
         return [
@@ -300,7 +356,7 @@
     came = []
     for i in range(1, 2 * tall):
         came.append(lax.ppermute(parts[i], ("grp", "tbl"), to(i // tall, i % tall)))
-    return parts[0], came, after
+    return parts[0], came
 
 
 def exchange_end(keep, came, factor):
@@ -339,9 +395,11 @@
     factor = 1.0 / math.sqrt(batch * owners * groups)
     tiled = by_exchange(owners, groups, *down.shape)
 
-    masked = mask_ids(slot_of_table, ids, lengths, maxlen, rows)
     if tiled:
-        keep, came, masked = exchange_start(x, ct, up, down, masked)
+        masked, own = prep(slot_of_table, ids, lengths, x, ct, down, up, maxlen, rows)
+        keep, came = exchange_start(x, ct, own)
+    else:
+        masked = mask_ids(slot_of_table, ids, lengths, maxlen, rows)
     got = lax.all_to_all(masked.reshape(owners, slots * maxlen, batch), "tbl", 0, 0)
     if tiled:
         got, keep = lax.optimization_barrier((got, keep))

time: 87.8 us -> 85.7 us (0.976)
  waiting for transfers between devices: 35.4 us -> 34 us
    pallas_call x1, Pallas kernels: 6.66 us -> 4.13 us  [part_grads(): pl.pallas_call(functools.partial(grads_kernel, owners=owners, groups=grou...]
    pallas_call x1, Pallas kernels: 1.68 us -> 3.68 us  [prep(): pl.pallas_call(functools.partial(prep_kernel, maxlen=maxlen, rows=rows),...]
    ppermute x1, waiting for transfers between devices: 1.26 us -> 0.01 us  [exchange_start(): cts = lax.ppermute(ct, 'tbl', other_core)]
  transfers between devices with their start and end apart: 10 -> 11, of which waited for: 5 -> 3; matrix products, arithmetic and copies ran while one was open for 0% -> 0% of each run, Pallas kernels for 11% -> 10%
where the time goes in v4:
time: 85.7 us; the launch traced here: 85.4 us
  waiting for transfers between devices  34 us (40%)
  Pallas kernels  30.7 us (36%)
  starting transfers between devices  18.5 us (22%)
  local copies, waits for them, and re-layouts  1.55 us (2%)
    ppermute x3, waiting for transfers between devices, exchange_start(): came.append(lax.ppermute(parts[i], ('grp', 'tbl'), to(i // tall, i % tall)))  28.2 us
    pallas_call x1, Pallas kernels, pool_slots(): pl.pallas_call(functools.partial(pool_kernel, first=first, chunk=math.gcd...  20.2 us
    ppermute x3, starting transfers between devices, exchange_end(): last.append(lax.ppermute(out[r], 'grp', to_z(r)))  5.77 us
    ppermute x3, waiting for transfers between devices, exchange_end(): last.append(lax.ppermute(out[r], 'grp', to_z(r)))  5.75 us
    pallas_call x1, Pallas kernels, part_grads(): pl.pallas_call(functools.partial(grads_kernel, owners=owners, groups=grou...  4.13 us
    ppermute x3, starting transfers between devices, exchange_start(): came.append(lax.ppermute(parts[i], ('grp', 'tbl'), to(i // tall, i % tall)))  4.05 us
    all_to_all x1, starting transfers between devices, on_device(): lax.all_to_all(masked.reshape(owners, slots * maxlen, batch), 'tbl', 0, 0)  3.89 us
    pallas_call x1, Pallas kernels, prep(): pl.pallas_call(functools.partial(prep_kernel, maxlen=maxlen, rows=rows),...  3.68 us
  transfers between devices with their start and end apart: 11, of which 3 were waited for; matrix products, arithmetic and copies ran while one was open for 0% of the time, Pallas kernels for 10%

profile of v4, /device:TPU:0, one launch (start us, length us, event | category | flops | bytes accessed | tf_op | source)
XLA Modules:
  0.0 85.4 jit_solution(15187916639534079692)
XLA Ops:
  0.6 0.6 collective-permute-start.1
  1.2 0.1 collective-permute-start.2
  1.3 3.7 %prep.1 = (s32[224,128]{1,0:T(8,128)}, bf16[2,128,256]{2,1,0:T(8,128)(2,1)S(1)}) custom-call(s32[1,26]{1,0:T(1,128)} %bitcast.6, s32[224,128]{1,0:T(8,128)} %bitcast.7, s32[26,128]{1,0:T(8,128)} %bitcast.8, bf16[128,3456]{1,0:T(8,128)(2,1)} %refs_0_.1, bf16[128,3456]{1,0:T(8,128)(2,1)} %refs_1_.1, bf16[3456,256]{1,0:T(8,128)(2,1)} %refs_5_.1, ...), custom_call_target="tpu_custom_call" | custom-call | tf_op jit(solution)/shard_map/prep/pallas_call | solution.py:80
  5.0 0.5 collective-permute-start
  5.5 3.9 %all-to-all-start = ((s32[4,56,128]{2,1,0:T(8,128)}), s32[4,56,128]{2,1,0:T(8,128)S(1)}, u32[]{:S(2)}, u32[]{:S(2)}) async-start(s32[4,56,128]{2,1,0:T(8,128)} %bitcast.3), calls=%async_computation | async-start | bytes 229376 | tf_op jit(solution)/shard_map/all_to_all | solution.py:403
  9.3 0.0 collective-permute-done.sib_ref
  9.3 0.0 collective-permute-done.1.refs_2_
  9.4 0.0 collective-permute-done.2.refs_3_
  9.4 4.1 %part_grads.1 = (f32[4,432,128]{2,1,0:T(8,128)S(1)}, bf16[4,432,128]{2,1,0:T(8,128)(2,1)S(1)}, bf16[4,432,128]{2,1,0:T(8,128)(2,1)S(1)}, bf16[4,432,128]{2,1,0:T(8,128)(2,1)S(1)}) custom-call(s32[1]{0:T(128)} %bitcast.4.pos_ref, bf16[2,128,256]{2,1,0:T(8,128)(2,1)S(1)} %get-tuple-element.18.own_ref, bf16[2,128,256]{2,1,0:T(8,128)(2,1)S(1)} %collective-permute-done.sib_ref, ...), custom_call_target="tpu_custom_call" | custom-call | tf_op jit(solution)/shard_map/part_grads/pallas_call | solution.py:273
  13.5 0.0 copy-start.1
  13.5 0.8 copy-done.1
  14.3 0.0 copy-start.3
  14.3 0.8 copy-done.3
  15.0 0.0 all-to-all-done.ids_ref
  15.0 20.2 %pool_slots.1 = bf16[4,7,128,128]{3,2,1,0:T(8,128)(2,1)} custom-call(s32[4,56,128]{2,1,0:T(8,128)S(1)} %all-to-all-done.ids_ref, bf16[7,6144,128]{2,1,0:T(8,128)(2,1)} %table_ref.1), custom_call_target="tpu_custom_call" | custom-call | tf_op jit(solution)/shard_map/pool_slots/pallas_call | solution.py:135
  35.2 0.0 copy-start.4
  35.2 0.0 copy-start.2
  35.2 3.6 %all-to-all-start.1 = ((bf16[4,7,128,128]{3,2,1,0:T(8,128)(2,1)}), bf16[4,7,128,128]{3,2,1,0:T(8,128)(2,1)S(1)}, u32[]{:S(2)}, u32[]{:S(2)}) async-start(bf16[4,7,128,128]{3,2,1,0:T(8,128)(2,1)} %pool_slots.1), calls=%async_computation.1 | async-start | bytes 1835008 | tf_op jit(solution)/shard_map/all_to_all | solution.py:410
  38.9 0.0 copy-start
  38.9 0.0 copy-done.4
  38.9 2.1 %collective-permute-start.3 = (bf16[4,432,128]{2,1,0:T(8,128)(2,1)S(1)}, bf16[4,432,128]{2,1,0:T(8,128)(2,1)S(1)}, u32[]{:S(2)}, u32[]{:S(2)}) collective-permute-start(bf16[4,432,128]{2,1,0:T(8,128)(2,1)S(1)} %copy-done.4), channel_id=1, source_target_pairs={{0,2},{1,3},{2,0},{3,1},{4,6},{5,7},{6,4},{7,5},{8,10},{9,11},{10,... | collective-permute-start | bytes 1327112 | tf_op jit(solution)/shard_map/ppermute | solution.py:358
  41.0 0.0 copy-done.2
  41.0 1.9 %collective-permute-start.4 = (bf16[4,432,128]{2,1,0:T(8,128)(2,1)S(1)}, bf16[4,432,128]{2,1,0:T(8,128)(2,1)S(1)}, u32[]{:S(2)}, u32[]{:S(2)}) collective-permute-start(bf16[4,432,128]{2,1,0:T(8,128)(2,1)S(1)} %copy-done.2), channel_id=1, source_target_pairs={{0,4},{1,5},{2,6},{3,7},{4,0},{5,1},{6,2},{7,3},{8,12},{9,13},{10,... | collective-permute-start | bytes 1327112 | tf_op jit(solution)/shard_map/ppermute | solution.py:358
  43.0 0.0 collective-permute-start.5
  43.0 28.2 %collective-permute-done.3.refs_0_ = bf16[4,432,128]{2,1,0:T(8,128)(2,1)S(1)} collective-permute-done((bf16[4,432,128]{2,1,0:T(8,128)(2,1)S(1)}, bf16[4,432,128]{2,1,0:T(8,128)(2,1)S(1)}, u32[]{:S(2)}, u32[]{:S(2)}) %collective-permute-start.3) | collective-permute-done | bytes 442400 | tf_op jit(solution)/shard_map/ppermute | solution.py:358
  71.2 0.0 collective-permute-done.4.refs_1_
  71.2 0.0 collective-permute-done.5.refs_2_
  71.2 0.2 fold.1
  71.4 1.8 %collective-permute-start.6 = (bf16[432,128]{1,0:T(8,128)(2,1)S(1)}, bf16[432,128]{1,0:T(8,128)(2,1)S(1)}, u32[]{:S(2)}, u32[]{:S(2)}) collective-permute-start(bf16[432,128]{1,0:T(8,128)(2,1)S(1)} %get-tuple-element.26), channel_id=1, source_target_pairs={{0,8},{4,12},{8,16},{12,20},{16,24},{20,28},{24,0},{28,4},{1,9},{5... | collective-permute-start | bytes 331784 | tf_op jit(solution)/shard_map/ppermute | solution.py:372
  73.2 2.6 %collective-permute-start.7 = (bf16[432,128]{1,0:T(8,128)(2,1)S(1)}, bf16[432,128]{1,0:T(8,128)(2,1)S(1)}, u32[]{:S(2)}, u32[]{:S(2)}) collective-permute-start(bf16[432,128]{1,0:T(8,128)(2,1)S(1)} %get-tuple-element.27), channel_id=1, source_target_pairs={{0,16},{4,20},{8,24},{12,28},{16,0},{20,4},{24,8},{28,12},{1,17},{... | collective-permute-start | bytes 331784 | tf_op jit(solution)/shard_map/ppermute | solution.py:372
  75.8 1.3 %collective-permute-start.8 = (bf16[432,128]{1,0:T(8,128)(2,1)S(1)}, bf16[432,128]{1,0:T(8,128)(2,1)S(1)}, u32[]{:S(2)}, u32[]{:S(2)}) collective-permute-start(bf16[432,128]{1,0:T(8,128)(2,1)S(1)} %get-tuple-element.28), channel_id=1, source_target_pairs={{0,24},{4,28},{8,0},{12,4},{16,8},{20,12},{24,16},{28,20},{1,25},{... | collective-permute-start | bytes 331784 | tf_op jit(solution)/shard_map/ppermute | solution.py:372
  77.1 2.0 %collective-permute-done.6.refs_1_ = bf16[432,128]{1,0:T(8,128)(2,1)S(1)} collective-permute-done((bf16[432,128]{1,0:T(8,128)(2,1)S(1)}, bf16[432,128]{1,0:T(8,128)(2,1)S(1)}, u32[]{:S(2)}, u32[]{:S(2)}) %collective-permute-start.6) | collective-permute-done | bytes 110624 | tf_op jit(solution)/shard_map/ppermute | solution.py:372
  79.1 3.8 %collective-permute-done.7.refs_2_ = bf16[432,128]{1,0:T(8,128)(2,1)S(1)} collective-permute-done((bf16[432,128]{1,0:T(8,128)(2,1)S(1)}, bf16[432,128]{1,0:T(8,128)(2,1)S(1)}, u32[]{:S(2)}, u32[]{:S(2)}) %collective-permute-start.7) | collective-permute-done | bytes 110624 | tf_op jit(solution)/shard_map/ppermute | solution.py:372
  82.9 0.0 collective-permute-done.8.refs_3_
  82.9 0.8 finish.1
  83.7 0.0 all-to-all-done.1.refs_0_
  83.7 0.0 copy-done
  83.7 1.7 %place.1 = bf16[128,3328]{1,0:T(8,128)(2,1)} custom-call(s32[26]{0:T(128)S(1)} %copy-done, bf16[4,7,128,128]{3,2,1,0:T(8,128)(2,1)S(1)} %all-to-all-done.1.refs_0_), custom_call_target="tpu_custom_call" | custom-call | tf_op jit(solution)/shard_map/place/pallas_call | solution.py:181
Async XLA Ops:
  0.6 8.7 %collective-permute-start.1 = (bf16[128,3456]{1,0:T(8,128)(2,1)}, bf16[128,3456]{1,0:T(8,128)(2,1)S(1)}, u32[]{:S(2)}, u32[]{:S(2)}) collective-permute-start(bf16[128,3456]{1,0:T(8,128)(2,1)} %refs_0_.1), channel_id=1, source_target_pairs={{0,1},{1,0},{2,3},{3,2},{4,5},{5,4},{6,7},{7,6},{8,9},{9,8},{10,11... | collective-permute-start | bytes 2654216 | tf_op jit(solution)/shard_map/ppermute | solution.py:344
  1.2 8.2 %collective-permute-start.2 = (bf16[128,3456]{1,0:T(8,128)(2,1)}, bf16[128,3456]{1,0:T(8,128)(2,1)S(1)}, u32[]{:S(2)}, u32[]{:S(2)}) collective-permute-start(bf16[128,3456]{1,0:T(8,128)(2,1)} %refs_1_.1), channel_id=1, source_target_pairs={{0,1},{1,0},{2,3},{3,2},{4,5},{5,4},{6,7},{7,6},{8,9},{9,8},{10,11... | collective-permute-start | bytes 2654216 | tf_op jit(solution)/shard_map/ppermute | solution.py:345
  5.0 4.4 %collective-permute-start = (bf16[2,128,256]{2,1,0:T(8,128)(2,1)S(1)}, bf16[2,128,256]{2,1,0:T(8,128)(2,1)S(1)}, u32[]{:S(2)}, u32[]{:S(2)}) collective-permute-start(bf16[2,128,256]{2,1,0:T(8,128)(2,1)S(1)} %get-tuple-element.18.own_ref), channel_id=1, source_target_pairs={{0,1},{1,0},{2,3},{3,2},{4,5},{5,4},{6,7},{7,6},{8,9},{9,8},{10,11... | collective-permute-start | bytes 393224 | tf_op jit(solution)/shard_map/ppermute | solution.py:346
  5.5 9.6 %all-to-all-start = ((s32[4,56,128]{2,1,0:T(8,128)}), s32[4,56,128]{2,1,0:T(8,128)S(1)}, u32[]{:S(2)}, u32[]{:S(2)}) async-start(s32[4,56,128]{2,1,0:T(8,128)} %bitcast.3), calls=%async_computation | async-start | bytes 229376 | tf_op jit(solution)/shard_map/all_to_all | solution.py:403
  13.5 0.8 copy-start.1
  14.3 0.8 copy-start.3
  35.2 3.7 %copy-start.4 = (bf16[4,432,128]{2,1,0:T(8,128)(2,1)S(1)}, bf16[4,432,128]{2,1,0:T(8,128)(2,1)}, u32[]{:S(2)}) copy-start(bf16[4,432,128]{2,1,0:T(8,128)(2,1)} %copy-done.3) | copy-start | bytes 1327108
  35.2 5.8 %copy-start.2 = (bf16[4,432,128]{2,1,0:T(8,128)(2,1)S(1)}, bf16[4,432,128]{2,1,0:T(8,128)(2,1)}, u32[]{:S(2)}) copy-start(bf16[4,432,128]{2,1,0:T(8,128)(2,1)} %copy-done.1) | copy-start | bytes 1327108
  35.2 48.5 %all-to-all-start.1 = ((bf16[4,7,128,128]{3,2,1,0:T(8,128)(2,1)}), bf16[4,7,128,128]{3,2,1,0:T(8,128)(2,1)S(1)}, u32[]{:S(2)}, u32[]{:S(2)}) async-start(bf16[4,7,128,128]{3,2,1,0:T(8,128)(2,1)} %pool_slots.1), calls=%async_computation.1 | async-start | bytes 1835008 | tf_op jit(solution)/shard_map/all_to_all | solution.py:410
  38.9 44.8 %copy-start = (s32[26]{0:T(128)S(1)}, s32[26]{0:T(128)}, u32[]{:S(2)}) copy-start(s32[26]{0:T(128)} %slot_ref.1) | copy-start | bytes 316
  38.9 32.2 %collective-permute-start.3 = (bf16[4,432,128]{2,1,0:T(8,128)(2,1)S(1)}, bf16[4,432,128]{2,1,0:T(8,128)(2,1)S(1)}, u32[]{:S(2)}, u32[]{:S(2)}) collective-permute-start(bf16[4,432,128]{2,1,0:T(8,128)(2,1)S(1)} %copy-done.4), channel_id=1, source_target_pairs={{0,2},{1,3},{2,0},{3,1},{4,6},{5,7},{6,4},{7,5},{8,10},{9,11},{10,... | collective-permute-start | bytes 1327112 | tf_op jit(solution)/shard_map/ppermute | solution.py:358
  41.0 30.1 %collective-permute-start.4 = (bf16[4,432,128]{2,1,0:T(8,128)(2,1)S(1)}, bf16[4,432,128]{2,1,0:T(8,128)(2,1)S(1)}, u32[]{:S(2)}, u32[]{:S(2)}) collective-permute-start(bf16[4,432,128]{2,1,0:T(8,128)(2,1)S(1)} %copy-done.2), channel_id=1, source_target_pairs={{0,4},{1,5},{2,6},{3,7},{4,0},{5,1},{6,2},{7,3},{8,12},{9,13},{10,... | collective-permute-start | bytes 1327112 | tf_op jit(solution)/shard_map/ppermute | solution.py:358
  43.0 28.2 %collective-permute-start.5 = (bf16[4,432,128]{2,1,0:T(8,128)(2,1)S(1)}, bf16[4,432,128]{2,1,0:T(8,128)(2,1)S(1)}, u32[]{:S(2)}, u32[]{:S(2)}) collective-permute-start(bf16[4,432,128]{2,1,0:T(8,128)(2,1)S(1)} %get-tuple-element.24), channel_id=1, source_target_pairs={{0,6},{1,7},{2,4},{3,5},{4,2},{5,3},{6,0},{7,1},{8,14},{9,15},{10,... | collective-permute-start | bytes 1327112 | tf_op jit(solution)/shard_map/ppermute | solution.py:358
  71.4 7.8 %collective-permute-start.6 = (bf16[432,128]{1,0:T(8,128)(2,1)S(1)}, bf16[432,128]{1,0:T(8,128)(2,1)S(1)}, u32[]{:S(2)}, u32[]{:S(2)}) collective-permute-start(bf16[432,128]{1,0:T(8,128)(2,1)S(1)} %get-tuple-element.26), channel_id=1, source_target_pairs={{0,8},{4,12},{8,16},{12,20},{16,24},{20,28},{24,0},{28,4},{1,9},{5... | collective-permute-start | bytes 331784 | tf_op jit(solution)/shard_map/ppermute | solution.py:372
  73.2 9.7 %collective-permute-start.7 = (bf16[432,128]{1,0:T(8,128)(2,1)S(1)}, bf16[432,128]{1,0:T(8,128)(2,1)S(1)}, u32[]{:S(2)}, u32[]{:S(2)}) collective-permute-start(bf16[432,128]{1,0:T(8,128)(2,1)S(1)} %get-tuple-element.27), channel_id=1, source_target_pairs={{0,16},{4,20},{8,24},{12,28},{16,0},{20,4},{24,8},{28,12},{1,17},{... | collective-permute-start | bytes 331784 | tf_op jit(solution)/shard_map/ppermute | solution.py:372
  75.8 7.1 %collective-permute-start.8 = (bf16[432,128]{1,0:T(8,128)(2,1)S(1)}, bf16[432,128]{1,0:T(8,128)(2,1)S(1)}, u32[]{:S(2)}, u32[]{:S(2)}) collective-permute-start(bf16[432,128]{1,0:T(8,128)(2,1)S(1)} %get-tuple-element.28), channel_id=1, source_target_pairs={{0,24},{4,28},{8,0},{12,4},{16,8},{20,12},{24,16},{28,20},{1,25},{... | collective-permute-start | bytes 331784 | tf_op jit(solution)/shard_map/ppermute | solution.py:372

commit v5 on v4

--- a/solution.py
+++ b/solution.py
@@ -92,101 +92,141 @@
     )(*[in_hbm(a) for a in sources])
 
 
-def pool_kernel(ids_ref, table_ref, out_ref, wide_ref, sum_ref, *rest, first, chunk):
-    rows, width = table_ref.shape[1:]
-    groups, _, batch, _ = out_ref.shape
-    near, sem = rest[:groups], rest[groups]
-    maxlen = near[0].shape[0]
-    step, steps = pl.program_id(0), pl.num_programs(0)
-
-    def fetch(g, at):
-        start = pl.multiple_of((first + at) * maxlen, maxlen)
-        return pltpu.make_async_copy(ids_ref.at[g, pl.ds(start, maxlen)], near[g], sem.at[g])
-
-    @pl.when(step == 0)
-    def _():
+def pool_kernel(ids_hbm, tables_hbm, out_hbm, *refs, maxlen):
+    groups, count, batch, width = out_hbm.shape
+    near, refs = refs[:groups], refs[groups:]
+    stage, wide, pooled, sum_ref = refs[0:2], refs[2:4], refs[4:6], refs[6]
+    ids_sem, first_sem, table_sem, out_sem = refs[7:]
+    rows = stage[0].shape[0]
+    firsts = first_sem.shape[0]
+    head = rows // firsts
+    piece = math.gcd(rows, 48)
+    pieces = rows // piece
+
+    def fetch_ids(g, slot):
+        start = pl.multiple_of(slot * maxlen, maxlen)
+        return pltpu.make_async_copy(ids_hbm.at[g, pl.ds(start, maxlen)], near[g], ids_sem.at[g])
+
+    def fetch_table(slot, at):
+        return pltpu.make_async_copy(tables_hbm.at[slot], stage[at], table_sem.at[at])
+
+    def fetch_first(i):
+        part = pl.ds(i * head, head)
+        return pltpu.make_async_copy(tables_hbm.at[0, part], stage[0].at[part], first_sem.at[i])
+
+    def put(slot, at):
+        return pltpu.make_async_copy(pooled[at], out_hbm.at[:, slot], out_sem.at[at])
+
+    def widen(at, start, size):
+        part = pl.ds(start, size)
+        wide[at][part, :] = stage[at][part, :].astype(F32)
+
+    def half(slot, at):
+        other = 1 - at
+
+        @pl.when(slot + 1 < count)
+        def _():
+            fetch_table(slot + 1, other).wait()
+
+        @pl.when(slot + 2 < count)
+        def _():
+            fetch_table(slot + 2, at).start()
+
+        @pl.when(slot >= 2)
+        def _():
+            put(slot - 2, at).wait()
+
         for g in range(groups):
-            fetch(g, 0).start()
-
-    def widen(i, carry):
-        start = pl.multiple_of(i * chunk, chunk)
-        wide_ref[pl.ds(start, chunk), :] = table_ref[0, pl.ds(start, chunk), :].astype(F32)
+            fetch_ids(g, slot).wait()
+            for b in range(batch):
+                bag = g * batch + b
+                for p in range(bag * pieces // (groups * batch), (bag + 1) * pieces // (groups * batch)):
+                    widen(other, p * piece, piece)
+                total = wide[at][pl.ds(near[g][0, b], 1), :]
+                for k in range(1, maxlen):
+                    total = total + wide[at][pl.ds(near[g][k, b], 1), :]
+                sum_ref[pl.ds(b, 1), :] = total
+            pooled[at][g] = sum_ref[...].astype(BF16)
+
+            @pl.when(slot + 1 < count)
+            def _(g=g):
+                fetch_ids(g, slot + 1).start()
+
+        put(slot, at).start()
+
+    for g in range(groups):
+        fetch_ids(g, 0).start()
+    for i in range(firsts):
+        fetch_first(i).start()
+    if count > 1:
+        fetch_table(1, 1).start()
+    for at in range(2):
+        wide[at][pl.ds(rows, 8), :] = jnp.zeros((8, width), F32)
+    for i in range(firsts):
+        fetch_first(i).wait()
+        widen(0, i * head, head)
+
+    def pair(i, carry):
+        half(2 * i, 0)
+
+        @pl.when(2 * i + 1 < count)
+        def _():
+            half(2 * i + 1, 1)
+
         return carry
 
-    lax.fori_loop(0, rows // chunk, widen, 0)
-    wide_ref[pl.ds(rows, 8), :] = jnp.zeros((8, width), F32)
-    for g in range(groups):
-        fetch(g, step).wait()
-        for b in range(batch):
-            total = wide_ref[pl.ds(near[g][0, b], 1), :]
-            for k in range(1, maxlen):
-                total = total + wide_ref[pl.ds(near[g][k, b], 1), :]
-            sum_ref[pl.ds(b, 1), :] = total
-        out_ref[g, 0] = sum_ref[...].astype(BF16)
-
-        @pl.when(step + 1 < steps)
-        def _(g=g):
-            fetch(g, step + 1).start()
-
-
-def pool_slots(ids, tables, first, count, maxlen):
+    lax.fori_loop(0, (count + 1) // 2, pair, 0)
+    for slot in range(max(count - 2, 0), count):
+        put(slot, slot % 2).wait()
+
+
+def pool_slots(ids, tables, maxlen):
     groups, _, batch = ids.shape
-    rows, width = tables.shape[1:]
-    return pl.pallas_call(
-        functools.partial(pool_kernel, first=first, chunk=math.gcd(rows, 512)),
-        grid=(count,),
-        in_specs=[
-            pl.BlockSpec(memory_space=pl.ANY),
-            pl.BlockSpec((1, rows, width), lambda s: (s + first, 0, 0)),
-        ],
-        out_specs=pl.BlockSpec((groups, 1, batch, width), lambda s: (0, s, 0, 0)),
-        out_shape=jax.ShapeDtypeStruct((groups, count, batch, width), BF16),
-        scratch_shapes=[pltpu.VMEM((rows + 8, width), F32), pltpu.VMEM((batch, width), F32)]
-        + [pltpu.SMEM((maxlen, batch), jnp.int32)] * groups
-        + [pltpu.SemaphoreType.DMA((groups,))],
-        compiler_params=room(12),
+    slots, rows, width = tables.shape
+    firsts = 4 if rows % 64 == 0 else 1
+    return pl.pallas_call(
+        functools.partial(pool_kernel, maxlen=maxlen),
+        in_specs=[whole(pl.ANY)] * 2,
+        out_specs=whole(pl.ANY),
+        out_shape=jax.ShapeDtypeStruct((groups, slots, batch, width), BF16),
+        scratch_shapes=[pltpu.SMEM((maxlen, batch), jnp.int32)] * groups
+        + [pltpu.VMEM((rows, width), BF16)] * 2
+        + [pltpu.VMEM((rows + 8, width), F32)] * 2
+        + [pltpu.VMEM((groups, batch, width), BF16)] * 2
+        + [pltpu.VMEM((batch, width), F32)]
+        + [pltpu.SemaphoreType.DMA((n,)) for n in (groups, firsts, 2, 2)],
+        compiler_params=room(16),
         name="pool_slots",
     )(ids, in_hbm(tables))
 
 
-def place_kernel(slot_ref, *refs, slots, firsts, counts):
-    parts, out_ref, sem = refs[:-2], refs[-2], refs[-1]
-    width = parts[0].shape[3]
+def place_kernel(slot_ref, pooled_ref, out_ref, sem):
+    slots, _, width = pooled_ref.shape[1:]
     feats = slot_ref.shape[0]
 
-    def put(f, part, owner, local):
+    def put(f, slot):
+        owner = lax.div(slot, slots)
         to = out_ref.at[:, pl.ds(f * width, width)]
-        return pltpu.make_async_copy(part.at[owner, local], to, sem.at[f])
+        return pltpu.make_async_copy(pooled_ref.at[owner, slot - owner * slots], to, sem.at[f])
 
     for f in range(feats):
-        slot = slot_ref[f]
-        owner = slot // slots
-        local = slot - owner * slots
-        for part, first, count in zip(parts, firsts, counts):
-            if len(parts) == 1:
-                put(f, part, owner, local).start()
-            else:
-
-                @pl.when((local >= first) & (local < first + count))
-                def _(f=f, part=part, owner=owner, at=local - first):
-                    put(f, part, owner, at).start()
-
+        put(f, slot_ref[f]).start()
     for f in range(feats):
-        put(f, parts[0], 0, 0).wait()
-
-
-def place(slot_of_table, parts, firsts, counts, slots):
-    batch, width = parts[0].shape[2:]
+        put(f, slot_ref[f]).wait()
+
+
+def place(slot_of_table, pooled):
+    batch, width = pooled.shape[2:]
     feats = slot_of_table.shape[0]
     return pl.pallas_call(
-        functools.partial(place_kernel, slots=slots, firsts=firsts, counts=counts),
-        in_specs=[whole(pltpu.SMEM)] + [whole(pl.ANY)] * len(parts),
+        place_kernel,
+        in_specs=[whole(pltpu.SMEM), whole(pl.ANY)],
         out_specs=whole(pl.ANY),
         out_shape=jax.ShapeDtypeStruct((batch, feats * width), BF16),
         scratch_shapes=[pltpu.SemaphoreType.DMA((feats,))],
         compiler_params=room(4),
         name="place",
-    )(slot_of_table, *parts)
+    )(slot_of_table, pooled)
 
 
 def grads_kernel(pos_ref, own_ref, sib_ref, *refs, owners, groups, chunks):
@@ -273,8 +313,8 @@
     return pl.pallas_call(
         functools.partial(grads_kernel, owners=owners, groups=groups, chunks=chunks),
         in_specs=[whole(pltpu.SMEM)] + [whole()] * 2 + [whole(pl.ANY)] * 4,
-        out_specs=[whole()] + [whole(pl.ANY)] * others,
-        out_shape=[jax.ShapeDtypeStruct(shape, F32)] + [jax.ShapeDtypeStruct(shape, BF16)] * others,
+        out_specs=[whole()] + [whole(pltpu.HBM)] * others,
+        out_shape=[jax.ShapeDtypeStruct(shape, F32)] + [pltpu.HBM(shape, BF16)] * others,
         scratch_shapes=[
             pltpu.VMEM((4 * batch, step), BF16),
             pltpu.VMEM((wide, tall * block), F32),
@@ -359,7 +399,7 @@
     return parts[0], came
 
 
-def exchange_end(keep, came, factor):
+def exchange_end(keep, came, embedded, factor):
     groups = lax.axis_size("grp")
     far = groups // 2
 
@@ -370,7 +410,8 @@
     last = []
     for r in range(1, far):
         last.append(lax.ppermute(out[r], "grp", to_z(r)))
-    return finish(out[0], last, factor)
+    embedded, keep = lax.optimization_barrier((embedded, out[0]))
+    return embedded, *finish(keep, last, factor)
 
 
 def grads_plain(x, ct, up, down, factor):
@@ -403,14 +444,11 @@
     got = lax.all_to_all(masked.reshape(owners, slots * maxlen, batch), "tbl", 0, 0)
     if tiled:
         got, keep = lax.optimization_barrier((got, keep))
-    firsts, counts = (0,), (slots,)
-    parts = []
-    for first, count in zip(firsts, counts):
-        pooled = pool_slots(got, tables, first, count, maxlen)
-        parts.append(lax.all_to_all(pooled, "tbl", 0, 0))
-    embedded = place(slot_of_table, parts, firsts, counts, slots)
+    pooled = pool_slots(got, tables, maxlen)
+    pooled = lax.all_to_all(pooled, "tbl", 0, 0)
+    embedded = place(slot_of_table, pooled)
     if tiled:
-        grad_up, grad_down = exchange_end(keep, came, factor)
+        embedded, grad_up, grad_down = exchange_end(keep, came, embedded, factor)
     else:
         grad_up, grad_down = grads_plain(x, ct, up, down, factor)
     return embedded, grad_up, grad_down

time: 85.7 us -> 81.6 us (0.952)
  local copies, waits for them, and re-layouts: 1.55 us -> 0.02 us
  waiting for transfers between devices: 34 us -> 32.8 us
  Pallas kernels: 30.7 us -> 29.6 us
    ppermute x3, waiting for transfers between devices: 5.75 us -> 4.09 us  [exchange_end(): last.append(lax.ppermute(out[r], 'grp', to_z(r)))]
    unnamed x10 -> x8, local copies, waits for them, and re-layouts: 1.55 us -> 0.02 us
    pallas_call x2, Pallas kernels: 21.8 us -> 20.6 us  [the longest x1 19 us: pool_slots(): pl.pallas_call(functools.partial(pool_kernel, maxlen=maxlen), in_specs=[w...]
  transfers between devices with their start and end apart: 11 -> 11, of which waited for: 3 -> 4; matrix products, arithmetic and copies ran while one was open for 0% -> 0% of each run, Pallas kernels for 10% -> 12%
where the time goes in v5:
time: 81.6 us; the launch traced here: 81.3 us
  waiting for transfers between devices  32.8 us (40%)
  Pallas kernels  29.6 us (36%)
  starting transfers between devices  18.1 us (22%)
    ppermute x3, waiting for transfers between devices, exchange_start(): came.append(lax.ppermute(parts[i], ('grp', 'tbl'), to(i // tall, i % tall)))  28.3 us
    pallas_call x1, Pallas kernels, pool_slots(): pl.pallas_call(functools.partial(pool_kernel, maxlen=maxlen), in_specs=[w...  19 us
    ppermute x3, starting transfers between devices, exchange_end(): last.append(lax.ppermute(out[r], 'grp', to_z(r)))  5.76 us
    pallas_call x1, Pallas kernels, part_grads(): pl.pallas_call(functools.partial(grads_kernel, owners=owners, groups=grou...  4.25 us
    ppermute x3, waiting for transfers between devices, exchange_end(): last.append(lax.ppermute(out[r], 'grp', to_z(r)))  4.09 us
    all_to_all x1, starting transfers between devices, on_device(): lax.all_to_all(masked.reshape(owners, slots * maxlen, batch), 'tbl', 0, 0)  3.89 us
    pallas_call x1, Pallas kernels, prep(): pl.pallas_call(functools.partial(prep_kernel, maxlen=maxlen, rows=rows),...  3.68 us
    ppermute x3, starting transfers between devices, exchange_start(): came.append(lax.ppermute(parts[i], ('grp', 'tbl'), to(i // tall, i % tall)))  3.68 us
  transfers between devices with their start and end apart: 11, of which 4 were waited for; matrix products, arithmetic and copies ran while one was open for 0% of the time, Pallas kernels for 12%

profile of v5, /device:TPU:0, one launch (start us, length us, event | category | flops | bytes accessed | tf_op | source)
XLA Modules:
  0.0 81.3 jit_solution(9891983316294506455)
XLA Ops:
  0.6 0.6 collective-permute-start.1
  1.2 0.1 collective-permute-start.2
  1.3 3.7 %prep.1 = (s32[224,128]{1,0:T(8,128)}, bf16[2,128,256]{2,1,0:T(8,128)(2,1)S(1)}) custom-call(s32[1,26]{1,0:T(1,128)} %bitcast.6, s32[224,128]{1,0:T(8,128)} %bitcast.7, s32[26,128]{1,0:T(8,128)} %bitcast.8, bf16[128,3456]{1,0:T(8,128)(2,1)} %refs_0_.1, bf16[128,3456]{1,0:T(8,128)(2,1)} %refs_1_.1, bf16[3456,256]{1,0:T(8,128)(2,1)} %refs_5_.1, ...), custom_call_target="tpu_custom_call" | custom-call | tf_op jit(solution)/shard_map/prep/pallas_call | solution.py:80
  5.0 0.5 collective-permute-start
  5.5 3.9 %all-to-all-start = ((s32[4,56,128]{2,1,0:T(8,128)}), s32[4,56,128]{2,1,0:T(8,128)S(1)}, u32[]{:S(2)}, u32[]{:S(2)}) async-start(s32[4,56,128]{2,1,0:T(8,128)} %bitcast.3), calls=%async_computation | async-start | bytes 229376 | tf_op jit(solution)/shard_map/all_to_all | solution.py:444
  9.3 0.0 collective-permute-done.sib_ref
  9.3 0.0 collective-permute-done.1.refs_2_
  9.4 0.0 collective-permute-done.2.refs_3_
  9.4 4.3 %part_grads.1 = (f32[4,432,128]{2,1,0:T(8,128)S(1)}, bf16[4,432,128]{2,1,0:T(8,128)(2,1)}, bf16[4,432,128]{2,1,0:T(8,128)(2,1)}, bf16[4,432,128]{2,1,0:T(8,128)(2,1)}) custom-call(s32[1]{0:T(128)} %bitcast.4.pos_ref, bf16[2,128,256]{2,1,0:T(8,128)(2,1)S(1)} %get-tuple-element.20.own_ref, bf16[2,128,256]{2,1,0:T(8,128)(2,1)S(1)} %collective-permute-done.sib_ref, ...), custom_call_target="tpu_custom_call" | custom-call | tf_op jit(solution)/shard_map/part_grads/pallas_call | solution.py:313
  13.6 0.4 all-to-all-done.ids_hbm
  14.0 19.0 %pool_slots.1 = bf16[4,7,128,128]{3,2,1,0:T(8,128)(2,1)} custom-call(s32[4,56,128]{2,1,0:T(8,128)S(1)} %all-to-all-done.ids_hbm, bf16[7,6144,128]{2,1,0:T(8,128)(2,1)} %tables_hbm.1), custom_call_target="tpu_custom_call" | custom-call | tf_op jit(solution)/shard_map/pool_slots/pallas_call | solution.py:187
  33.0 0.0 copy-start.3
  33.0 0.0 copy-start.2
  33.1 0.0 copy-start.1
  33.1 0.0 copy-start
  33.1 3.6 %all-to-all-start.1 = ((bf16[4,7,128,128]{3,2,1,0:T(8,128)(2,1)}), bf16[4,7,128,128]{3,2,1,0:T(8,128)(2,1)S(1)}, u32[]{:S(2)}, u32[]{:S(2)}) async-start(bf16[4,7,128,128]{3,2,1,0:T(8,128)(2,1)} %pool_slots.1), calls=%async_computation.1 | async-start | bytes 1835008 | tf_op jit(solution)/shard_map/all_to_all | solution.py:448
  36.7 0.0 copy-done.3
  36.7 2.0 %collective-permute-start.3 = (bf16[4,432,128]{2,1,0:T(8,128)(2,1)S(1)}, bf16[4,432,128]{2,1,0:T(8,128)(2,1)S(1)}, u32[]{:S(2)}, u32[]{:S(2)}) collective-permute-start(bf16[4,432,128]{2,1,0:T(8,128)(2,1)S(1)} %copy-done.3), channel_id=1, source_target_pairs={{0,2},{1,3},{2,0},{3,1},{4,6},{5,7},{6,4},{7,5},{8,10},{9,11},{10,... | collective-permute-start | bytes 1327112 | tf_op jit(solution)/shard_map/ppermute | solution.py:398
  38.7 0.0 copy-done.2
  38.7 1.7 %collective-permute-start.4 = (bf16[4,432,128]{2,1,0:T(8,128)(2,1)S(1)}, bf16[4,432,128]{2,1,0:T(8,128)(2,1)S(1)}, u32[]{:S(2)}, u32[]{:S(2)}) collective-permute-start(bf16[4,432,128]{2,1,0:T(8,128)(2,1)S(1)} %copy-done.2), channel_id=1, source_target_pairs={{0,4},{1,5},{2,6},{3,7},{4,0},{5,1},{6,2},{7,3},{8,12},{9,13},{10,... | collective-permute-start | bytes 1327112 | tf_op jit(solution)/shard_map/ppermute | solution.py:398
  40.4 0.0 copy-done.1
  40.4 0.0 collective-permute-start.5
  40.4 28.3 %collective-permute-done.3.refs_0_ = bf16[4,432,128]{2,1,0:T(8,128)(2,1)S(1)} collective-permute-done((bf16[4,432,128]{2,1,0:T(8,128)(2,1)S(1)}, bf16[4,432,128]{2,1,0:T(8,128)(2,1)S(1)}, u32[]{:S(2)}, u32[]{:S(2)}) %collective-permute-start.3) | collective-permute-done | bytes 442400 | tf_op jit(solution)/shard_map/ppermute | solution.py:398
  68.7 0.0 collective-permute-done.4.refs_1_
  68.7 0.0 collective-permute-done.5.refs_2_
  68.7 0.2 fold.1
  68.9 1.8 %collective-permute-start.6 = (bf16[432,128]{1,0:T(8,128)(2,1)S(1)}, bf16[432,128]{1,0:T(8,128)(2,1)S(1)}, u32[]{:S(2)}, u32[]{:S(2)}) collective-permute-start(bf16[432,128]{1,0:T(8,128)(2,1)S(1)} %get-tuple-element.30), channel_id=1, source_target_pairs={{0,8},{4,12},{8,16},{12,20},{16,24},{20,28},{24,0},{28,4},{1,9},{5... | collective-permute-start | bytes 331784 | tf_op jit(solution)/shard_map/ppermute | solution.py:412
  70.7 2.6 %collective-permute-start.7 = (bf16[432,128]{1,0:T(8,128)(2,1)S(1)}, bf16[432,128]{1,0:T(8,128)(2,1)S(1)}, u32[]{:S(2)}, u32[]{:S(2)}) collective-permute-start(bf16[432,128]{1,0:T(8,128)(2,1)S(1)} %get-tuple-element.31), channel_id=1, source_target_pairs={{0,16},{4,20},{8,24},{12,28},{16,0},{20,4},{24,8},{28,12},{1,17},{... | collective-permute-start | bytes 331784 | tf_op jit(solution)/shard_map/ppermute | solution.py:412
  73.3 1.3 %collective-permute-start.8 = (bf16[432,128]{1,0:T(8,128)(2,1)S(1)}, bf16[432,128]{1,0:T(8,128)(2,1)S(1)}, u32[]{:S(2)}, u32[]{:S(2)}) collective-permute-start(bf16[432,128]{1,0:T(8,128)(2,1)S(1)} %get-tuple-element.32), channel_id=1, source_target_pairs={{0,24},{4,28},{8,0},{12,4},{16,8},{20,12},{24,16},{28,20},{1,25},{... | collective-permute-start | bytes 331784 | tf_op jit(solution)/shard_map/ppermute | solution.py:412
  74.6 0.0 all-to-all-done.1.pooled_ref
  74.7 0.0 copy-done
  74.7 1.7 %place.1 = bf16[128,3328]{1,0:T(8,128)(2,1)} custom-call(s32[26]{0:T(128)S(1)} %copy-done, bf16[4,7,128,128]{3,2,1,0:T(8,128)(2,1)S(1)} %all-to-all-done.1.pooled_ref), custom_call_target="tpu_custom_call" | custom-call | tf_op jit(solution)/shard_map/place/pallas_call | solution.py:221
  76.3 0.3 collective-permute-done.6.refs_1_
  76.7 3.7 %collective-permute-done.7.refs_2_ = bf16[432,128]{1,0:T(8,128)(2,1)S(1)} collective-permute-done((bf16[432,128]{1,0:T(8,128)(2,1)S(1)}, bf16[432,128]{1,0:T(8,128)(2,1)S(1)}, u32[]{:S(2)}, u32[]{:S(2)}) %collective-permute-start.7) | collective-permute-done | bytes 110624 | tf_op jit(solution)/shard_map/ppermute | solution.py:412
  80.4 0.0 collective-permute-done.8.refs_3_
  80.4 0.8 %finish.1 = (f32[64,432]{1,0:T(8,128)}, f32[64,432]{1,0:T(8,128)}) custom-call(f32[432,128]{1,0:T(8,128)S(1)} %get-tuple-element.29.refs_0_, bf16[432,128]{1,0:T(8,128)(2,1)S(1)} %collective-permute-done.6.refs_1_, bf16[432,128]{1,0:T(8,128)(2,1)S(1)} %collective-permute-done.7.refs_2_, bf16[432,128]{1,0:T(8,128)(2,1)S(1)} %collective-permute-done.8.refs_3_), custom_call_target="tpu_custom_call" | custom-call | tf_op jit(solution)/shard_map/finish/pallas_call | solution.py:368
Async XLA Ops:
  0.6 8.7 %collective-permute-start.1 = (bf16[128,3456]{1,0:T(8,128)(2,1)}, bf16[128,3456]{1,0:T(8,128)(2,1)S(1)}, u32[]{:S(2)}, u32[]{:S(2)}) collective-permute-start(bf16[128,3456]{1,0:T(8,128)(2,1)} %refs_0_.1), channel_id=1, source_target_pairs={{0,1},{1,0},{2,3},{3,2},{4,5},{5,4},{6,7},{7,6},{8,9},{9,8},{10,11... | collective-permute-start | bytes 2654216 | tf_op jit(solution)/shard_map/ppermute | solution.py:384
  1.2 8.2 %collective-permute-start.2 = (bf16[128,3456]{1,0:T(8,128)(2,1)}, bf16[128,3456]{1,0:T(8,128)(2,1)S(1)}, u32[]{:S(2)}, u32[]{:S(2)}) collective-permute-start(bf16[128,3456]{1,0:T(8,128)(2,1)} %refs_1_.1), channel_id=1, source_target_pairs={{0,1},{1,0},{2,3},{3,2},{4,5},{5,4},{6,7},{7,6},{8,9},{9,8},{10,11... | collective-permute-start | bytes 2654216 | tf_op jit(solution)/shard_map/ppermute | solution.py:385
  5.0 4.4 %collective-permute-start = (bf16[2,128,256]{2,1,0:T(8,128)(2,1)S(1)}, bf16[2,128,256]{2,1,0:T(8,128)(2,1)S(1)}, u32[]{:S(2)}, u32[]{:S(2)}) collective-permute-start(bf16[2,128,256]{2,1,0:T(8,128)(2,1)S(1)} %get-tuple-element.20.own_ref), channel_id=1, source_target_pairs={{0,1},{1,0},{2,3},{3,2},{4,5},{5,4},{6,7},{7,6},{8,9},{9,8},{10,11... | collective-permute-start | bytes 393224 | tf_op jit(solution)/shard_map/ppermute | solution.py:386
  5.5 8.6 %all-to-all-start = ((s32[4,56,128]{2,1,0:T(8,128)}), s32[4,56,128]{2,1,0:T(8,128)S(1)}, u32[]{:S(2)}, u32[]{:S(2)}) async-start(s32[4,56,128]{2,1,0:T(8,128)} %bitcast.3), calls=%async_computation | async-start | bytes 229376 | tf_op jit(solution)/shard_map/all_to_all | solution.py:444
  33.0 3.7 %copy-start.3 = (bf16[4,432,128]{2,1,0:T(8,128)(2,1)S(1)}, bf16[4,432,128]{2,1,0:T(8,128)(2,1)}, u32[]{:S(2)}) copy-start(bf16[4,432,128]{2,1,0:T(8,128)(2,1)} %get-tuple-element.24) | copy-start | bytes 1327108
  33.0 5.7 %copy-start.2 = (bf16[4,432,128]{2,1,0:T(8,128)(2,1)S(1)}, bf16[4,432,128]{2,1,0:T(8,128)(2,1)}, u32[]{:S(2)}) copy-start(bf16[4,432,128]{2,1,0:T(8,128)(2,1)} %get-tuple-element.25) | copy-start | bytes 1327108
  33.1 7.4 %copy-start.1 = (bf16[4,432,128]{2,1,0:T(8,128)(2,1)S(1)}, bf16[4,432,128]{2,1,0:T(8,128)(2,1)}, u32[]{:S(2)}) copy-start(bf16[4,432,128]{2,1,0:T(8,128)(2,1)} %get-tuple-element.26) | copy-start | bytes 1327108
  33.1 41.6 %copy-start = (s32[26]{0:T(128)S(1)}, s32[26]{0:T(128)}, u32[]{:S(2)}) copy-start(s32[26]{0:T(128)} %slot_ref.1) | copy-start | bytes 316
  33.1 41.6 %all-to-all-start.1 = ((bf16[4,7,128,128]{3,2,1,0:T(8,128)(2,1)}), bf16[4,7,128,128]{3,2,1,0:T(8,128)(2,1)S(1)}, u32[]{:S(2)}, u32[]{:S(2)}) async-start(bf16[4,7,128,128]{3,2,1,0:T(8,128)(2,1)} %pool_slots.1), calls=%async_computation.1 | async-start | bytes 1835008 | tf_op jit(solution)/shard_map/all_to_all | solution.py:448
  36.7 31.9 %collective-permute-start.3 = (bf16[4,432,128]{2,1,0:T(8,128)(2,1)S(1)}, bf16[4,432,128]{2,1,0:T(8,128)(2,1)S(1)}, u32[]{:S(2)}, u32[]{:S(2)}) collective-permute-start(bf16[4,432,128]{2,1,0:T(8,128)(2,1)S(1)} %copy-done.3), channel_id=1, source_target_pairs={{0,2},{1,3},{2,0},{3,1},{4,6},{5,7},{6,4},{7,5},{8,10},{9,11},{10,... | collective-permute-start | bytes 1327112 | tf_op jit(solution)/shard_map/ppermute | solution.py:398
  38.7 30.0 %collective-permute-start.4 = (bf16[4,432,128]{2,1,0:T(8,128)(2,1)S(1)}, bf16[4,432,128]{2,1,0:T(8,128)(2,1)S(1)}, u32[]{:S(2)}, u32[]{:S(2)}) collective-permute-start(bf16[4,432,128]{2,1,0:T(8,128)(2,1)S(1)} %copy-done.2), channel_id=1, source_target_pairs={{0,4},{1,5},{2,6},{3,7},{4,0},{5,1},{6,2},{7,3},{8,12},{9,13},{10,... | collective-permute-start | bytes 1327112 | tf_op jit(solution)/shard_map/ppermute | solution.py:398
  40.4 28.3 %collective-permute-start.5 = (bf16[4,432,128]{2,1,0:T(8,128)(2,1)S(1)}, bf16[4,432,128]{2,1,0:T(8,128)(2,1)S(1)}, u32[]{:S(2)}, u32[]{:S(2)}) collective-permute-start(bf16[4,432,128]{2,1,0:T(8,128)(2,1)S(1)} %copy-done.1), channel_id=1, source_target_pairs={{0,6},{1,7},{2,4},{3,5},{4,2},{5,3},{6,0},{7,1},{8,14},{9,15},{10,... | collective-permute-start | bytes 1327112 | tf_op jit(solution)/shard_map/ppermute | solution.py:398
  68.9 7.8 %collective-permute-start.6 = (bf16[432,128]{1,0:T(8,128)(2,1)S(1)}, bf16[432,128]{1,0:T(8,128)(2,1)S(1)}, u32[]{:S(2)}, u32[]{:S(2)}) collective-permute-start(bf16[432,128]{1,0:T(8,128)(2,1)S(1)} %get-tuple-element.30), channel_id=1, source_target_pairs={{0,8},{4,12},{8,16},{12,20},{16,24},{20,28},{24,0},{28,4},{1,9},{5... | collective-permute-start | bytes 331784 | tf_op jit(solution)/shard_map/ppermute | solution.py:412
  70.7 9.7 %collective-permute-start.7 = (bf16[432,128]{1,0:T(8,128)(2,1)S(1)}, bf16[432,128]{1,0:T(8,128)(2,1)S(1)}, u32[]{:S(2)}, u32[]{:S(2)}) collective-permute-start(bf16[432,128]{1,0:T(8,128)(2,1)S(1)} %get-tuple-element.31), channel_id=1, source_target_pairs={{0,16},{4,20},{8,24},{12,28},{16,0},{20,4},{24,8},{28,12},{1,17},{... | collective-permute-start | bytes 331784 | tf_op jit(solution)/shard_map/ppermute | solution.py:412
  73.3 7.1 %collective-permute-start.8 = (bf16[432,128]{1,0:T(8,128)(2,1)S(1)}, bf16[432,128]{1,0:T(8,128)(2,1)S(1)}, u32[]{:S(2)}, u32[]{:S(2)}) collective-permute-start(bf16[432,128]{1,0:T(8,128)(2,1)S(1)} %get-tuple-element.32), channel_id=1, source_target_pairs={{0,24},{4,28},{8,0},{12,4},{16,8},{20,12},{24,16},{28,20},{1,25},{... | collective-permute-start | bytes 331784 | tf_op jit(solution)/shard_map/ppermute | solution.py:412

commit v6 on v5

--- a/solution.py
+++ b/solution.py
@@ -24,6 +24,14 @@
 
 def in_hbm(x):
     return pltpu.with_memory_space_constraint(x, pltpu.HBM)
+
+
+def owner_at(t, d, owners):
+    return 2 * lax.rem((t >> 1) + (d >> 1), owners // 2) + ((t & 1) ^ (d & 1))
+
+
+def owner_pairs(d, owners):
+    return [(t, 2 * ((t // 2 + d // 2) % (owners // 2)) + (t % 2 ^ d % 2)) for t in range(owners)]
 
 
 def masked_ids(slot_ref, ids_ref, lens_ref, maxlen, rows):
@@ -37,23 +45,9 @@
     return jnp.where(keep, ids_ref[...], rows)
 
 
-def mask_kernel(slot_ref, ids_ref, lens_ref, out_ref, *, maxlen, rows):
-    out_ref[...] = masked_ids(slot_ref, ids_ref, lens_ref, maxlen, rows)
-
-
-def mask_ids(slot_of_table, ids, lengths, maxlen, rows):
-    return pl.pallas_call(
-        functools.partial(mask_kernel, maxlen=maxlen, rows=rows),
-        in_specs=[whole()] * 3,
-        out_specs=whole(),
-        out_shape=jax.ShapeDtypeStruct((ids.shape[1], ids.shape[0]), jnp.int32),
-        compiler_params=room(4),
-        name="mask_ids",
-    )(slot_of_table.reshape(1, -1), ids.T, lengths.T)
-
-
-def prep_kernel(*refs, maxlen, rows):
-    sources, (masked_ref, rank_ref), targets, sem = refs[:7], refs[7:9], refs[9:16], refs[16]
+def prep_kernel(pos_ref, *refs, owners, maxlen, rows):
+    sources, mine, rank_ref = refs[:7], refs[7 : 7 + owners], refs[7 + owners]
+    targets, masked_ref, sem = refs[8 + owners : 15 + owners], refs[15 + owners], refs[16 + owners]
     slot_ref, ids_ref, lens_ref, x_ref, ct_ref, down_ref, up_ref = targets
     loads = [
         pltpu.make_async_copy(src, dst, sem.at[i]) for i, (src, dst) in enumerate(zip(sources, targets))
@@ -63,6 +57,11 @@
     for load in loads[:3]:
         load.wait()
     masked_ref[...] = masked_ids(slot_ref, ids_ref, lens_ref, maxlen, rows)
+    t = lax.rem(pos_ref[0], owners)
+    entries = mine[0].shape[0]
+    for d in range(owners):
+        start = pl.multiple_of(owner_at(t, d, owners) * entries, maxlen)
+        mine[d][...] = masked_ref[pl.ds(start, entries), :]
     for load in loads[3:5]:
         load.wait()
     x = x_ref[...]
@@ -75,26 +74,27 @@
     ).astype(BF16)
 
 
-def prep(slot_of_table, ids, lengths, x, ct, down, up, maxlen, rows):
+def prep(pos, slot_of_table, ids, lengths, x, ct, down, up, owners, maxlen, rows):
     sources = [slot_of_table.reshape(1, -1), ids.T, lengths.T, x, ct, down, up]
-    return pl.pallas_call(
-        functools.partial(prep_kernel, maxlen=maxlen, rows=rows),
-        in_specs=[whole(pl.ANY)] * 7,
-        out_specs=[whole()] * 2,
-        out_shape=[
-            jax.ShapeDtypeStruct(ids.shape[::-1], jnp.int32),
-            jax.ShapeDtypeStruct((2, x.shape[0], down.shape[1]), BF16),
-        ],
+    batch, entries = ids.shape
+    *mine, rank = pl.pallas_call(
+        functools.partial(prep_kernel, owners=owners, maxlen=maxlen, rows=rows),
+        in_specs=[whole(pltpu.SMEM)] + [whole(pl.ANY)] * 7,
+        out_specs=[whole()] * (owners + 1),
+        out_shape=[jax.ShapeDtypeStruct((entries // owners, batch), jnp.int32)] * owners
+        + [jax.ShapeDtypeStruct((2, batch, down.shape[1]), BF16)],
         scratch_shapes=[pltpu.VMEM(a.shape, a.dtype) for a in sources]
-        + [pltpu.SemaphoreType.DMA((7,))],
+        + [pltpu.VMEM((entries, batch), jnp.int32), pltpu.SemaphoreType.DMA((7,))],
         compiler_params=room(16),
         name="prep",
-    )(*[in_hbm(a) for a in sources])
-
-
-def pool_kernel(ids_hbm, tables_hbm, out_hbm, *refs, maxlen):
-    groups, count, batch, width = out_hbm.shape
-    near, refs = refs[:groups], refs[groups:]
+    )(pos, *[in_hbm(a) for a in sources])
+    return mine, rank
+
+
+def pool_kernel(*refs, groups, maxlen):
+    ids_hbm, tables_hbm, outs = refs[:groups], refs[groups], refs[groups + 1 : 2 * groups + 1]
+    near, refs = refs[2 * groups + 1 : 3 * groups + 1], refs[3 * groups + 1 :]
+    count, batch, width = outs[0].shape
     stage, wide, pooled, sum_ref = refs[0:2], refs[2:4], refs[4:6], refs[6]
     ids_sem, first_sem, table_sem, out_sem = refs[7:]
     rows = stage[0].shape[0]
@@ -105,7 +105,7 @@
 
     def fetch_ids(g, slot):
         start = pl.multiple_of(slot * maxlen, maxlen)
-        return pltpu.make_async_copy(ids_hbm.at[g, pl.ds(start, maxlen)], near[g], ids_sem.at[g])
+        return pltpu.make_async_copy(ids_hbm[g].at[pl.ds(start, maxlen)], near[g], ids_sem.at[g])
 
     def fetch_table(slot, at):
         return pltpu.make_async_copy(tables_hbm.at[slot], stage[at], table_sem.at[at])
@@ -114,8 +114,8 @@
         part = pl.ds(i * head, head)
         return pltpu.make_async_copy(tables_hbm.at[0, part], stage[0].at[part], first_sem.at[i])
 
-    def put(slot, at):
-        return pltpu.make_async_copy(pooled[at], out_hbm.at[:, slot], out_sem.at[at])
+    def put(slot, at, g):
+        return pltpu.make_async_copy(pooled[at].at[g], outs[g].at[slot], out_sem.at[at * groups + g])
 
     def widen(at, start, size):
         part = pl.ds(start, size)
@@ -134,7 +134,8 @@
 
         @pl.when(slot >= 2)
         def _():
-            put(slot - 2, at).wait()
+            for g in range(groups):
+                put(slot - 2, at, g).wait()
 
         for g in range(groups):
             fetch_ids(g, slot).wait()
@@ -147,12 +148,11 @@
                     total = total + wide[at][pl.ds(near[g][k, b], 1), :]
                 sum_ref[pl.ds(b, 1), :] = total
             pooled[at][g] = sum_ref[...].astype(BF16)
+            put(slot, at, g).start()
 
             @pl.when(slot + 1 < count)
             def _(g=g):
                 fetch_ids(g, slot + 1).start()
-
-        put(slot, at).start()
 
     for g in range(groups):
         fetch_ids(g, 0).start()
@@ -177,56 +177,66 @@
 
     lax.fori_loop(0, (count + 1) // 2, pair, 0)
     for slot in range(max(count - 2, 0), count):
-        put(slot, slot % 2).wait()
+        for g in range(groups):
+            put(slot, slot % 2, g).wait()
 
 
 def pool_slots(ids, tables, maxlen):
-    groups, _, batch = ids.shape
+    groups, batch = len(ids), ids[0].shape[1]
     slots, rows, width = tables.shape
     firsts = 4 if rows % 64 == 0 else 1
     return pl.pallas_call(
-        functools.partial(pool_kernel, maxlen=maxlen),
-        in_specs=[whole(pl.ANY)] * 2,
-        out_specs=whole(pl.ANY),
-        out_shape=jax.ShapeDtypeStruct((groups, slots, batch, width), BF16),
+        functools.partial(pool_kernel, groups=groups, maxlen=maxlen),
+        in_specs=[whole(pl.ANY)] * (groups + 1),
+        out_specs=[whole(pl.ANY)] * groups,
+        out_shape=[jax.ShapeDtypeStruct((slots, batch, width), BF16)] * groups,
         scratch_shapes=[pltpu.SMEM((maxlen, batch), jnp.int32)] * groups
         + [pltpu.VMEM((rows, width), BF16)] * 2
         + [pltpu.VMEM((rows + 8, width), F32)] * 2
         + [pltpu.VMEM((groups, batch, width), BF16)] * 2
         + [pltpu.VMEM((batch, width), F32)]
-        + [pltpu.SemaphoreType.DMA((n,)) for n in (groups, firsts, 2, 2)],
+        + [pltpu.SemaphoreType.DMA((n,)) for n in (groups, firsts, 2, 2 * groups)],
         compiler_params=room(16),
         name="pool_slots",
-    )(ids, in_hbm(tables))
-
-
-def place_kernel(slot_ref, pooled_ref, out_ref, sem):
-    slots, _, width = pooled_ref.shape[1:]
+    )(*ids, in_hbm(tables))
+
+
+def place_kernel(pos_ref, slot_ref, *refs):
+    parts, out_ref, sem = refs[:-2], refs[-2], refs[-1]
+    owners = len(parts)
+    slots, _, width = parts[0].shape
     feats = slot_ref.shape[0]
-
-    def put(f, slot):
-        owner = lax.div(slot, slots)
+    t = lax.rem(pos_ref[0], owners)
+
+    def put(f, part, local):
         to = out_ref.at[:, pl.ds(f * width, width)]
-        return pltpu.make_async_copy(pooled_ref.at[owner, slot - owner * slots], to, sem.at[f])
+        return pltpu.make_async_copy(part.at[local], to, sem.at[f])
+
+    for d, part in enumerate(parts):
+        first = owner_at(t, d, owners) * slots
+        for f in range(feats):
+            local = slot_ref[f] - first
+
+            @pl.when((local >= 0) & (local < slots))
+            def _(f=f, part=part, local=local):
+                put(f, part, local).start()
 
     for f in range(feats):
-        put(f, slot_ref[f]).start()
-    for f in range(feats):
-        put(f, slot_ref[f]).wait()
-
-
-def place(slot_of_table, pooled):
-    batch, width = pooled.shape[2:]
+        put(f, parts[0], 0).wait()
+
+
+def place(pos, slot_of_table, parts):
+    _, batch, width = parts[0].shape
     feats = slot_of_table.shape[0]
     return pl.pallas_call(
         place_kernel,
-        in_specs=[whole(pltpu.SMEM), whole(pl.ANY)],
+        in_specs=[whole(pltpu.SMEM)] * 2 + [whole(pl.ANY)] * len(parts),
         out_specs=whole(pl.ANY),
         out_shape=jax.ShapeDtypeStruct((batch, feats * width), BF16),
         scratch_shapes=[pltpu.SemaphoreType.DMA((feats,))],
         compiler_params=room(4),
         name="place",
-    )(slot_of_table, pooled)
+    )(pos, slot_of_table, *parts)
 
 
 def grads_kernel(pos_ref, own_ref, sib_ref, *refs, owners, groups, chunks):
@@ -376,10 +386,9 @@
     return up, down.T
 
 
-def exchange_start(x, ct, own):
+def exchange_start(pos, x, ct, own):
     owners, groups = lax.axis_size("tbl"), lax.axis_size("grp")
     tall = owners // 2
-    pos = lax.axis_index(("grp", "tbl")).astype(jnp.int32).reshape(1)
     other_core = [(i, i ^ 1) for i in range(owners)]
     xs = lax.ppermute(x, "tbl", other_core)
     cts = lax.ppermute(ct, "tbl", other_core)
@@ -436,17 +445,20 @@
     factor = 1.0 / math.sqrt(batch * owners * groups)
     tiled = by_exchange(owners, groups, *down.shape)
 
+    pos = lax.axis_index(("grp", "tbl")).astype(jnp.int32).reshape(1)
+    mine, own = prep(pos, slot_of_table, ids, lengths, x, ct, down, up, owners, maxlen, rows)
+    got = list(mine[:1])
+    for d in range(1, owners):
+        got.append(lax.ppermute(mine[d], "tbl", owner_pairs(d, owners)))
     if tiled:
-        masked, own = prep(slot_of_table, ids, lengths, x, ct, down, up, maxlen, rows)
-        keep, came = exchange_start(x, ct, own)
-    else:
-        masked = mask_ids(slot_of_table, ids, lengths, maxlen, rows)
-    got = lax.all_to_all(masked.reshape(owners, slots * maxlen, batch), "tbl", 0, 0)
-    if tiled:
+        keep, came = exchange_start(pos, x, ct, own)
         got, keep = lax.optimization_barrier((got, keep))
     pooled = pool_slots(got, tables, maxlen)
-    pooled = lax.all_to_all(pooled, "tbl", 0, 0)
-    embedded = place(slot_of_table, pooled)
+    parts = list(pooled[:1])
+    for d in range(1, owners):
+        back = [(b, a) for a, b in owner_pairs(d, owners)]
+        parts.append(lax.ppermute(pooled[d], "tbl", back))
+    embedded = place(pos, slot_of_table, parts)
     if tiled:
         embedded, grad_up, grad_down = exchange_end(keep, came, embedded, factor)
     else:

time: 81.6 us -> 61.6 us (0.75)
  waiting for transfers between devices: 32.8 us -> 13.7 us
  starting transfers between devices: 18.1 us -> 16.9 us
    ppermute x3, waiting for transfers between devices: 28.3 us -> 0.01 us  [exchange_start(): came.append(lax.ppermute(parts[i], ('grp', 'tbl'), to(i // tall, i % tall)))]
    ppermute x0 -> x6, waiting for transfers between devices: none -> 12.1 us  [the longest x3 7.72 us: on_device(): got.append(lax.ppermute(mine[d], 'tbl', owner_pairs(d, owners)))]
    all_to_all x2 -> x0, starting transfers between devices: 7.53 us -> none  [the longest x1 3.89 us: on_device(): lax.all_to_all(masked.reshape(owners, slots * maxlen, batch), 'tbl', 0, 0)]
    ppermute x0 -> x6, starting transfers between devices: none -> 5.7 us  [the longest x3 2.91 us: on_device(): got.append(lax.ppermute(mine[d], 'tbl', owner_pairs(d, owners)))]
    ppermute x3, waiting for transfers between devices: 4.09 us -> 0.67 us  [exchange_end(): last.append(lax.ppermute(out[r], 'grp', to_z(r)))]
    ppermute x1, waiting for transfers between devices: 0.01 us -> 0.99 us  [exchange_start(): sib = lax.ppermute(own, 'tbl', other_core)]
  transfers between devices with their start and end apart: 11 -> 15, of which waited for: 4 -> 6; matrix products, arithmetic and copies ran while one was open for 0% -> 0% of each run, Pallas kernels for 12% -> 41%
where the time goes in v6:
time: 61.6 us; the launch traced here: 61.4 us
  Pallas kernels  30.1 us (49%)
  starting transfers between devices  16.9 us (27%)
  waiting for transfers between devices  13.7 us (22%)
  between operations  0.71 us (1%)
    pallas_call x1, Pallas kernels, pool_slots(): pl.pallas_call(functools.partial(pool_kernel, groups=groups, maxlen=maxle...  19.4 us
    ppermute x3, waiting for transfers between devices, on_device(): got.append(lax.ppermute(mine[d], 'tbl', owner_pairs(d, owners)))  7.72 us
    ppermute x3, starting transfers between devices, exchange_end(): last.append(lax.ppermute(out[r], 'grp', to_z(r)))  5.56 us
    ppermute x3, starting transfers between devices, exchange_start(): came.append(lax.ppermute(parts[i], ('grp', 'tbl'), to(i // tall, i % tall)))  4.47 us
    ppermute x3, waiting for transfers between devices, on_device(): parts.append(lax.ppermute(pooled[d], 'tbl', back))  4.35 us
    pallas_call x1, Pallas kernels, part_grads(): pl.pallas_call(functools.partial(grads_kernel, owners=owners, groups=grou...  4.24 us
    pallas_call x1, Pallas kernels, prep(): pl.pallas_call(functools.partial(prep_kernel, owners=owners, maxlen=maxle...  3.68 us
    ppermute x3, starting transfers between devices, on_device(): got.append(lax.ppermute(mine[d], 'tbl', owner_pairs(d, owners)))  2.91 us
  transfers between devices with their start and end apart: 15, of which 6 were waited for; matrix products, arithmetic and copies ran while one was open for 0% of the time, Pallas kernels for 41%

profile of v6, /device:TPU:0, one launch (start us, length us, event | category | flops | bytes accessed | tf_op | source)
XLA Modules:
  0.0 61.4 jit_solution(10341392392254187259)
XLA Ops:
  0.6 0.6 collective-permute-start.4
  1.2 0.1 collective-permute-start.5
  1.3 3.7 %prep.1 = (s32[56,128]{1,0:T(8,128)S(1)}, s32[56,128]{1,0:T(8,128)S(1)}, s32[56,128]{1,0:T(8,128)S(1)}, s32[56,128]{1,0:T(8,128)S(1)}, bf16[2,128,256]{2,1,0:T(8,128)(2,1)S(1)}) custom-call(s32[1]{0:T(128)} %bitcast.pos_ref, s32[1,26]{1,0:T(1,128)} %bitcast.5, s32[224,128]{1,0:T(8,128)} %bitcast.6, s32[26,128]{1,0:T(8,128)} %bitcast.7, ...), custom_call_target="tpu_custom_call" | custom-call | tf_op jit(solution)/shard_map/prep/pallas_call | solution.py:80
  5.0 0.5 collective-permute-start.3
  5.5 1.0 %collective-permute-done.3.sib_ref = bf16[2,128,256]{2,1,0:T(8,128)(2,1)S(1)} collective-permute-done((bf16[2,128,256]{2,1,0:T(8,128)(2,1)S(1)}, bf16[2,128,256]{2,1,0:T(8,128)(2,1)S(1)}, u32[]{:S(2)}, u32[]{:S(2)}) %collective-permute-start.3) | collective-permute-done | bytes 131104 | tf_op jit(solution)/shard_map/ppermute | solution.py:395
  6.4 0.0 collective-permute-done.4.refs_2_
  6.4 0.0 collective-permute-done.5.refs_3_
  6.4 4.2 %part_grads.1 = (f32[4,432,128]{2,1,0:T(8,128)S(1)}, bf16[4,432,128]{2,1,0:T(8,128)(2,1)}, bf16[4,432,128]{2,1,0:T(8,128)(2,1)}, bf16[4,432,128]{2,1,0:T(8,128)(2,1)}) custom-call(s32[1]{0:T(128)} %bitcast.pos_ref, bf16[2,128,256]{2,1,0:T(8,128)(2,1)S(1)} %get-tuple-element.33.own_ref, bf16[2,128,256]{2,1,0:T(8,128)(2,1)S(1)} %collective-permute-done.3.sib_ref, ...), custom_call_target="tpu_custom_call" | custom-call | tf_op jit(solution)/shard_map/part_grads/pallas_call | solution.py:323
  10.7 2.9 %collective-permute-start.9 = (bf16[4,432,128]{2,1,0:T(8,128)(2,1)}, bf16[4,432,128]{2,1,0:T(8,128)(2,1)S(1)}, u32[]{:S(2)}, u32[]{:S(2)}) collective-permute-start(bf16[4,432,128]{2,1,0:T(8,128)(2,1)} %get-tuple-element.44), channel_id=1, source_target_pairs={{0,2},{1,3},{2,0},{3,1},{4,6},{5,7},{6,4},{7,5},{8,10},{9,11},{10,... | collective-permute-start | bytes 1327112 | tf_op jit(solution)/shard_map/ppermute | solution.py:407
  13.6 1.5 %collective-permute-start.10 = (bf16[4,432,128]{2,1,0:T(8,128)(2,1)}, bf16[4,432,128]{2,1,0:T(8,128)(2,1)S(1)}, u32[]{:S(2)}, u32[]{:S(2)}) collective-permute-start(bf16[4,432,128]{2,1,0:T(8,128)(2,1)} %get-tuple-element.45), channel_id=1, source_target_pairs={{0,4},{1,5},{2,6},{3,7},{4,0},{5,1},{6,2},{7,3},{8,12},{9,13},{10,... | collective-permute-start | bytes 1327112 | tf_op jit(solution)/shard_map/ppermute | solution.py:407
  15.1 0.1 collective-permute-start.11
  15.2 0.0 collective-permute-start
  15.2 1.9 %collective-permute-start.1 = (s32[56,128]{1,0:T(8,128)S(1)}, s32[56,128]{1,0:T(8,128)S(1)}, u32[]{:S(2)}, u32[]{:S(2)}) collective-permute-start(s32[56,128]{1,0:T(8,128)S(1)} %get-tuple-element.31), channel_id=1, source_target_pairs={{0,2},{1,3},{2,0},{3,1},{4,6},{5,7},{6,4},{7,5},{8,10},{9,11},{10,... | collective-permute-start | bytes 86024 | tf_op jit(solution)/shard_map/ppermute | solution.py:452
  17.1 0.0 collective-permute-done.refs_1_
  17.1 1.0 %collective-permute-start.2 = (s32[56,128]{1,0:T(8,128)S(1)}, s32[56,128]{1,0:T(8,128)S(1)}, u32[]{:S(2)}, u32[]{:S(2)}) collective-permute-start(s32[56,128]{1,0:T(8,128)S(1)} %get-tuple-element.32), channel_id=1, source_target_pairs={{0,3},{1,2},{2,1},{3,0},{4,7},{5,6},{6,5},{7,4},{8,11},{9,10},{10,... | collective-permute-start | bytes 86024 | tf_op jit(solution)/shard_map/ppermute | solution.py:452
  18.1 7.6 %collective-permute-done.1.refs_2_ = s32[56,128]{1,0:T(8,128)S(1)} collective-permute-done((s32[56,128]{1,0:T(8,128)S(1)}, s32[56,128]{1,0:T(8,128)S(1)}, u32[]{:S(2)}, u32[]{:S(2)}) %collective-permute-start.1) | collective-permute-done | bytes 28704 | tf_op jit(solution)/shard_map/ppermute | solution.py:452
  25.7 0.1 collective-permute-done.2.refs_3_
  25.8 19.4 %pool_slots.1 = (bf16[7,128,128]{2,1,0:T(8,128)(2,1)S(1)}, bf16[7,128,128]{2,1,0:T(8,128)(2,1)S(1)}, bf16[7,128,128]{2,1,0:T(8,128)(2,1)S(1)}, bf16[7,128,128]{2,1,0:T(8,128)(2,1)S(1)}) custom-call(s32[56,128]{1,0:T(8,128)S(1)} %get-tuple-element.35.refs_0_, s32[56,128]{1,0:T(8,128)S(1)} %collective-permute-done.refs_1_, ...), custom_call_target="tpu_custom_call" | custom-call | tf_op jit(solution)/shard_map/pool_slots/pallas_call | solution.py:188
  45.2 0.0 copy-start
  45.3 0.8 %collective-permute-start.6 = (bf16[7,128,128]{2,1,0:T(8,128)(2,1)S(1)}, bf16[7,128,128]{2,1,0:T(8,128)(2,1)S(1)}, u32[]{:S(2)}, u32[]{:S(2)}) collective-permute-start(bf16[7,128,128]{2,1,0:T(8,128)(2,1)S(1)} %get-tuple-element.40), channel_id=1, source_target_pairs={{1,0},{0,1},{3,2},{2,3},{5,4},{4,5},{7,6},{6,7},{9,8},{8,9},{11,10... | collective-permute-start | bytes 688136 | tf_op jit(solution)/shard_map/ppermute | solution.py:460
  46.0 2.0 %collective-permute-start.7 = (bf16[7,128,128]{2,1,0:T(8,128)(2,1)S(1)}, bf16[7,128,128]{2,1,0:T(8,128)(2,1)S(1)}, u32[]{:S(2)}, u32[]{:S(2)}) collective-permute-start(bf16[7,128,128]{2,1,0:T(8,128)(2,1)S(1)} %get-tuple-element.41), channel_id=1, source_target_pairs={{2,0},{3,1},{0,2},{1,3},{6,4},{7,5},{4,6},{5,7},{10,8},{11,9},{8,1... | collective-permute-start | bytes 688136 | tf_op jit(solution)/shard_map/ppermute | solution.py:460
  48.0 0.0 collective-permute-done.9.refs_0_
  48.0 0.0 collective-permute-start.8
  48.0 0.0 collective-permute-done.10.refs_1_
  48.0 0.0 collective-permute-done.11.refs_2_
  48.1 0.2 fold.1
  48.3 1.6 %collective-permute-start.12 = (bf16[432,128]{1,0:T(8,128)(2,1)S(1)}, bf16[432,128]{1,0:T(8,128)(2,1)S(1)}, u32[]{:S(2)}, u32[]{:S(2)}) collective-permute-start(bf16[432,128]{1,0:T(8,128)(2,1)S(1)} %get-tuple-element.50), channel_id=1, source_target_pairs={{0,8},{4,12},{8,16},{12,20},{16,24},{20,28},{24,0},{28,4},{1,9},{5... | collective-permute-start | bytes 331784 | tf_op jit(solution)/shard_map/ppermute | solution.py:421
  49.9 2.6 %collective-permute-start.13 = (bf16[432,128]{1,0:T(8,128)(2,1)S(1)}, bf16[432,128]{1,0:T(8,128)(2,1)S(1)}, u32[]{:S(2)}, u32[]{:S(2)}) collective-permute-start(bf16[432,128]{1,0:T(8,128)(2,1)S(1)} %get-tuple-element.51), channel_id=1, source_target_pairs={{0,16},{4,20},{8,24},{12,28},{16,0},{20,4},{24,8},{28,12},{1,17},{... | collective-permute-start | bytes 331784 | tf_op jit(solution)/shard_map/ppermute | solution.py:421
  52.5 0.0 collective-permute-done.6.refs_1_
  52.5 1.3 %collective-permute-start.14 = (bf16[432,128]{1,0:T(8,128)(2,1)S(1)}, bf16[432,128]{1,0:T(8,128)(2,1)S(1)}, u32[]{:S(2)}, u32[]{:S(2)}) collective-permute-start(bf16[432,128]{1,0:T(8,128)(2,1)S(1)} %get-tuple-element.52), channel_id=1, source_target_pairs={{0,24},{4,28},{8,0},{12,4},{16,8},{20,12},{24,16},{28,20},{1,25},{... | collective-permute-start | bytes 331784 | tf_op jit(solution)/shard_map/ppermute | solution.py:421
  53.8 0.6 %collective-permute-done.7.refs_2_ = bf16[7,128,128]{2,1,0:T(8,128)(2,1)S(1)} collective-permute-done((bf16[7,128,128]{2,1,0:T(8,128)(2,1)S(1)}, bf16[7,128,128]{2,1,0:T(8,128)(2,1)S(1)}, u32[]{:S(2)}, u32[]{:S(2)}) %collective-permute-start.7) | collective-permute-done | bytes 229408 | tf_op jit(solution)/shard_map/ppermute | solution.py:460
  54.5 3.7 %collective-permute-done.8.refs_3_ = bf16[7,128,128]{2,1,0:T(8,128)(2,1)S(1)} collective-permute-done((bf16[7,128,128]{2,1,0:T(8,128)(2,1)S(1)}, bf16[7,128,128]{2,1,0:T(8,128)(2,1)S(1)}, u32[]{:S(2)}, u32[]{:S(2)}) %collective-permute-start.8) | collective-permute-done | bytes 229408 | tf_op jit(solution)/shard_map/ppermute | solution.py:460
  58.2 0.0 copy-done
  58.2 1.7 %place.1 = bf16[128,3328]{1,0:T(8,128)(2,1)} custom-call(s32[1]{0:T(128)} %bitcast.pos_ref, s32[26]{0:T(128)S(1)} %copy-done, bf16[7,128,128]{2,1,0:T(8,128)(2,1)S(1)} %get-tuple-element.39.refs_0_, bf16[7,128,128]{2,1,0:T(8,128)(2,1)S(1)} %collective-permute-done.6.refs_1_, bf16[7,128,128]{2,1,0:T(8,128)(2,1)S(1)} %collective-permute-done.7.refs_2_, ...), custom_call_target="tpu_custom_call" | custom-call | tf_op jit(solution)/shard_map/place/pallas_call | solution.py:231
  59.9 0.0 collective-permute-done.12.refs_1_
  59.9 0.7 %collective-permute-done.13.refs_2_ = bf16[432,128]{1,0:T(8,128)(2,1)S(1)} collective-permute-done((bf16[432,128]{1,0:T(8,128)(2,1)S(1)}, bf16[432,128]{1,0:T(8,128)(2,1)S(1)}, u32[]{:S(2)}, u32[]{:S(2)}) %collective-permute-start.13) | collective-permute-done | bytes 110624 | tf_op jit(solution)/shard_map/ppermute | solution.py:421
  60.6 0.0 collective-permute-done.14.refs_3_
  60.6 0.8 %finish.1 = (f32[64,432]{1,0:T(8,128)}, f32[64,432]{1,0:T(8,128)}) custom-call(f32[432,128]{1,0:T(8,128)S(1)} %get-tuple-element.49.refs_0_, bf16[432,128]{1,0:T(8,128)(2,1)S(1)} %collective-permute-done.12.refs_1_, bf16[432,128]{1,0:T(8,128)(2,1)S(1)} %collective-permute-done.13.refs_2_, bf16[432,128]{1,0:T(8,128)(2,1)S(1)} %collective-permute-done.14.refs_3_), custom_call_target="tpu_custom_call" | custom-call | tf_op jit(solution)/shard_map/finish/pallas_call | solution.py:378
Async XLA Ops:
  0.6 5.8 %collective-permute-start.4 = (bf16[128,3456]{1,0:T(8,128)(2,1)}, bf16[128,3456]{1,0:T(8,128)(2,1)S(1)}, u32[]{:S(2)}, u32[]{:S(2)}) collective-permute-start(bf16[128,3456]{1,0:T(8,128)(2,1)} %refs_0_.1), channel_id=1, source_target_pairs={{0,1},{1,0},{2,3},{3,2},{4,5},{5,4},{6,7},{7,6},{8,9},{9,8},{10,11... | collective-permute-start | bytes 2654216 | tf_op jit(solution)/shard_map/ppermute | solution.py:393
  1.2 5.3 %collective-permute-start.5 = (bf16[128,3456]{1,0:T(8,128)(2,1)}, bf16[128,3456]{1,0:T(8,128)(2,1)S(1)}, u32[]{:S(2)}, u32[]{:S(2)}) collective-permute-start(bf16[128,3456]{1,0:T(8,128)(2,1)} %refs_1_.1), channel_id=1, source_target_pairs={{0,1},{1,0},{2,3},{3,2},{4,5},{5,4},{6,7},{7,6},{8,9},{9,8},{10,11... | collective-permute-start | bytes 2654216 | tf_op jit(solution)/shard_map/ppermute | solution.py:394
  5.0 1.5 %collective-permute-start.3 = (bf16[2,128,256]{2,1,0:T(8,128)(2,1)S(1)}, bf16[2,128,256]{2,1,0:T(8,128)(2,1)S(1)}, u32[]{:S(2)}, u32[]{:S(2)}) collective-permute-start(bf16[2,128,256]{2,1,0:T(8,128)(2,1)S(1)} %get-tuple-element.33.own_ref), channel_id=1, source_target_pairs={{0,1},{1,0},{2,3},{3,2},{4,5},{5,4},{6,7},{7,6},{8,9},{9,8},{10,11... | collective-permute-start | bytes 393224 | tf_op jit(solution)/shard_map/ppermute | solution.py:395
  10.7 37.3 %collective-permute-start.9 = (bf16[4,432,128]{2,1,0:T(8,128)(2,1)}, bf16[4,432,128]{2,1,0:T(8,128)(2,1)S(1)}, u32[]{:S(2)}, u32[]{:S(2)}) collective-permute-start(bf16[4,432,128]{2,1,0:T(8,128)(2,1)} %get-tuple-element.44), channel_id=1, source_target_pairs={{0,2},{1,3},{2,0},{3,1},{4,6},{5,7},{6,4},{7,5},{8,10},{9,11},{10,... | collective-permute-start | bytes 1327112 | tf_op jit(solution)/shard_map/ppermute | solution.py:407
  13.6 34.4 %collective-permute-start.10 = (bf16[4,432,128]{2,1,0:T(8,128)(2,1)}, bf16[4,432,128]{2,1,0:T(8,128)(2,1)S(1)}, u32[]{:S(2)}, u32[]{:S(2)}) collective-permute-start(bf16[4,432,128]{2,1,0:T(8,128)(2,1)} %get-tuple-element.45), channel_id=1, source_target_pairs={{0,4},{1,5},{2,6},{3,7},{4,0},{5,1},{6,2},{7,3},{8,12},{9,13},{10,... | collective-permute-start | bytes 1327112 | tf_op jit(solution)/shard_map/ppermute | solution.py:407
  15.1 32.9 %collective-permute-start.11 = (bf16[4,432,128]{2,1,0:T(8,128)(2,1)}, bf16[4,432,128]{2,1,0:T(8,128)(2,1)S(1)}, u32[]{:S(2)}, u32[]{:S(2)}) collective-permute-start(bf16[4,432,128]{2,1,0:T(8,128)(2,1)} %get-tuple-element.46), channel_id=1, source_target_pairs={{0,6},{1,7},{2,4},{3,5},{4,2},{5,3},{6,0},{7,1},{8,14},{9,15},{10,... | collective-permute-start | bytes 1327112 | tf_op jit(solution)/shard_map/ppermute | solution.py:407
  15.2 2.0 %collective-permute-start = (s32[56,128]{1,0:T(8,128)S(1)}, s32[56,128]{1,0:T(8,128)S(1)}, u32[]{:S(2)}, u32[]{:S(2)}) collective-permute-start(s32[56,128]{1,0:T(8,128)S(1)} %get-tuple-element.30), channel_id=1, source_target_pairs={{0,1},{1,0},{2,3},{3,2},{4,5},{5,4},{6,7},{7,6},{8,9},{9,8},{10,11... | collective-permute-start | bytes 86024 | tf_op jit(solution)/shard_map/ppermute | solution.py:452
  15.2 10.6 %collective-permute-start.1 = (s32[56,128]{1,0:T(8,128)S(1)}, s32[56,128]{1,0:T(8,128)S(1)}, u32[]{:S(2)}, u32[]{:S(2)}) collective-permute-start(s32[56,128]{1,0:T(8,128)S(1)} %get-tuple-element.31), channel_id=1, source_target_pairs={{0,2},{1,3},{2,0},{3,1},{4,6},{5,7},{6,4},{7,5},{8,10},{9,11},{10,... | collective-permute-start | bytes 86024 | tf_op jit(solution)/shard_map/ppermute | solution.py:452
  17.1 8.7 %collective-permute-start.2 = (s32[56,128]{1,0:T(8,128)S(1)}, s32[56,128]{1,0:T(8,128)S(1)}, u32[]{:S(2)}, u32[]{:S(2)}) collective-permute-start(s32[56,128]{1,0:T(8,128)S(1)} %get-tuple-element.32), channel_id=1, source_target_pairs={{0,3},{1,2},{2,1},{3,0},{4,7},{5,6},{6,5},{7,4},{8,11},{9,10},{10,... | collective-permute-start | bytes 86024 | tf_op jit(solution)/shard_map/ppermute | solution.py:452
  45.2 12.9 %copy-start = (s32[26]{0:T(128)S(1)}, s32[26]{0:T(128)}, u32[]{:S(2)}) copy-start(s32[26]{0:T(128)} %slot_ref.1) | copy-start | bytes 316
  45.3 7.3 %collective-permute-start.6 = (bf16[7,128,128]{2,1,0:T(8,128)(2,1)S(1)}, bf16[7,128,128]{2,1,0:T(8,128)(2,1)S(1)}, u32[]{:S(2)}, u32[]{:S(2)}) collective-permute-start(bf16[7,128,128]{2,1,0:T(8,128)(2,1)S(1)} %get-tuple-element.40), channel_id=1, source_target_pairs={{1,0},{0,1},{3,2},{2,3},{5,4},{4,5},{7,6},{6,7},{9,8},{8,9},{11,10... | collective-permute-start | bytes 688136 | tf_op jit(solution)/shard_map/ppermute | solution.py:460
  46.0 8.5 %collective-permute-start.7 = (bf16[7,128,128]{2,1,0:T(8,128)(2,1)S(1)}, bf16[7,128,128]{2,1,0:T(8,128)(2,1)S(1)}, u32[]{:S(2)}, u32[]{:S(2)}) collective-permute-start(bf16[7,128,128]{2,1,0:T(8,128)(2,1)S(1)} %get-tuple-element.41), channel_id=1, source_target_pairs={{2,0},{3,1},{0,2},{1,3},{6,4},{7,5},{4,6},{5,7},{10,8},{11,9},{8,1... | collective-permute-start | bytes 688136 | tf_op jit(solution)/shard_map/ppermute | solution.py:460
  48.0 10.2 %collective-permute-start.8 = (bf16[7,128,128]{2,1,0:T(8,128)(2,1)S(1)}, bf16[7,128,128]{2,1,0:T(8,128)(2,1)S(1)}, u32[]{:S(2)}, u32[]{:S(2)}) collective-permute-start(bf16[7,128,128]{2,1,0:T(8,128)(2,1)S(1)} %get-tuple-element.42), channel_id=1, source_target_pairs={{3,0},{2,1},{1,2},{0,3},{7,4},{6,5},{5,6},{4,7},{11,8},{10,9},{9,1... | collective-permute-start | bytes 688136 | tf_op jit(solution)/shard_map/ppermute | solution.py:460
  48.3 11.7 %collective-permute-start.12 = (bf16[432,128]{1,0:T(8,128)(2,1)S(1)}, bf16[432,128]{1,0:T(8,128)(2,1)S(1)}, u32[]{:S(2)}, u32[]{:S(2)}) collective-permute-start(bf16[432,128]{1,0:T(8,128)(2,1)S(1)} %get-tuple-element.50), channel_id=1, source_target_pairs={{0,8},{4,12},{8,16},{12,20},{16,24},{20,28},{24,0},{28,4},{1,9},{5... | collective-permute-start | bytes 331784 | tf_op jit(solution)/shard_map/ppermute | solution.py:421
  49.9 10.7 %collective-permute-start.13 = (bf16[432,128]{1,0:T(8,128)(2,1)S(1)}, bf16[432,128]{1,0:T(8,128)(2,1)S(1)}, u32[]{:S(2)}, u32[]{:S(2)}) collective-permute-start(bf16[432,128]{1,0:T(8,128)(2,1)S(1)} %get-tuple-element.51), channel_id=1, source_target_pairs={{0,16},{4,20},{8,24},{12,28},{16,0},{20,4},{24,8},{28,12},{1,17},{... | collective-permute-start | bytes 331784 | tf_op jit(solution)/shard_map/ppermute | solution.py:421
  52.5 8.1 %collective-permute-start.14 = (bf16[432,128]{1,0:T(8,128)(2,1)S(1)}, bf16[432,128]{1,0:T(8,128)(2,1)S(1)}, u32[]{:S(2)}, u32[]{:S(2)}) collective-permute-start(bf16[432,128]{1,0:T(8,128)(2,1)S(1)} %get-tuple-element.52), channel_id=1, source_target_pairs={{0,24},{4,28},{8,0},{12,4},{16,8},{20,12},{24,16},{28,20},{1,25},{... | collective-permute-start | bytes 331784 | tf_op jit(solution)/shard_map/ppermute | solution.py:421

commit v7 on v6

--- a/solution.py
+++ b/solution.py
@@ -28,6 +28,12 @@
 
 def owner_at(t, d, owners):
     return 2 * lax.rem((t >> 1) + (d >> 1), owners // 2) + ((t & 1) ^ (d & 1))
+
+
+def along_z(z, r, far):
+    if far & (far - 1) == 0:
+        return z ^ r
+    return (z + r) % far if isinstance(z, int) else lax.rem(z + r, far)
 
 
 def owner_pairs(d, owners):
@@ -45,14 +51,20 @@
     return jnp.where(keep, ids_ref[...], rows)
 
 
-def prep_kernel(pos_ref, *refs, owners, maxlen, rows):
+def prep_kernel(pos_ref, *refs, owners, maxlen, rows, chunks):
     sources, mine, rank_ref = refs[:7], refs[7 : 7 + owners], refs[7 + owners]
     targets, masked_ref, sem = refs[8 + owners : 15 + owners], refs[15 + owners], refs[16 + owners]
     slot_ref, ids_ref, lens_ref, x_ref, ct_ref, down_ref, up_ref = targets
-    loads = [
-        pltpu.make_async_copy(src, dst, sem.at[i]) for i, (src, dst) in enumerate(zip(sources, targets))
-    ]
-    for load in loads:
+    span = x_ref.shape[1] // chunks
+    loads = [pltpu.make_async_copy(sources[i], targets[i], sem.at[i]) for i in range(5)]
+    weights = []
+    for c in range(chunks):
+        at = pl.ds(c * span, span)
+        for i, part in ((5, (at, slice(None))), (6, (slice(None), at))):
+            weights.append(
+                pltpu.make_async_copy(sources[i].at[part], targets[i].at[part], sem.at[5 + len(weights)])
+            )
+    for load in loads + weights:
         load.start()
     for load in loads[:3]:
         load.wait()
@@ -62,29 +74,37 @@
     for d in range(owners):
         start = pl.multiple_of(owner_at(t, d, owners) * entries, maxlen)
         mine[d][...] = masked_ref[pl.ds(start, entries), :]
-    for load in loads[3:5]:
+    for load in loads[3:]:
         load.wait()
-    x = x_ref[...]
-    dz = (ct_ref[...].astype(F32) * x.astype(F32)).astype(BF16)
-    loads[5].wait()
-    rank_ref[0] = jnp.dot(x, down_ref[...], preferred_element_type=F32).astype(BF16)
-    loads[6].wait()
-    rank_ref[1] = lax.dot_general(
-        dz, up_ref[...], (((1,), (1,)), ((), ())), preferred_element_type=F32
-    ).astype(BF16)
+    low = dlow = None
+    for c in range(chunks):
+        at = slice(c * span, (c + 1) * span)
+        x = x_ref[:, at]
+        dz = (ct_ref[:, at].astype(F32) * x.astype(F32)).astype(BF16)
+        weights[2 * c].wait()
+        one = jnp.dot(x, down_ref[at, :], preferred_element_type=F32)
+        low = one if c == 0 else low + one
+        weights[2 * c + 1].wait()
+        one = lax.dot_general(
+            dz, up_ref[:, at], (((1,), (1,)), ((), ())), preferred_element_type=F32
+        )
+        dlow = one if c == 0 else dlow + one
+    rank_ref[0] = low.astype(BF16)
+    rank_ref[1] = dlow.astype(BF16)
 
 
 def prep(pos, slot_of_table, ids, lengths, x, ct, down, up, owners, maxlen, rows):
     sources = [slot_of_table.reshape(1, -1), ids.T, lengths.T, x, ct, down, up]
     batch, entries = ids.shape
+    chunks = 3 if x.shape[1] % (3 * LANES) == 0 else 1
     *mine, rank = pl.pallas_call(
-        functools.partial(prep_kernel, owners=owners, maxlen=maxlen, rows=rows),
+        functools.partial(prep_kernel, owners=owners, maxlen=maxlen, rows=rows, chunks=chunks),
         in_specs=[whole(pltpu.SMEM)] + [whole(pl.ANY)] * 7,
         out_specs=[whole()] * (owners + 1),
         out_shape=[jax.ShapeDtypeStruct((entries // owners, batch), jnp.int32)] * owners
         + [jax.ShapeDtypeStruct((2, batch, down.shape[1]), BF16)],
         scratch_shapes=[pltpu.VMEM(a.shape, a.dtype) for a in sources]
-        + [pltpu.VMEM((entries, batch), jnp.int32), pltpu.SemaphoreType.DMA((7,))],
+        + [pltpu.VMEM((entries, batch), jnp.int32), pltpu.SemaphoreType.DMA((5 + 2 * chunks,))],
         compiler_params=room(16),
         name="prep",
     )(pos, *[in_hbm(a) for a in sources])
@@ -201,42 +221,40 @@
     )(*ids, in_hbm(tables))
 
 
-def place_kernel(pos_ref, slot_ref, *refs):
-    parts, out_ref, sem = refs[:-2], refs[-2], refs[-1]
-    owners = len(parts)
+def place_kernel(pos_ref, slot_ref, *refs, owners, firsts):
+    parts, out_ref, sem = refs[: len(firsts)], refs[-2], refs[-1]
     slots, _, width = parts[0].shape
-    feats = slot_ref.shape[0]
     t = lax.rem(pos_ref[0], owners)
 
-    def put(f, part, local):
-        to = out_ref.at[:, pl.ds(f * width, width)]
-        return pltpu.make_async_copy(part.at[local], to, sem.at[f])
-
-    for d, part in enumerate(parts):
-        first = owner_at(t, d, owners) * slots
-        for f in range(feats):
-            local = slot_ref[f] - first
-
-            @pl.when((local >= 0) & (local < slots))
-            def _(f=f, part=part, local=local):
-                put(f, part, local).start()
-
-    for f in range(feats):
-        put(f, parts[0], 0).wait()
-
-
-def place(pos, slot_of_table, parts):
+    def each(act):
+        for d, part in zip(firsts, parts):
+            first = owner_at(t, d, owners) * slots
+            for f in range(slot_ref.shape[0]):
+                local = slot_ref[f] - first
+
+                @pl.when((local >= 0) & (local < slots))
+                def _(f=f, part=part, local=local):
+                    to = out_ref.at[:, pl.ds(f * width, width)]
+                    act(pltpu.make_async_copy(part.at[local], to, sem.at[f]))
+
+    each(lambda copy: copy.start())
+    each(lambda copy: copy.wait())
+
+
+def place(pos, slot_of_table, parts, firsts, owners, before=None):
     _, batch, width = parts[0].shape
     feats = slot_of_table.shape[0]
+    more = [] if before is None else [before]
     return pl.pallas_call(
-        place_kernel,
-        in_specs=[whole(pltpu.SMEM)] * 2 + [whole(pl.ANY)] * len(parts),
+        functools.partial(place_kernel, owners=owners, firsts=firsts),
+        in_specs=[whole(pltpu.SMEM)] * 2 + [whole(pl.ANY)] * (len(parts) + len(more)),
         out_specs=whole(pl.ANY),
         out_shape=jax.ShapeDtypeStruct((batch, feats * width), BF16),
+        input_output_aliases={2 + len(parts): 0} if more else {},
         scratch_shapes=[pltpu.SemaphoreType.DMA((feats,))],
         compiler_params=room(4),
         name="place",
-    )(pos, slot_of_table, *parts)
+    )(pos, slot_of_table, *parts, *more)
 
 
 def grads_kernel(pos_ref, own_ref, sib_ref, *refs, owners, groups, chunks):
@@ -298,7 +316,7 @@
         rx, ry = i // tall, i % tall
         cols = slice(ry * block, (ry + 1) * block)
         for r in range(far):
-            g = 2 * lax.rem(z + r, far) + (x + rx - 2 * x * rx)
+            g = 2 * along_z(z, r, far) + (x + rx - 2 * x * rx)
             found = sum_ref[pl.ds(pl.multiple_of(g * each, 16), each), cols]
             if i:
                 near_ref[i - 1, r] = found.astype(BF16)
@@ -413,7 +431,7 @@
     far = groups // 2
 
     def to_z(r):
-        return [(i, 2 * ((i // 2 + r) % far) + i % 2) for i in range(groups)]
+        return [(i, 2 * along_z(i // 2, r, far) + i % 2) for i in range(groups)]
 
     out = fold(keep, came)
     last = []
@@ -458,7 +476,8 @@
     for d in range(1, owners):
         back = [(b, a) for a, b in owner_pairs(d, owners)]
         parts.append(lax.ppermute(pooled[d], "tbl", back))
-    embedded = place(pos, slot_of_table, parts)
+    embedded = place(pos, slot_of_table, parts[:-1], range(owners - 1), owners)
+    embedded = place(pos, slot_of_table, parts[-1:], (owners - 1,), owners, embedded)
     if tiled:
         embedded, grad_up, grad_down = exchange_end(keep, came, embedded, factor)
     else:

time: 61.6 us -> 62.6 us (1.016)
  Pallas kernels: 30.1 us -> 31.7 us
  starting transfers between devices: 16.9 us -> 15.8 us
    pallas_call x1 -> x2, Pallas kernels: 1.72 us -> 3.11 us  [place(): pl.pallas_call(functools.partial(place_kernel, owners=owners, firsts=firs...]
    ppermute x3, waiting for transfers between devices: 0.67 us -> 1.8 us  [exchange_end(): last.append(lax.ppermute(out[r], 'grp', to_z(r)))]
    ppermute x3, starting transfers between devices: 5.56 us -> 4.45 us  [exchange_end(): last.append(lax.ppermute(out[r], 'grp', to_z(r)))]
  transfers between devices with their start and end apart: 15 -> 15, of which waited for: 6 -> 6; matrix products, arithmetic and copies ran while one was open for 0% -> 0% of each run, Pallas kernels for 41% -> 43%
where the time goes in v7:
time: 62.6 us; the launch traced here: 62.5 us
  Pallas kernels  31.7 us (51%)
  starting transfers between devices  15.8 us (25%)
  waiting for transfers between devices  14.3 us (23%)
  between operations  0.72 us (1%)
    pallas_call x1, Pallas kernels, pool_slots(): pl.pallas_call(functools.partial(pool_kernel, groups=groups, maxlen=maxle...  19.4 us
    ppermute x3, waiting for transfers between devices, on_device(): got.append(lax.ppermute(mine[d], 'tbl', owner_pairs(d, owners)))  7.72 us
    ppermute x3, starting transfers between devices, exchange_start(): came.append(lax.ppermute(parts[i], ('grp', 'tbl'), to(i // tall, i % tall)))  4.47 us
    ppermute x3, starting transfers between devices, exchange_end(): last.append(lax.ppermute(out[r], 'grp', to_z(r)))  4.45 us
    pallas_call x1, Pallas kernels, part_grads(): pl.pallas_call(functools.partial(grads_kernel, owners=owners, groups=grou...  4.24 us
    pallas_call x1, Pallas kernels, prep(): pl.pallas_call(functools.partial(prep_kernel, owners=owners, maxlen=maxle...  3.84 us
    ppermute x3, waiting for transfers between devices, on_device(): parts.append(lax.ppermute(pooled[d], 'tbl', back))  3.82 us
    pallas_call x2, Pallas kernels, place(): pl.pallas_call(functools.partial(place_kernel, owners=owners, firsts=firs...  3.11 us
  transfers between devices with their start and end apart: 15, of which 6 were waited for; matrix products, arithmetic and copies ran while one was open for 0% of the time, Pallas kernels for 43%

profile of v7, /device:TPU:0, one launch (start us, length us, event | category | flops | bytes accessed | tf_op | source)
XLA Modules:
  0.0 62.5 jit_solution(1251443794861686424)
XLA Ops:
  0.6 0.6 collective-permute-start.4
  1.2 0.1 collective-permute-start.5
  1.3 3.8 %prep.1 = (s32[56,128]{1,0:T(8,128)S(1)}, s32[56,128]{1,0:T(8,128)S(1)}, s32[56,128]{1,0:T(8,128)S(1)}, s32[56,128]{1,0:T(8,128)S(1)}, bf16[2,128,256]{2,1,0:T(8,128)(2,1)S(1)}) custom-call(s32[1]{0:T(128)} %bitcast.pos_ref, s32[1,26]{1,0:T(1,128)} %bitcast.5, s32[224,128]{1,0:T(8,128)} %bitcast.6, s32[26,128]{1,0:T(8,128)} %bitcast.7, ...), custom_call_target="tpu_custom_call" | custom-call | tf_op jit(solution)/shard_map/prep/pallas_call | solution.py:100
  5.1 0.5 collective-permute-start.3
  5.6 1.0 %collective-permute-done.3.sib_ref = bf16[2,128,256]{2,1,0:T(8,128)(2,1)S(1)} collective-permute-done((bf16[2,128,256]{2,1,0:T(8,128)(2,1)S(1)}, bf16[2,128,256]{2,1,0:T(8,128)(2,1)S(1)}, u32[]{:S(2)}, u32[]{:S(2)}) %collective-permute-start.3) | collective-permute-done | bytes 131104 | tf_op jit(solution)/shard_map/ppermute | solution.py:413
  6.6 0.0 collective-permute-done.4.refs_2_
  6.6 0.0 collective-permute-done.5.refs_3_
  6.6 4.2 %part_grads.1 = (f32[4,432,128]{2,1,0:T(8,128)S(1)}, bf16[4,432,128]{2,1,0:T(8,128)(2,1)}, bf16[4,432,128]{2,1,0:T(8,128)(2,1)}, bf16[4,432,128]{2,1,0:T(8,128)(2,1)}) custom-call(s32[1]{0:T(128)} %bitcast.pos_ref, bf16[2,128,256]{2,1,0:T(8,128)(2,1)S(1)} %get-tuple-element.33.own_ref, bf16[2,128,256]{2,1,0:T(8,128)(2,1)S(1)} %collective-permute-done.3.sib_ref, ...), custom_call_target="tpu_custom_call" | custom-call | tf_op jit(solution)/shard_map/part_grads/pallas_call | solution.py:341
  10.9 2.9 %collective-permute-start.9 = (bf16[4,432,128]{2,1,0:T(8,128)(2,1)}, bf16[4,432,128]{2,1,0:T(8,128)(2,1)S(1)}, u32[]{:S(2)}, u32[]{:S(2)}) collective-permute-start(bf16[4,432,128]{2,1,0:T(8,128)(2,1)} %get-tuple-element.44), channel_id=1, source_target_pairs={{0,2},{1,3},{2,0},{3,1},{4,6},{5,7},{6,4},{7,5},{8,10},{9,11},{10,... | collective-permute-start | bytes 1327112 | tf_op jit(solution)/shard_map/ppermute | solution.py:425
  13.8 1.5 %collective-permute-start.10 = (bf16[4,432,128]{2,1,0:T(8,128)(2,1)}, bf16[4,432,128]{2,1,0:T(8,128)(2,1)S(1)}, u32[]{:S(2)}, u32[]{:S(2)}) collective-permute-start(bf16[4,432,128]{2,1,0:T(8,128)(2,1)} %get-tuple-element.45), channel_id=1, source_target_pairs={{0,4},{1,5},{2,6},{3,7},{4,0},{5,1},{6,2},{7,3},{8,12},{9,13},{10,... | collective-permute-start | bytes 1327112 | tf_op jit(solution)/shard_map/ppermute | solution.py:425
  15.3 0.0 collective-permute-start.11
  15.3 0.0 collective-permute-start
  15.3 1.9 %collective-permute-start.1 = (s32[56,128]{1,0:T(8,128)S(1)}, s32[56,128]{1,0:T(8,128)S(1)}, u32[]{:S(2)}, u32[]{:S(2)}) collective-permute-start(s32[56,128]{1,0:T(8,128)S(1)} %get-tuple-element.31), channel_id=1, source_target_pairs={{0,2},{1,3},{2,0},{3,1},{4,6},{5,7},{6,4},{7,5},{8,10},{9,11},{10,... | collective-permute-start | bytes 86024 | tf_op jit(solution)/shard_map/ppermute | solution.py:470
  17.3 0.0 collective-permute-done.refs_1_
  17.3 1.0 %collective-permute-start.2 = (s32[56,128]{1,0:T(8,128)S(1)}, s32[56,128]{1,0:T(8,128)S(1)}, u32[]{:S(2)}, u32[]{:S(2)}) collective-permute-start(s32[56,128]{1,0:T(8,128)S(1)} %get-tuple-element.32), channel_id=1, source_target_pairs={{0,3},{1,2},{2,1},{3,0},{4,7},{5,6},{6,5},{7,4},{8,11},{9,10},{10,... | collective-permute-start | bytes 86024 | tf_op jit(solution)/shard_map/ppermute | solution.py:470
  18.3 7.6 %collective-permute-done.1.refs_2_ = s32[56,128]{1,0:T(8,128)S(1)} collective-permute-done((s32[56,128]{1,0:T(8,128)S(1)}, s32[56,128]{1,0:T(8,128)S(1)}, u32[]{:S(2)}, u32[]{:S(2)}) %collective-permute-start.1) | collective-permute-done | bytes 28704 | tf_op jit(solution)/shard_map/ppermute | solution.py:470
  25.9 0.1 collective-permute-done.2.refs_3_
  26.0 19.4 %pool_slots.1 = (bf16[7,128,128]{2,1,0:T(8,128)(2,1)S(1)}, bf16[7,128,128]{2,1,0:T(8,128)(2,1)S(1)}, bf16[7,128,128]{2,1,0:T(8,128)(2,1)S(1)}, bf16[7,128,128]{2,1,0:T(8,128)(2,1)S(1)}) custom-call(s32[56,128]{1,0:T(8,128)S(1)} %get-tuple-element.35.refs_0_, s32[56,128]{1,0:T(8,128)S(1)} %collective-permute-done.refs_1_, ...), custom_call_target="tpu_custom_call" | custom-call | tf_op jit(solution)/shard_map/pool_slots/pallas_call | solution.py:208
  45.4 0.0 copy-start
  45.4 0.8 %collective-permute-start.7 = (bf16[7,128,128]{2,1,0:T(8,128)(2,1)S(1)}, bf16[7,128,128]{2,1,0:T(8,128)(2,1)S(1)}, u32[]{:S(2)}, u32[]{:S(2)}) collective-permute-start(bf16[7,128,128]{2,1,0:T(8,128)(2,1)S(1)} %get-tuple-element.41), channel_id=1, source_target_pairs={{1,0},{0,1},{3,2},{2,3},{5,4},{4,5},{7,6},{6,7},{9,8},{8,9},{11,10... | collective-permute-start | bytes 688136 | tf_op jit(solution)/shard_map/ppermute | solution.py:478
  46.2 2.0 %collective-permute-start.8 = (bf16[7,128,128]{2,1,0:T(8,128)(2,1)S(1)}, bf16[7,128,128]{2,1,0:T(8,128)(2,1)S(1)}, u32[]{:S(2)}, u32[]{:S(2)}) collective-permute-start(bf16[7,128,128]{2,1,0:T(8,128)(2,1)S(1)} %get-tuple-element.42), channel_id=1, source_target_pairs={{2,0},{3,1},{0,2},{1,3},{6,4},{7,5},{4,6},{5,7},{10,8},{11,9},{8,1... | collective-permute-start | bytes 688136 | tf_op jit(solution)/shard_map/ppermute | solution.py:478
  48.2 0.0 collective-permute-done.9.refs_0_
  48.2 0.0 collective-permute-start.6
  48.2 0.0 collective-permute-done.10.refs_1_
  48.2 0.0 collective-permute-done.11.refs_2_
  48.2 0.2 fold.1
  48.4 1.6 %collective-permute-start.12 = (bf16[432,128]{1,0:T(8,128)(2,1)S(1)}, bf16[432,128]{1,0:T(8,128)(2,1)S(1)}, u32[]{:S(2)}, u32[]{:S(2)}) collective-permute-start(bf16[432,128]{1,0:T(8,128)(2,1)S(1)} %get-tuple-element.50), channel_id=1, source_target_pairs={{0,8},{4,12},{8,0},{12,4},{16,24},{20,28},{24,16},{28,20},{1,9},{5... | collective-permute-start | bytes 331784 | tf_op jit(solution)/shard_map/ppermute | solution.py:439
  50.1 2.6 %collective-permute-start.13 = (bf16[432,128]{1,0:T(8,128)(2,1)S(1)}, bf16[432,128]{1,0:T(8,128)(2,1)S(1)}, u32[]{:S(2)}, u32[]{:S(2)}) collective-permute-start(bf16[432,128]{1,0:T(8,128)(2,1)S(1)} %get-tuple-element.51), channel_id=1, source_target_pairs={{0,16},{4,20},{8,24},{12,28},{16,0},{20,4},{24,8},{28,12},{1,17},{... | collective-permute-start | bytes 331784 | tf_op jit(solution)/shard_map/ppermute | solution.py:439
  52.7 0.0 collective-permute-done.7.refs_1_
  52.7 0.2 collective-permute-start.14
  52.9 1.8 %collective-permute-done.8.refs_2_ = bf16[7,128,128]{2,1,0:T(8,128)(2,1)S(1)} collective-permute-done((bf16[7,128,128]{2,1,0:T(8,128)(2,1)S(1)}, bf16[7,128,128]{2,1,0:T(8,128)(2,1)S(1)}, u32[]{:S(2)}, u32[]{:S(2)}) %collective-permute-start.8) | collective-permute-done | bytes 229408 | tf_op jit(solution)/shard_map/ppermute | solution.py:478
  54.6 0.0 copy-done
  54.6 1.6 %place.2.refs_1_ = bf16[128,3328]{1,0:T(8,128)(2,1)} custom-call(s32[1]{0:T(128)} %bitcast.pos_ref, s32[26]{0:T(128)S(1)} %copy-done, bf16[7,128,128]{2,1,0:T(8,128)(2,1)S(1)} %get-tuple-element.40.refs_0_, bf16[7,128,128]{2,1,0:T(8,128)(2,1)S(1)} %collective-permute-done.7.refs_1_, bf16[7,128,128]{2,1,0:T(8,128)(2,1)S(1)} %collective-permute-done.8.refs_2_), custom_call_target="tpu_custom_call" | custom-call | tf_op jit(solution)/shard_map/place/pallas_call | solution.py:248
  56.3 2.1 %collective-permute-done.6.refs_0_ = bf16[7,128,128]{2,1,0:T(8,128)(2,1)S(1)} collective-permute-done((bf16[7,128,128]{2,1,0:T(8,128)(2,1)S(1)}, bf16[7,128,128]{2,1,0:T(8,128)(2,1)S(1)}, u32[]{:S(2)}, u32[]{:S(2)}) %collective-permute-start.6) | collective-permute-done | bytes 229408 | tf_op jit(solution)/shard_map/ppermute | solution.py:478
  58.4 1.5 %place.3 = bf16[128,3328]{1,0:T(8,128)(2,1)} custom-call(s32[1]{0:T(128)} %bitcast.pos_ref, s32[26]{0:T(128)S(1)} %copy-done, bf16[7,128,128]{2,1,0:T(8,128)(2,1)S(1)} %collective-permute-done.6.refs_0_, bf16[128,3328]{1,0:T(8,128)(2,1)} %place.2.refs_1_), custom_call_target="tpu_custom_call", output_to_operand_aliasing={{}: (3, {})} | custom-call | tf_op jit(solution)/shard_map/place/pallas_call | solution.py:248
  59.8 0.0 collective-permute-done.12.refs_1_
  59.8 1.8 %collective-permute-done.13.refs_2_ = bf16[432,128]{1,0:T(8,128)(2,1)S(1)} collective-permute-done((bf16[432,128]{1,0:T(8,128)(2,1)S(1)}, bf16[432,128]{1,0:T(8,128)(2,1)S(1)}, u32[]{:S(2)}, u32[]{:S(2)}) %collective-permute-start.13) | collective-permute-done | bytes 110624 | tf_op jit(solution)/shard_map/ppermute | solution.py:439
  61.6 0.0 collective-permute-done.14.refs_3_
  61.6 0.8 %finish.1 = (f32[64,432]{1,0:T(8,128)}, f32[64,432]{1,0:T(8,128)}) custom-call(f32[432,128]{1,0:T(8,128)S(1)} %get-tuple-element.49.refs_0_, bf16[432,128]{1,0:T(8,128)(2,1)S(1)} %collective-permute-done.12.refs_1_, bf16[432,128]{1,0:T(8,128)(2,1)S(1)} %collective-permute-done.13.refs_2_, bf16[432,128]{1,0:T(8,128)(2,1)S(1)} %collective-permute-done.14.refs_3_), custom_call_target="tpu_custom_call" | custom-call | tf_op jit(solution)/shard_map/finish/pallas_call | solution.py:396
Async XLA Ops:
  0.6 6.0 %collective-permute-start.4 = (bf16[128,3456]{1,0:T(8,128)(2,1)}, bf16[128,3456]{1,0:T(8,128)(2,1)S(1)}, u32[]{:S(2)}, u32[]{:S(2)}) collective-permute-start(bf16[128,3456]{1,0:T(8,128)(2,1)} %refs_0_.1), channel_id=1, source_target_pairs={{0,1},{1,0},{2,3},{3,2},{4,5},{5,4},{6,7},{7,6},{8,9},{9,8},{10,11... | collective-permute-start | bytes 2654216 | tf_op jit(solution)/shard_map/ppermute | solution.py:411
  1.2 5.4 %collective-permute-start.5 = (bf16[128,3456]{1,0:T(8,128)(2,1)}, bf16[128,3456]{1,0:T(8,128)(2,1)S(1)}, u32[]{:S(2)}, u32[]{:S(2)}) collective-permute-start(bf16[128,3456]{1,0:T(8,128)(2,1)} %refs_1_.1), channel_id=1, source_target_pairs={{0,1},{1,0},{2,3},{3,2},{4,5},{5,4},{6,7},{7,6},{8,9},{9,8},{10,11... | collective-permute-start | bytes 2654216 | tf_op jit(solution)/shard_map/ppermute | solution.py:412
  5.1 1.5 %collective-permute-start.3 = (bf16[2,128,256]{2,1,0:T(8,128)(2,1)S(1)}, bf16[2,128,256]{2,1,0:T(8,128)(2,1)S(1)}, u32[]{:S(2)}, u32[]{:S(2)}) collective-permute-start(bf16[2,128,256]{2,1,0:T(8,128)(2,1)S(1)} %get-tuple-element.33.own_ref), channel_id=1, source_target_pairs={{0,1},{1,0},{2,3},{3,2},{4,5},{5,4},{6,7},{7,6},{8,9},{9,8},{10,11... | collective-permute-start | bytes 393224 | tf_op jit(solution)/shard_map/ppermute | solution.py:413
  10.9 37.3 %collective-permute-start.9 = (bf16[4,432,128]{2,1,0:T(8,128)(2,1)}, bf16[4,432,128]{2,1,0:T(8,128)(2,1)S(1)}, u32[]{:S(2)}, u32[]{:S(2)}) collective-permute-start(bf16[4,432,128]{2,1,0:T(8,128)(2,1)} %get-tuple-element.44), channel_id=1, source_target_pairs={{0,2},{1,3},{2,0},{3,1},{4,6},{5,7},{6,4},{7,5},{8,10},{9,11},{10,... | collective-permute-start | bytes 1327112 | tf_op jit(solution)/shard_map/ppermute | solution.py:425
  13.8 34.4 %collective-permute-start.10 = (bf16[4,432,128]{2,1,0:T(8,128)(2,1)}, bf16[4,432,128]{2,1,0:T(8,128)(2,1)S(1)}, u32[]{:S(2)}, u32[]{:S(2)}) collective-permute-start(bf16[4,432,128]{2,1,0:T(8,128)(2,1)} %get-tuple-element.45), channel_id=1, source_target_pairs={{0,4},{1,5},{2,6},{3,7},{4,0},{5,1},{6,2},{7,3},{8,12},{9,13},{10,... | collective-permute-start | bytes 1327112 | tf_op jit(solution)/shard_map/ppermute | solution.py:425
  15.3 32.9 %collective-permute-start.11 = (bf16[4,432,128]{2,1,0:T(8,128)(2,1)}, bf16[4,432,128]{2,1,0:T(8,128)(2,1)S(1)}, u32[]{:S(2)}, u32[]{:S(2)}) collective-permute-start(bf16[4,432,128]{2,1,0:T(8,128)(2,1)} %get-tuple-element.46), channel_id=1, source_target_pairs={{0,6},{1,7},{2,4},{3,5},{4,2},{5,3},{6,0},{7,1},{8,14},{9,15},{10,... | collective-permute-start | bytes 1327112 | tf_op jit(solution)/shard_map/ppermute | solution.py:425
  15.3 2.0 %collective-permute-start = (s32[56,128]{1,0:T(8,128)S(1)}, s32[56,128]{1,0:T(8,128)S(1)}, u32[]{:S(2)}, u32[]{:S(2)}) collective-permute-start(s32[56,128]{1,0:T(8,128)S(1)} %get-tuple-element.30), channel_id=1, source_target_pairs={{0,1},{1,0},{2,3},{3,2},{4,5},{5,4},{6,7},{7,6},{8,9},{9,8},{10,11... | collective-permute-start | bytes 86024 | tf_op jit(solution)/shard_map/ppermute | solution.py:470
  15.3 10.6 %collective-permute-start.1 = (s32[56,128]{1,0:T(8,128)S(1)}, s32[56,128]{1,0:T(8,128)S(1)}, u32[]{:S(2)}, u32[]{:S(2)}) collective-permute-start(s32[56,128]{1,0:T(8,128)S(1)} %get-tuple-element.31), channel_id=1, source_target_pairs={{0,2},{1,3},{2,0},{3,1},{4,6},{5,7},{6,4},{7,5},{8,10},{9,11},{10,... | collective-permute-start | bytes 86024 | tf_op jit(solution)/shard_map/ppermute | solution.py:470
  17.3 8.7 %collective-permute-start.2 = (s32[56,128]{1,0:T(8,128)S(1)}, s32[56,128]{1,0:T(8,128)S(1)}, u32[]{:S(2)}, u32[]{:S(2)}) collective-permute-start(s32[56,128]{1,0:T(8,128)S(1)} %get-tuple-element.32), channel_id=1, source_target_pairs={{0,3},{1,2},{2,1},{3,0},{4,7},{5,6},{6,5},{7,4},{8,11},{9,10},{10,... | collective-permute-start | bytes 86024 | tf_op jit(solution)/shard_map/ppermute | solution.py:470
  45.4 9.2 %copy-start = (s32[26]{0:T(128)S(1)}, s32[26]{0:T(128)}, u32[]{:S(2)}) copy-start(s32[26]{0:T(128)} %slot_ref.3) | copy-start | bytes 316
  45.4 7.3 %collective-permute-start.7 = (bf16[7,128,128]{2,1,0:T(8,128)(2,1)S(1)}, bf16[7,128,128]{2,1,0:T(8,128)(2,1)S(1)}, u32[]{:S(2)}, u32[]{:S(2)}) collective-permute-start(bf16[7,128,128]{2,1,0:T(8,128)(2,1)S(1)} %get-tuple-element.41), channel_id=1, source_target_pairs={{1,0},{0,1},{3,2},{2,3},{5,4},{4,5},{7,6},{6,7},{9,8},{8,9},{11,10... | collective-permute-start | bytes 688136 | tf_op jit(solution)/shard_map/ppermute | solution.py:478
  46.2 8.5 %collective-permute-start.8 = (bf16[7,128,128]{2,1,0:T(8,128)(2,1)S(1)}, bf16[7,128,128]{2,1,0:T(8,128)(2,1)S(1)}, u32[]{:S(2)}, u32[]{:S(2)}) collective-permute-start(bf16[7,128,128]{2,1,0:T(8,128)(2,1)S(1)} %get-tuple-element.42), channel_id=1, source_target_pairs={{2,0},{3,1},{0,2},{1,3},{6,4},{7,5},{4,6},{5,7},{10,8},{11,9},{8,1... | collective-permute-start | bytes 688136 | tf_op jit(solution)/shard_map/ppermute | solution.py:478
  48.2 10.2 %collective-permute-start.6 = (bf16[7,128,128]{2,1,0:T(8,128)(2,1)S(1)}, bf16[7,128,128]{2,1,0:T(8,128)(2,1)S(1)}, u32[]{:S(2)}, u32[]{:S(2)}) collective-permute-start(bf16[7,128,128]{2,1,0:T(8,128)(2,1)S(1)} %get-tuple-element.39), channel_id=1, source_target_pairs={{3,0},{2,1},{1,2},{0,3},{7,4},{6,5},{5,6},{4,7},{11,8},{10,9},{9,1... | collective-permute-start | bytes 688136 | tf_op jit(solution)/shard_map/ppermute | solution.py:478
  48.4 11.4 %collective-permute-start.12 = (bf16[432,128]{1,0:T(8,128)(2,1)S(1)}, bf16[432,128]{1,0:T(8,128)(2,1)S(1)}, u32[]{:S(2)}, u32[]{:S(2)}) collective-permute-start(bf16[432,128]{1,0:T(8,128)(2,1)S(1)} %get-tuple-element.50), channel_id=1, source_target_pairs={{0,8},{4,12},{8,0},{12,4},{16,24},{20,28},{24,16},{28,20},{1,9},{5... | collective-permute-start | bytes 331784 | tf_op jit(solution)/shard_map/ppermute | solution.py:439
  50.1 11.6 %collective-permute-start.13 = (bf16[432,128]{1,0:T(8,128)(2,1)S(1)}, bf16[432,128]{1,0:T(8,128)(2,1)S(1)}, u32[]{:S(2)}, u32[]{:S(2)}) collective-permute-start(bf16[432,128]{1,0:T(8,128)(2,1)S(1)} %get-tuple-element.51), channel_id=1, source_target_pairs={{0,16},{4,20},{8,24},{12,28},{16,0},{20,4},{24,8},{28,12},{1,17},{... | collective-permute-start | bytes 331784 | tf_op jit(solution)/shard_map/ppermute | solution.py:439
  52.7 9.0 %collective-permute-start.14 = (bf16[432,128]{1,0:T(8,128)(2,1)S(1)}, bf16[432,128]{1,0:T(8,128)(2,1)S(1)}, u32[]{:S(2)}, u32[]{:S(2)}) collective-permute-start(bf16[432,128]{1,0:T(8,128)(2,1)S(1)} %get-tuple-element.52), channel_id=1, source_target_pairs={{0,24},{4,28},{8,16},{12,20},{16,8},{20,12},{24,0},{28,4},{1,25},{... | collective-permute-start | bytes 331784 | tf_op jit(solution)/shard_map/ppermute | solution.py:439
